TPU v7x, 256 devices: a whole 4x4x8 slice. The times are simulated.
256 devices in a mesh: row: 8 (over x, core), col: 4 (over y), depth: 8 (over z).
Axes of the slice: x: 4, y: 4, z: 8, core: 2. Of those that a mesh axis runs over, the one named last changes fastest.
Arguments:
- left_values: bfloat16 [384, 32, 4, 529], P('row', ('col', 'depth')), may hold values from -1.25 to 1.25
- left_columns: int32 [384, 32, 4], P('row', ('col', 'depth')), may hold values from 0 to 39, as said below
- right_values: bfloat16 [32, 40, 4, 3, 529], P(('col', 'depth'), 'row'), may hold values from -1.75 to 1.75
- right_columns: int32 [32, 40, 4, 3], P(('col', 'depth'), 'row'), may hold values from 0 to 31, as said below
Outputs:
- product_matrix: bfloat16 [8832, 2944], P('row', ('col', 'depth'))
Inputs may be any that keep to these rules, and one draw needn't show every extreme that they name: `left_columns`: within one block row and panel the 4 entries are distinct. `right_columns`: within one block row and column tile the 3 entries are distinct.
All inputs are finite; a program needn't handle non-finite values.
Results may differ from a plain program's by a relative error of at most 0.001.
Values may be sent and summed in bfloat16 or wider, within the bound.
No kernel may reach another device: no remote copies, remote signals or barrier semaphores. Data moves between devices by JAX's collectives and lax.ppermute only.
A program may use at most 128 MiB of HBM per device.

v0:
```python
import math

import jax
import jax.numpy as jnp
from jax import lax
from jax.sharding import PartitionSpec as P

PANEL = 40
CTW = 32


def in_one_piece(arrays, axis, dim, along):
    widths = [math.prod(a.shape[along:]) for a in arrays]
    both = jnp.concatenate(
        [a.reshape(*a.shape[:along], w) for a, w in zip(arrays, widths)], axis=along
    )
    whole = lax.all_gather(both, axis, axis=dim, tiled=True)
    pieces = jnp.split(whole, [sum(widths[:k]) for k in range(1, len(widths))], axis=along)
    return tuple(
        (b.reshape(*whole.shape[:along], *a.shape[along:]) for a, b in zip(arrays, pieces))
    )


def dense_left(values, columns, panel_width):
    rows_here, panels, slots, square = values.shape
    block_edge = math.isqrt(square)
    onehot = (
        columns.astype(jnp.float32)[..., None] == jnp.arange(panel_width, dtype=jnp.float32)
    ).astype(jnp.bfloat16)
    blocks = values.reshape(rows_here, panels, slots, block_edge, block_edge)
    filled = jnp.einsum(
        "mqsp,mqsab->qmapb", onehot, blocks, preferred_element_type=jnp.float32
    ).astype(jnp.bfloat16)
    return filled.reshape(panels, rows_here * block_edge, panel_width * block_edge)


def dense_right(values, columns, tile_width):
    panels, rows_here, tiles, slots, square = values.shape
    block_edge = math.isqrt(square)
    onehot = (
        columns.astype(jnp.float32)[..., None] == jnp.arange(tile_width, dtype=jnp.float32)
    ).astype(jnp.bfloat16)
    blocks = values.reshape(panels, rows_here, tiles, slots, block_edge, block_edge)
    filled = jnp.einsum(
        "qrtuc,qrtuab->qratcb", onehot, blocks, preferred_element_type=jnp.float32
    ).astype(jnp.bfloat16)
    return filled.reshape(panels, rows_here * block_edge, tiles * tile_width * block_edge)


def contract(left_values, left_codes, right_values, right_codes):
    left_filled = dense_left(left_values, left_codes, PANEL)
    pieces = in_one_piece((right_values, right_codes), "row", 1, 4)
    right_filled = dense_right(pieces[0], pieces[1], CTW)
    return jnp.einsum("qmk,qkn->mn", left_filled, right_filled, preferred_element_type=jnp.float32)


def body(left_values, left_columns, right_values, right_columns):
    right_codes = right_columns.astype(jnp.bfloat16)
    partial_sums = contract(left_values, left_columns, right_values, right_codes)
    result = lax.psum_scatter(partial_sums, ("col", "depth"), scatter_dimension=1, tiled=True)
    return result.astype(jnp.bfloat16)


def solution(mesh):
    placed = (
        P("row", ("col", "depth"), None, None),
        P("row", ("col", "depth"), None),
        P(("col", "depth"), "row", None, None, None),
        P(("col", "depth"), "row", None, None),
    )
    return jax.shard_map(
        body, mesh=mesh, in_specs=placed, out_specs=P("row", ("col", "depth")), check_vma=False
    )
```

profile of v0, /device:TPU:16, one launch (start us, length us, event | category | flops | bytes accessed | tf_op | source)
XLA Modules:
  0.0 355.5 jit_solution(7815934439125300105)
XLA Ops:
  0.0 0.7 convert_bitcast_fusion.1
  0.7 0.2 copy.35
  0.9 1.0 pad_maximum_fusion
  1.8 13.6 %all_gather.3 = bf16[1,40,4,3,530]{4,2,3,0,1:T(4,128)(2,1)S(1)} all-gather(bf16[1,5,4,3,530]{4,2,3,0,1:T(4,128)(2,1)S(1)} %pad_maximum_fusion), channel_id=1, replica_groups=mesh['row'=8,'col'=4,'depth'=8] {'row'}, dimensions={1}, use_global_device_ids=true | all-gather | bytes 572400 | tf_op jit(solution)/shard_map/all_gather | solution.py:17
  15.4 0.1 split.9
  15.5 1.2 copy.36
  16.8 6.2 %copy.39 = bf16[40,4,3,23,23]{4,2,3,1,0:T(4,128)(2,1)} copy(bf16[40,4,3,23,23]{0,1,4,3,2:T(4,128)(2,1)S(1)} %bitcast.44) | data formatting | bytes 1015680 | tf_op jit(solution)/shard_map/reshape.13
  23.0 0.2 copy.43
  23.2 0.1 copy.38
  23.3 17.1 %convert_bitcast_fusion = bf16[1,40,23,4,32,23]{4,5,2,3,1,0:T(8,128)(2,1)} fusion(bf16[40,4,3,23,23]{4,2,3,1,0:T(4,128)(2,1)} %copy.39, f32[40,4,3]{2,1,0:T(4,128)S(1)} %copy.38), kind=kOutput, calls=%fused_computation | convolution fusion | flops 18974720 | bytes 5926720 | tf_op jit(solution)/shard_map/qrtuc,qrtuab->qratcb/dot_general | solution.py:44
  40.4 41.1 %copy.40 = bf16[1,40,23,4,32,23]{5,4,3,2,1,0:T(8,128)(2,1)} copy(bf16[1,40,23,4,32,23]{4,5,2,3,1,0:T(8,128)(2,1)} %convert_bitcast_fusion) | data formatting | bytes 10833920 | tf_op jit(solution)/shard_map/convert_element_type | solution.py:46
  81.5 0.0 copy-start
  81.5 0.0 copy-start.1
  81.5 36.1 %reshape.47 = bf16[920,2944]{1,0:T(8,128)(2,1)} reshape(bf16[1,40,23,4,32,23]{5,4,3,2,1,0:T(8,128)(2,1)} %copy.40) | data formatting | bytes 10833920 | tf_op jit(solution)/shard_map/reshape.17
  117.7 0.0 copy-done
  117.7 0.9 copy.31
  118.6 3.5 copy.32
  122.0 0.0 copy-done.1
  122.0 0.1 copy.30
  122.1 5.7 %fusion.1 = bf16[1,48,23,40,23]{3,4,2,1,0:T(8,128)(2,1)} fusion(bf16[48,4,23,23]{3,1,2,0:T(4,128)(2,1)S(1)} %copy.32, f32[48,4]{1,0:T(8,128)S(1)} %copy.30), kind=kOutput, calls=%fused_computation.2 | convolution fusion | flops 9148800 | bytes 2235264 | tf_op jit(solution)/shard_map/mqsp,mqsab->qmapb/dot_general | solution.py:31
  127.9 23.6 %copy.33 = bf16[1,48,23,40,23]{2,1,4,3,0:T(8,128)(2,1)} copy(bf16[1,48,23,40,23]{3,4,2,1,0:T(8,128)(2,1)} %fusion.1) | data formatting | bytes 4062720 | tf_op jit(solution)/shard_map/convert_element_type | solution.py:33
  151.5 13.4 %reshape.44 = bf16[1104,920]{0,1:T(8,128)(2,1)S(1)} reshape(bf16[1,48,23,40,23]{2,1,4,3,0:T(8,128)(2,1)} %copy.33) | data formatting | bytes 4062720 | tf_op jit(solution)/shard_map/reshape.16
  164.9 13.3 %fusion.8 = f32[1104,2944]{0,1:T(8,128)} fusion(bf16[1104,920]{0,1:T(8,128)(2,1)S(1)} %reshape.44, bf16[920,2944]{1,0:T(8,128)(2,1)} %reshape.47), kind=kOutput, calls=%fused_computation.14 | convolution fusion | flops 5980323840 | bytes 20449024 | tf_op jit(solution)/shard_map/qmk,qkn->mn/dot_general | solution.py:54
  178.2 0.0 copy-start.2
  178.2 162.6 %fusion = f32[1104,96]{0,1:T(8,128)S(1)} fusion(f32[1104,2944]{0,1:T(8,128)} %fusion.8), kind=kCustom, calls=%all-reduce-scatter | all-reduce-scatter fusion | flops 3391489 | bytes 13425664
  340.8 3.0 collective-permute-start
  343.9 2.0 collective-permute-start.1
  345.9 0.0 copy-done.2
  345.9 0.6 dynamic-slice.4
  347.2 6.8 %collective-permute-done.1 = bf16[1104,28]{0,1:T(8,128)(2,1)S(1)} collective-permute-done((bf16[1104,28]{0,1:T(8,128)(2,1)S(1)}, bf16[1104,28]{0,1:T(8,128)(2,1)S(1)}, u32[]{:S(2)}, u32[]{:S(2)}) %collective-permute-start.1) | collective-permute-done | bytes 61856
  354.0 0.0 collective-permute-done
  354.0 0.8 concatenate.4
  354.8 0.7 dynamic-slice_convert_fusion
  (4 shorter events, 0.1 us)
Async XLA Ops:
  81.5 36.2 %copy-start = (bf16[48,1,4,529]{3,2,1,0:T(4,128)(2,1)S(1)}, bf16[48,1,4,529]{3,2,1,0:T(4,128)(2,1)}, u32[]{:S(2)}) copy-start(bf16[48,1,4,529]{3,2,1,0:T(4,128)(2,1)} %param.4) | copy-start | bytes 609412
  81.5 40.5 %copy-start.1 = (s32[48,1,4]{0,2,1:T(4,128)S(1)}, s32[48,1,4]{0,2,1:T(4,128)}, u32[]{:S(2)}) copy-start(s32[48,1,4]{0,2,1:T(4,128)} %param.5) | copy-start | bytes 2308
  178.2 167.7 %copy-start.2 = (u32[256]{0:T(256)S(1)}, u32[256]{0:T(256)}, u32[]{:S(2)}) copy-start(u32[256]{0:T(256)} %constant.6) | copy-start | bytes 3076
  340.8 13.1 %collective-permute-start = (bf16[1104,96]{0,1:T(8,128)(2,1)S(1)}, bf16[1104,96]{0,1:T(8,128)(2,1)S(1)}, u32[]{:S(2)}, u32[]{:S(2)}) collective-permute-start(bf16[1104,96]{0,1:T(8,128)(2,1)S(1)} %convert.3), channel_id=1, source_target_pairs={{0,1},{1,2},{2,3},{3,4},{4,5},{5,6},{6,7},{7,8},{8,9},{9,10},{10,1... | collective-permute-start | bytes 635912
  343.9 10.0 %collective-permute-start.1 = (bf16[1104,28]{0,1:T(8,128)(2,1)S(1)}, bf16[1104,28]{0,1:T(8,128)(2,1)S(1)}, u32[]{:S(2)}, u32[]{:S(2)}) collective-permute-start(bf16[1104,28]{0,1:T(8,128)(2,1)S(1)} %slice), channel_id=1, source_target_pairs={{0,2},{1,3},{2,4},{3,5},{4,6},{5,7},{6,8},{7,9},{8,10},{9,11},{10,... | collective-permute-start | bytes 185480
where the time goes:
time: 359 us; the launch traced here: 356 us
  blocking collectives  176 us (49%)
  local copies, waits for them, and re-layouts  129 us (36%)
  matrix products  36.2 us (10%)
  waiting for transfers between devices  6.78 us (2%)
  starting transfers between devices  5.06 us (1%)
    unnamed x1, blocking collectives  163 us
    another operation x4, local copies, waits for them, and re-layouts  59.2 us
    convert_element_type x1, local copies, waits for them, and re-layouts, dense_right(): filled = jnp.einsum('qrtuc,qrtuab->qratcb', onehot, blocks, preferred_ele...  41.1 us
    convert_element_type x1, local copies, waits for them, and re-layouts, dense_left(): filled = jnp.einsum('mqsp,mqsab->qmapb', onehot, blocks, preferred_elemen...  23.6 us
    dot_general x1, matrix products, dense_right(): jnp.einsum('qrtuc,qrtuab->qratcb', onehot, blocks, preferred_element_type...  17.1 us
    all_gather x1, blocking collectives, in_one_piece(): whole = lax.all_gather(both, axis, axis=dim, tiled=True)  13.6 us
    dot_general x1, matrix products, contract(): jnp.einsum('qmk,qkn->mn', left_filled, right_filled, preferred_element_ty...  13.3 us
  transfers between devices with their start and end apart: 2, of which 1 were waited for; matrix products, arithmetic and copies ran while one was open for 0% of the time, Pallas kernels for 0%

commit v1 on v0

v1 whole, which is shorter than its diff:
```python
import functools

import jax
import jax.numpy as jnp
from jax import lax
from jax.experimental import pallas as pl
from jax.experimental.pallas import tpu as pltpu
from jax.sharding import PartitionSpec as P

BLK = 23
LANES = 128
APAD = 24
KROW = 32
SLOTS = 4
USLOTS = 3
TILES = 4
PANEL = 40
HERE = 5
GROUP = 8
CHUNK = 96
WIDE = 4 * CHUNK
ROWS = 48


def place(z, windows, lane, src, dst):
    first, last = src // LANES, (src + BLK - 1) // LANES
    shift = (dst - src) % LANES
    split = dst + min(BLK, LANES * (first + 1) - src)
    rolled = pltpu.roll(windows(first), shift, 1) if shift else windows(first)
    z = jnp.where((lane >= dst) & (lane < split), rolled, z)
    if last != first:
        rolled = pltpu.roll(windows(last), shift, 1) if shift else windows(last)
        z = jnp.where((lane >= split) & (lane < dst + BLK), rolled, z)
    return z


def pack_kernel(left_ref, left_cols_ref, right_ref, right_cols_ref, left_out, right_out, left_tmp, right_tmp):
    lane = lax.broadcasted_iota(jnp.int32, (ROWS, LANES), 1)
    for a in range(BLK):
        z = jnp.zeros((ROWS, LANES), jnp.float32)
        for s in range(SLOTS):
            z = place(
                z,
                lambda j, s=s: left_ref[s, :, j * LANES : (j + 1) * LANES],
                lane,
                BLK * a,
                KROW * s,
            )
        left_tmp[pl.ds(a, ROWS, stride=APAD), :] = z
    left_tmp[pl.ds(BLK, ROWS, stride=APAD), :] = left_cols_ref[...]
    for i in range(ROWS):
        left_out[i] = left_tmp[i * APAD : (i + 1) * APAD, :].astype(jnp.bfloat16)
    lane = lax.broadcasted_iota(jnp.int32, (16, LANES), 1)
    for a in range(BLK):
        z = jnp.zeros((16, LANES), jnp.float32)
        for k in range(HERE):
            z = place(
                z,
                lambda j, k=k: right_ref[k, :, j * LANES : (j + 1) * LANES],
                lane,
                BLK * a,
                BLK * k,
            )
        right_tmp[pl.ds(a, 16, stride=APAD), :] = z
    right_tmp[pl.ds(BLK, 16, stride=APAD), :] = right_cols_ref[...]
    for d in range(GROUP):
        for u in range(USLOTS):
            row = (d // 2) * 4 + u
            right_out[d, u] = right_tmp[row * APAD : (row + 1) * APAD, :].astype(jnp.bfloat16)


def pack(left_values, left_columns, right_values, right_columns):
    wide = 5 * LANES
    left = jnp.pad(
        jnp.transpose(left_values[:, 0].astype(jnp.float32), (1, 0, 2)), ((0, 0), (0, 0), (0, wide - BLK * BLK))
    )
    left_cols = jnp.pad(left_columns[:, 0].astype(jnp.float32), ((0, 0), (0, LANES - SLOTS)))
    right = jnp.pad(
        right_values[0].astype(jnp.float32), ((0, 0), (0, 0), (0, 1), (0, wide - BLK * BLK))
    ).reshape(HERE, 16, wide)
    right_cols = jnp.pad(
        jnp.transpose(right_columns[0], (1, 2, 0)).astype(jnp.float32), ((0, 0), (0, 1), (0, LANES - HERE))
    ).reshape(16, LANES)
    return pl.pallas_call(
        pack_kernel,
        out_shape=(
            jax.ShapeDtypeStruct((ROWS, APAD, LANES), jnp.bfloat16),
            jax.ShapeDtypeStruct((GROUP, USLOTS, APAD, LANES), jnp.bfloat16),
        ),
        in_specs=[pl.BlockSpec(memory_space=pltpu.VMEM)] * 4,
        out_specs=(pl.BlockSpec(memory_space=pltpu.VMEM),) * 2,
        scratch_shapes=[
            pltpu.VMEM((ROWS * APAD, LANES), jnp.float32),
            pltpu.VMEM((16 * APAD, LANES), jnp.float32),
        ],
    )(left, left_cols, right, right_cols)


def product_kernel(lidx_ref, dest_ref, right_ref, *refs):
    lefts, (out_ref, wide_ref, sum_ref, part_ref) = refs[:GROUP], refs[GROUP:]
    lane = lax.broadcasted_iota(jnp.int32, (APAD, WIDE), 1)

    def fill(n, carry):
        for k in range(HERE):
            z = jnp.zeros((APAD, WIDE), jnp.float32)
            for u in range(USLOTS):
                at = dest_ref[(n * USLOTS + u) * HERE + k]
                block = right_ref[n, u].astype(jnp.float32)
                rolled = pltpu.roll(block, (at + 4 * LANES - BLK * k) % LANES, 1)
                rolled = jnp.concatenate([rolled] * 3, axis=1)
                z = jnp.where((lane >= at) & (lane < at + BLK), rolled, z)
            full = jnp.concatenate([z, jnp.zeros((KROW - APAD, WIDE), jnp.float32)], axis=0)
            full = full.astype(jnp.bfloat16)
            for q in range(3):
                wide_ref[n * HERE + k, q] = full[:, q * LANES : (q + 1) * LANES]
        return carry

    lax.fori_loop(0, 8 * GROUP, fill, 0)

    def step(g, carry):
        for m in range(8):
            i = g * 8 + m
            total = jnp.zeros((APAD, WIDE), jnp.float32)
            for j in range(0, GROUP, 2):
                at = [lidx_ref[(i * GROUP + j) * SLOTS + s] for s in range(2 * SLOTS)]
                weights = jnp.concatenate(
                    [jnp.concatenate([wide_ref[n, q] for n in at], axis=0) for q in range(3)], axis=1
                )
                rows = jnp.concatenate([lefts[j][i], lefts[j + 1][i]], axis=1)
                total = total + jnp.dot(rows, weights, preferred_element_type=jnp.float32)
            part_ref[m * BLK : m * BLK + APAD, :] = total
        sum_ref[pl.ds(pl.multiple_of(g * 8 * BLK, 8), 8 * BLK), :] = part_ref[0 : 8 * BLK, :]
        return carry

    lax.fori_loop(0, ROWS // 8, step, 0)
    count = ROWS * BLK
    for q in range(3):
        turned = sum_ref[0:1152, q * LANES : (q + 1) * LANES].T
        out_ref[q * LANES : (q + 1) * LANES, :] = turned[:, :count]


def product(lidx, dest, right, lefts):
    return pl.pallas_call(
        product_kernel,
        out_shape=jax.ShapeDtypeStruct((WIDE, ROWS * BLK), jnp.float32),
        in_specs=[pl.BlockSpec(memory_space=pltpu.SMEM)] * 2
        + [pl.BlockSpec(memory_space=pltpu.VMEM)] * (1 + GROUP),
        out_specs=pl.BlockSpec(memory_space=pltpu.VMEM),
        scratch_shapes=[
            pltpu.VMEM((GROUP * PANEL, 3, KROW, LANES), jnp.bfloat16),
            pltpu.VMEM((1152, WIDE), jnp.float32),
            pltpu.VMEM((8 * APAD, WIDE), jnp.float32),
        ],
        cost_estimate=pl.CostEstimate(flops=6_000_000_000, bytes_accessed=8_000_000, transcendentals=0),
    )(lidx, dest, right, *lefts)


def shift(x, axis, by, n):
    return lax.ppermute(x, axis, [(i, (i + by) % n) for i in range(n)])


def gather_depth(own):
    f1, b1 = shift(own, "depth", 1, 8), shift(own, "depth", -1, 8)
    f2, b2 = shift(f1, "depth", 1, 8), shift(b1, "depth", -1, 8)
    f3, b3 = shift(f2, "depth", 1, 8), shift(b2, "depth", -1, 8)
    half = ROWS // 2
    f4, b4 = shift(f3[:half], "depth", 1, 8), shift(b3[half:], "depth", -1, 8)
    far = jnp.concatenate([f4, b4], axis=0)
    return [own, f1, b1, f2, b2, f3, b3, far], (0, -1, 1, -2, 2, -3, 3, 4)


def body(left_values, left_columns, right_values, right_columns):
    c, d = lax.axis_index("col"), lax.axis_index("depth")
    left, right = pack(left_values, left_columns, right_values, right_columns)
    lefts, offsets = gather_depth(left)
    right = lax.all_to_all(right, "depth", 0, 0)
    first = lax.all_gather(right[:4], "row", axis=1)
    second = lax.all_gather(right[4:], "row", axis=1)
    right = jnp.concatenate([first, second], axis=0).reshape(64, USLOTS, APAD, LANES)
    rcol = right[:, :, BLK, :HERE].astype(jnp.int32)
    local = rcol - 16 * (d % 2)
    dest = jnp.where(
        (local >= 0) & (local < 16), CHUNK * ((local // 4 - c) % 4) + BLK * (local % 4), 4 * LANES
    )
    lidx = jnp.stack(
        [x[:, BLK, :SLOTS].astype(jnp.int32) + PANEL * ((d + o) % 8) for x, o in zip(lefts, offsets)], axis=1
    )
    parts = product(lidx.reshape(-1), dest.reshape(-1), right, lefts)
    own, ahead, far, behind = (parts[CHUNK * q : CHUNK * q + 4 * BLK] for q in range(4))
    cut = 48
    from_behind = shift(far[:cut], "col", 1, 4)
    from_ahead = shift(far[cut:], "col", -1, 4)
    ahead = jnp.concatenate([ahead[:cut] + from_behind, ahead[cut:]], axis=0)
    behind = jnp.concatenate([behind[:cut], behind[cut:] + from_ahead], axis=0)
    total = own + shift(ahead, "col", 1, 4) + shift(behind, "col", -1, 4)
    done = total.astype(jnp.bfloat16)
    home = [(y * 8 + z, (z // 2) * 8 + (z % 2) * 4 + y) for y in range(4) for z in range(8)]
    return lax.ppermute(done, ("col", "depth"), home).T


def solution(mesh):
    placed = (
        P("row", ("col", "depth"), None, None),
        P("row", ("col", "depth"), None),
        P(("col", "depth"), "row", None, None, None),
        P(("col", "depth"), "row", None, None),
    )
    return jax.shard_map(
        body, mesh=mesh, in_specs=placed, out_specs=P("row", ("col", "depth")), check_vma=False
    )
```

time: 359 us -> 138 us (0.38)
  blocking collectives: 176 us -> 26.8 us
  local copies, waits for them, and re-layouts: 129 us -> 10.7 us
  waiting for transfers between devices: 6.78 us -> 47.3 us
  matrix products: 36.2 us -> 0 us
  Pallas kernels: 0 us -> 21.8 us
  starting transfers between devices: 5.06 us -> 25.3 us
    unnamed x1 -> x0, blocking collectives: 163 us -> none
    convert_element_type x3 -> x0, local copies, waits for them, and re-layouts: 65.4 us -> none  [the longest x1 41.1 us: dense_right(): filled = jnp.einsum('qrtuc,qrtuab->qratcb', onehot, blocks, preferred_ele...]
    another operation x4 -> x2, local copies, waits for them, and re-layouts: 59.2 us -> 0.2 us  [body(): jnp.stack([x[:, BLK, :SLOTS].astype(jnp.int32) + PANEL * ((d + o) % 8) fo...]
    ppermute x0 -> x13, waiting for transfers between devices: none -> 41.6 us  [the longest x12 29.4 us: shift(): return lax.ppermute(x, axis, [(i, (i + by) % n) for i in range(n)])]
    dot_general x3 -> x0, matrix products: 36.2 us -> none  [the longest x1 17.1 us: dense_right(): jnp.einsum('qrtuc,qrtuab->qratcb', onehot, blocks, preferred_element_type...]
    pallas_call x0 -> x2, Pallas kernels: none -> 21.8 us  [the longest x1 19 us: product(): pl.pallas_call(product_kernel, out_shape=jax.ShapeDtypeStruct((WIDE, ROWS...]
    ppermute x0 -> x13, starting transfers between devices: none -> 16.9 us  [the longest x12 15 us: shift(): return lax.ppermute(x, axis, [(i, (i + by) % n) for i in range(n)])]
    all_gather x1 -> x2, blocking collectives: 13.6 us -> 26.8 us  [the longest x1 13.6 us: body(): first = lax.all_gather(right[:4], 'row', axis=1)]
  transfers between devices with their start and end apart: 2 -> 14, of which waited for: 1 -> 9; matrix products, arithmetic and copies ran while one was open for 0% -> 4% of each run, Pallas kernels for 0% -> 0%
where the time goes in v1:
time: 138 us; the launch traced here: 137 us
  waiting for transfers between devices  47.3 us (34%)
  blocking collectives  26.8 us (19%)
  starting transfers between devices  25.3 us (18%)
  Pallas kernels  21.8 us (16%)
  local copies, waits for them, and re-layouts  10.7 us (8%)
  other arithmetic  4.76 us (3%)
    ppermute x12, waiting for transfers between devices, shift(): return lax.ppermute(x, axis, [(i, (i + by) % n) for i in range(n)])  29.4 us
    pallas_call x1, Pallas kernels, product(): pl.pallas_call(product_kernel, out_shape=jax.ShapeDtypeStruct((WIDE, ROWS...  19 us
    ppermute x12, starting transfers between devices, shift(): return lax.ppermute(x, axis, [(i, (i + by) % n) for i in range(n)])  15 us
    all_gather x1, blocking collectives, body(): first = lax.all_gather(right[:4], 'row', axis=1)  13.6 us
    all_gather x1, blocking collectives, body(): second = lax.all_gather(right[4:], 'row', axis=1)  13.2 us
    ppermute x1, waiting for transfers between devices, body(): return lax.ppermute(done, ('col', 'depth'), home).T  12.2 us
    all_to_all x1, starting transfers between devices, body(): right = lax.all_to_all(right, 'depth', 0, 0)  8.47 us
    all_to_all x1, waiting for transfers between devices, body(): right = lax.all_to_all(right, 'depth', 0, 0)  5.76 us
  transfers between devices with their start and end apart: 14, of which 9 were waited for; matrix products, arithmetic and copies ran while one was open for 4% of the time, Pallas kernels for 0%

profile of v1, /device:TPU:16, one launch (start us, length us, event | category | flops | bytes accessed | tf_op | source)
XLA Modules:
  0.0 137.2 jit_solution(856172273322645987)
XLA Ops:
  0.0 0.7 convert_bitcast_fusion.1
  0.7 0.8 copy.35
  1.5 0.6 pad.23.clone
  2.1 0.6 pad.21.left_cols_ref
  2.7 0.9 pad_convert_fusion.1
  3.7 0.8 reshape.31.right_ref
  4.4 1.0 copy.57
  5.4 0.8 pad_convert_fusion.left_ref
  6.2 2.8 %shard_map.46 = (bf16[48,24,128]{2,1,0:T(8,128)(2,1)}, bf16[8,3,24,128]{3,2,1,0:T(8,128)(2,1)}) custom-call(f32[4,48,640]{2,1,0:T(8,128)} %pad_convert_fusion.left_ref, f32[48,128]{1,0:T(8,128)} %pad.21.left_cols_ref, f32[5,16,640]{2,1,0:T(8,128)} %reshape.31.right_ref, f32[16,128]{1,0:T(8,128)} %bitcast.32), custom_call_target="tpu_custom_call" | custom-call | tf_op jit(solution)/shard_map/pallas_call | solution.py:84
  9.0 8.5 %all-to-all-start = ((bf16[8,3,24,128]{3,2,1,0:T(8,128)(2,1)}), bf16[8,3,24,128]{3,2,1,0:T(8,128)(2,1)S(1)}, u32[]{:S(2)}, u32[]{:S(2)}) async-start(bf16[8,3,24,128]{3,2,1,0:T(8,128)(2,1)} %get-tuple-element.8), calls=%async_computation | async-start | bytes 294912 | tf_op jit(solution)/shard_map/all_to_all | solution.py:176
  17.5 3.2 %collective-permute-start.1 = (bf16[48,24,128]{2,1,0:T(8,128)(2,1)}, bf16[48,24,128]{2,1,0:T(8,128)(2,1)S(1)}, u32[]{:S(2)}, u32[]{:S(2)}) collective-permute-start(bf16[48,24,128]{2,1,0:T(8,128)(2,1)} %get-tuple-element.7.refs_0_), channel_id=1, source_target_pairs={{0,7},{1,0},{2,1},{3,2},{4,3},{5,4},{6,5},{7,6},{8,15},{9,8},{10,9... | collective-permute-start | bytes 884744 | tf_op jit(solution)/shard_map/ppermute | solution.py:159
  20.7 1.0 slice.69
  21.8 0.1 copy.38
  21.9 5.8 %all-to-all-done = bf16[8,3,24,128]{3,2,1,0:T(8,128)(2,1)S(1)} async-done(((bf16[8,3,24,128]{3,2,1,0:T(8,128)(2,1)}), bf16[8,3,24,128]{3,2,1,0:T(8,128)(2,1)S(1)}, u32[]{:S(2)}, u32[]{:S(2)}) %all-to-all-start) | async-done | bytes 147488 | tf_op jit(solution)/shard_map/all_to_all | solution.py:176
  27.7 13.6 %all-gather = bf16[4,24,24,128]{3,2,1,0:T(8,128)(2,1)S(1)} all-gather(bf16[4,3,24,128]{3,2,1,0:T(8,128)(2,1)S(1)} %get-tuple-element.13), channel_id=2, replica_groups=mesh['row'=8,'col'=4,'depth'=8] {'row'}, dimensions={1}, use_global_device_ids=true | all-gather | bytes 663552 | tf_op jit(solution)/shard_map/all_gather | solution.py:177
  41.3 13.2 %all-gather.1 = bf16[4,24,24,128]{3,2,1,0:T(8,128)(2,1)S(1)} all-gather(bf16[4,3,24,128]{3,2,1,0:T(8,128)(2,1)S(1)} %get-tuple-element.14), channel_id=3, replica_groups=mesh['row'=8,'col'=4,'depth'=8] {'row'}, dimensions={1}, use_global_device_ids=true | all-gather | bytes 663552 | tf_op jit(solution)/shard_map/all_gather | solution.py:178
  54.5 0.1 pad_maximum_fusion
  54.6 0.4 collective-permute-start.3
  55.0 1.7 %collective-permute-start.2 = (bf16[48,24,128]{2,1,0:T(8,128)(2,1)S(1)}, bf16[48,24,128]{2,1,0:T(8,128)(2,1)}, u32[]{:S(2)}, u32[]{:S(2)}) collective-permute-start(bf16[48,24,128]{2,1,0:T(8,128)(2,1)S(1)} %collective-permute-done.refs_1_), channel_id=1, source_target_pairs={{0,1},{1,2},{2,3},{3,4},{4,5},{5,6},{6,7},{7,0},{8,9},{9,10},{10,1... | collective-permute-start | bytes 884744 | tf_op jit(solution)/shard_map/ppermute | solution.py:159
  56.7 0.4 fusion.3
  57.1 0.2 sub.25
  57.4 0.6 fusion.8.dest_ref
  58.0 0.1 copy.40
  58.1 5.9 %collective-permute-done.3.refs_4_ = bf16[48,24,128]{2,1,0:T(8,128)(2,1)S(1)} collective-permute-done((bf16[48,24,128]{2,1,0:T(8,128)(2,1)S(1)}, bf16[48,24,128]{2,1,0:T(8,128)(2,1)S(1)}, u32[]{:S(2)}, u32[]{:S(2)}) %collective-permute-start.3) | collective-permute-done | bytes 294944 | tf_op jit(solution)/shard_map/ppermute | solution.py:159
  64.0 1.6 %collective-permute-start.5 = (bf16[48,24,128]{2,1,0:T(8,128)(2,1)S(1)}, bf16[48,24,128]{2,1,0:T(8,128)(2,1)S(1)}, u32[]{:S(2)}, u32[]{:S(2)}) collective-permute-start(bf16[48,24,128]{2,1,0:T(8,128)(2,1)S(1)} %collective-permute-done.3.refs_4_), channel_id=1, source_target_pairs={{0,7},{1,0},{2,1},{3,2},{4,3},{5,4},{6,5},{7,6},{8,15},{9,8},{10,9... | collective-permute-start | bytes 884744 | tf_op jit(solution)/shard_map/ppermute | solution.py:159
  65.5 0.5 collective-permute-start.4
  66.3 0.9 slice.91
  67.3 5.1 %collective-permute-done.5.refs_6_ = bf16[48,24,128]{2,1,0:T(8,128)(2,1)S(1)} collective-permute-done((bf16[48,24,128]{2,1,0:T(8,128)(2,1)S(1)}, bf16[48,24,128]{2,1,0:T(8,128)(2,1)S(1)}, u32[]{:S(2)}, u32[]{:S(2)}) %collective-permute-start.5) | collective-permute-done | bytes 294944 | tf_op jit(solution)/shard_map/ppermute | solution.py:159
  72.5 2.7 %collective-permute-start.7 = (bf16[24,24,128]{2,1,0:T(8,128)(2,1)S(1)}, bf16[24,24,128]{2,1,0:T(8,128)(2,1)S(1)}, u32[]{:S(2)}, u32[]{:S(2)}) collective-permute-start(bf16[24,24,128]{2,1,0:T(8,128)(2,1)S(1)} %slice.96), channel_id=1, source_target_pairs={{0,7},{1,0},{2,1},{3,2},{4,3},{5,4},{6,5},{7,6},{8,15},{9,8},{10,9... | collective-permute-start | bytes 442376 | tf_op jit(solution)/shard_map/ppermute | solution.py:159
  75.4 0.3 collective-permute-start.6
  75.8 6.2 %collective-permute-done.6 = bf16[24,24,128]{2,1,0:T(8,128)(2,1)S(1)} collective-permute-done((bf16[24,24,128]{2,1,0:T(8,128)(2,1)S(1)}, bf16[24,24,128]{2,1,0:T(8,128)(2,1)S(1)}, u32[]{:S(2)}, u32[]{:S(2)}) %collective-permute-start.6) | collective-permute-done | bytes 147488 | tf_op jit(solution)/shard_map/ppermute | solution.py:159
  82.3 0.2 copy.54
  82.4 0.7 reshape.28.lidx_ref
  83.2 19.0 %shard_map.47 = f32[384,1104]{1,0:T(8,128)} custom-call(s32[1536]{0:T(1024)} %reshape.28.lidx_ref, s32[960]{0:T(1024)} %fusion.8.dest_ref, bf16[64,3,24,128]{3,2,1,0:T(8,128)(2,1)} %bitcast.28, bf16[48,24,128]{2,1,0:T(8,128)(2,1)} %get-tuple-element.7.refs_0_, bf16[48,24,128]{2,1,0:T(8,128)(2,1)} %copy-done.6, bf16[48,24,128]{2,1,0:T(8,128)(2,1)} %copy-done.5, ...), custom_call_target="tpu_custom_call" | custom-call | flops 6000000000 | bytes 8000000 | tf_op jit(solution)/shard_map/pallas_call | solution.py:143
  102.2 1.2 fusion.11
  103.4 0.5 collective-permute-start.10
  103.9 0.9 slice.103
  104.9 1.7 %collective-permute-start.8 = (f32[48,1104]{1,0:T(8,128)S(1)}, f32[48,1104]{1,0:T(8,128)S(1)}, u32[]{:S(2)}, u32[]{:S(2)}) collective-permute-start(f32[48,1104]{1,0:T(8,128)S(1)} %slice.103), channel_id=1, source_target_pairs={{0,8},{8,16},{16,24},{24,0},{1,9},{9,17},{17,25},{25,1},{2,10},{10... | collective-permute-start | bytes 635912 | tf_op jit(solution)/shard_map/ppermute | solution.py:159
  106.5 2.9 %collective-permute-done.10 = f32[44,1104]{1,0:T(8,128)S(1)} collective-permute-done((f32[44,1104]{1,0:T(8,128)S(1)}, f32[44,1104]{1,0:T(8,128)S(1)}, u32[]{:S(2)}, u32[]{:S(2)}) %collective-permute-start.10) | collective-permute-done | bytes 194336 | tf_op jit(solution)/shard_map/ppermute | solution.py:159
  109.4 1.0 slice_add_fusion.1
  110.4 0.5 collective-permute-done.8
  111.0 1.5 %collective-permute-start.11 = (f32[92,1104]{1,0:T(8,128)S(1)}, f32[92,1104]{1,0:T(8,128)S(1)}, u32[]{:S(2)}, u32[]{:S(2)}) collective-permute-start(f32[92,1104]{1,0:T(8,128)S(1)} %pad_maximum_fusion.2), channel_id=1, source_target_pairs={{0,24},{8,0},{16,8},{24,16},{1,25},{9,1},{17,9},{25,17},{2,26},{10... | collective-permute-start | bytes 1218824 | tf_op jit(solution)/shard_map/ppermute | solution.py:159
  112.5 0.9 collective-permute-start.9
  113.4 6.2 %collective-permute-done.11 = f32[92,1104]{1,0:T(8,128)S(1)} collective-permute-done((f32[92,1104]{1,0:T(8,128)S(1)}, f32[92,1104]{1,0:T(8,128)S(1)}, u32[]{:S(2)}, u32[]{:S(2)}) %collective-permute-start.11) | collective-permute-done | bytes 406304 | tf_op jit(solution)/shard_map/ppermute | solution.py:159
  119.6 2.7 %collective-permute-done.9 = f32[92,1104]{1,0:T(8,128)S(1)} collective-permute-done((f32[92,1104]{1,0:T(8,128)S(1)}, f32[92,1104]{1,0:T(8,128)S(1)}, u32[]{:S(2)}, u32[]{:S(2)}) %collective-permute-start.9) | collective-permute-done | bytes 406304 | tf_op jit(solution)/shard_map/ppermute | solution.py:159
  122.3 1.9 %collective-permute-start.12 = (bf16[92,1104]{1,0:T(8,128)(2,1)S(1)}, bf16[92,1104]{1,0:T(8,128)(2,1)S(1)}, u32[]{:S(2)}, u32[]{:S(2)}) collective-permute-start(bf16[92,1104]{1,0:T(8,128)(2,1)S(1)} %fusion.1), channel_id=1, source_target_pairs={{0,0},{1,4},{2,8},{3,12},{4,16},{5,20},{6,24},{7,28},{8,1},{9,5},{... | collective-permute-start | bytes 609416 | tf_op jit(solution)/shard_map/ppermute | solution.py:198
  124.3 12.2 %collective-permute-done.12 = bf16[92,1104]{1,0:T(8,128)(2,1)S(1)} collective-permute-done((bf16[92,1104]{1,0:T(8,128)(2,1)S(1)}, bf16[92,1104]{1,0:T(8,128)(2,1)S(1)}, u32[]{:S(2)}, u32[]{:S(2)}) %collective-permute-start.12) | collective-permute-done | bytes 203168 | tf_op jit(solution)/shard_map/ppermute | solution.py:198
  136.5 0.7 copy.60
  (59 shorter events, 1.2 us)
Async XLA Ops:
  9.0 18.6 %all-to-all-start = ((bf16[8,3,24,128]{3,2,1,0:T(8,128)(2,1)}), bf16[8,3,24,128]{3,2,1,0:T(8,128)(2,1)S(1)}, u32[]{:S(2)}, u32[]{:S(2)}) async-start(bf16[8,3,24,128]{3,2,1,0:T(8,128)(2,1)} %get-tuple-element.8), calls=%async_computation | async-start | bytes 294912 | tf_op jit(solution)/shard_map/all_to_all | solution.py:176
  17.5 37.1 %collective-permute-start.1 = (bf16[48,24,128]{2,1,0:T(8,128)(2,1)}, bf16[48,24,128]{2,1,0:T(8,128)(2,1)S(1)}, u32[]{:S(2)}, u32[]{:S(2)}) collective-permute-start(bf16[48,24,128]{2,1,0:T(8,128)(2,1)} %get-tuple-element.7.refs_0_), channel_id=1, source_target_pairs={{0,7},{1,0},{2,1},{3,2},{4,3},{5,4},{6,5},{7,6},{8,15},{9,8},{10,9... | collective-permute-start | bytes 884744 | tf_op jit(solution)/shard_map/ppermute | solution.py:159
  20.7 34.3 %collective-permute-start = (bf16[48,24,128]{2,1,0:T(8,128)(2,1)}, bf16[48,24,128]{2,1,0:T(8,128)(2,1)S(1)}, u32[]{:S(2)}, u32[]{:S(2)}) collective-permute-start(bf16[48,24,128]{2,1,0:T(8,128)(2,1)} %get-tuple-element.7.refs_0_), channel_id=1, source_target_pairs={{0,1},{1,2},{2,3},{3,4},{4,5},{5,6},{6,7},{7,0},{8,9},{9,10},{10,1... | collective-permute-start | bytes 884744 | tf_op jit(solution)/shard_map/ppermute | solution.py:159
  54.6 28.6 %copy-start.1 = (bf16[8,8,3,24,128]{4,3,2,1,0:T(8,128)(2,1)}, bf16[8,8,3,24,128]{4,3,2,1,0:T(8,128)(2,1)S(1)}, u32[]{:S(2)}) copy-start(bf16[8,8,3,24,128]{4,3,2,1,0:T(8,128)(2,1)S(1)} %pad_maximum_fusion) | copy-start | bytes 3538948
  54.6 28.6 %copy-start.5 = (bf16[48,24,128]{2,1,0:T(8,128)(2,1)}, bf16[48,24,128]{2,1,0:T(8,128)(2,1)S(1)}, u32[]{:S(2)}) copy-start(bf16[48,24,128]{2,1,0:T(8,128)(2,1)S(1)} %collective-permute-done.1.refs_2_) | copy-start | bytes 884740
  54.6 9.3 %collective-permute-start.3 = (bf16[48,24,128]{2,1,0:T(8,128)(2,1)S(1)}, bf16[48,24,128]{2,1,0:T(8,128)(2,1)S(1)}, u32[]{:S(2)}, u32[]{:S(2)}) collective-permute-start(bf16[48,24,128]{2,1,0:T(8,128)(2,1)S(1)} %collective-permute-done.1.refs_2_), channel_id=1, source_target_pairs={{0,7},{1,0},{2,1},{3,2},{4,3},{5,4},{6,5},{7,6},{8,15},{9,8},{10,9... | collective-permute-start | bytes 884744 | tf_op jit(solution)/shard_map/ppermute | solution.py:159
  55.0 28.1 %copy-start.6 = (bf16[48,24,128]{2,1,0:T(8,128)(2,1)}, bf16[48,24,128]{2,1,0:T(8,128)(2,1)S(1)}, u32[]{:S(2)}) copy-start(bf16[48,24,128]{2,1,0:T(8,128)(2,1)S(1)} %collective-permute-done.refs_1_) | copy-start | bytes 884740
  55.0 10.5 %collective-permute-start.2 = (bf16[48,24,128]{2,1,0:T(8,128)(2,1)S(1)}, bf16[48,24,128]{2,1,0:T(8,128)(2,1)}, u32[]{:S(2)}, u32[]{:S(2)}) collective-permute-start(bf16[48,24,128]{2,1,0:T(8,128)(2,1)S(1)} %collective-permute-done.refs_1_), channel_id=1, source_target_pairs={{0,1},{1,2},{2,3},{3,4},{4,5},{5,6},{6,7},{7,0},{8,9},{9,10},{10,1... | collective-permute-start | bytes 884744 | tf_op jit(solution)/shard_map/ppermute | solution.py:159
  64.0 3.4 %copy-start.7 = (bf16[48,24,128]{2,1,0:T(8,128)(2,1)}, bf16[48,24,128]{2,1,0:T(8,128)(2,1)S(1)}, u32[]{:S(2)}) copy-start(bf16[48,24,128]{2,1,0:T(8,128)(2,1)S(1)} %collective-permute-done.3.refs_4_) | copy-start | bytes 884740
  64.0 8.5 %collective-permute-start.5 = (bf16[48,24,128]{2,1,0:T(8,128)(2,1)S(1)}, bf16[48,24,128]{2,1,0:T(8,128)(2,1)S(1)}, u32[]{:S(2)}, u32[]{:S(2)}) collective-permute-start(bf16[48,24,128]{2,1,0:T(8,128)(2,1)S(1)} %collective-permute-done.3.refs_4_), channel_id=1, source_target_pairs={{0,7},{1,0},{2,1},{3,2},{4,3},{5,4},{6,5},{7,6},{8,15},{9,8},{10,9... | collective-permute-start | bytes 884744 | tf_op jit(solution)/shard_map/ppermute | solution.py:159
  65.5 9.7 %collective-permute-start.4 = (bf16[48,24,128]{2,1,0:T(8,128)(2,1)}, bf16[48,24,128]{2,1,0:T(8,128)(2,1)S(1)}, u32[]{:S(2)}, u32[]{:S(2)}) collective-permute-start(bf16[48,24,128]{2,1,0:T(8,128)(2,1)} %collective-permute-done.2.refs_3_), channel_id=1, source_target_pairs={{0,1},{1,2},{2,3},{3,4},{4,5},{5,6},{6,7},{7,0},{8,9},{9,10},{10,1... | collective-permute-start | bytes 884744 | tf_op jit(solution)/shard_map/ppermute | solution.py:159
  72.5 10.7 %copy-start.2 = (bf16[48,24,128]{2,1,0:T(8,128)(2,1)}, bf16[48,24,128]{2,1,0:T(8,128)(2,1)S(1)}, u32[]{:S(2)}) copy-start(bf16[48,24,128]{2,1,0:T(8,128)(2,1)S(1)} %collective-permute-done.5.refs_6_) | copy-start | bytes 884740
  72.5 9.5 %collective-permute-start.7 = (bf16[24,24,128]{2,1,0:T(8,128)(2,1)S(1)}, bf16[24,24,128]{2,1,0:T(8,128)(2,1)S(1)}, u32[]{:S(2)}, u32[]{:S(2)}) collective-permute-start(bf16[24,24,128]{2,1,0:T(8,128)(2,1)S(1)} %slice.96), channel_id=1, source_target_pairs={{0,7},{1,0},{2,1},{3,2},{4,3},{5,4},{6,5},{7,6},{8,15},{9,8},{10,9... | collective-permute-start | bytes 442376 | tf_op jit(solution)/shard_map/ppermute | solution.py:159
  75.2 8.0 %copy-start.3 = (bf16[48,24,128]{2,1,0:T(8,128)(2,1)}, bf16[48,24,128]{2,1,0:T(8,128)(2,1)S(1)}, u32[]{:S(2)}) copy-start(bf16[48,24,128]{2,1,0:T(8,128)(2,1)S(1)} %collective-permute-done.4.refs_5_) | copy-start | bytes 884740
  75.4 6.6 %collective-permute-start.6 = (bf16[24,24,128]{2,1,0:T(8,128)(2,1)S(1)}, bf16[24,24,128]{2,1,0:T(8,128)(2,1)S(1)}, u32[]{:S(2)}, u32[]{:S(2)}) collective-permute-start(bf16[24,24,128]{2,1,0:T(8,128)(2,1)S(1)} %slice.95), channel_id=1, source_target_pairs={{0,1},{1,2},{2,3},{3,4},{4,5},{5,6},{6,7},{7,0},{8,9},{9,10},{10,1... | collective-permute-start | bytes 442376 | tf_op jit(solution)/shard_map/ppermute | solution.py:159
  82.1 1.1 copy-start.4
  102.2 8.7 %copy-start = (f32[384,1104]{1,0:T(8,128)S(1)}, f32[384,1104]{1,0:T(8,128)}, u32[]{:S(2)}) copy-start(f32[384,1104]{1,0:T(8,128)} %shard_map.47) | copy-start | bytes 5087236
  103.4 6.0 %collective-permute-start.10 = (f32[44,1104]{1,0:T(8,128)S(1)}, f32[44,1104]{1,0:T(8,128)S(1)}, u32[]{:S(2)}, u32[]{:S(2)}) collective-permute-start(f32[44,1104]{1,0:T(8,128)S(1)} %get-tuple-element.12), channel_id=1, source_target_pairs={{0,24},{8,0},{16,8},{24,16},{1,25},{9,1},{17,9},{25,17},{2,26},{10... | collective-permute-start | bytes 582920 | tf_op jit(solution)/shard_map/ppermute | solution.py:159
  104.9 6.0 %collective-permute-start.8 = (f32[48,1104]{1,0:T(8,128)S(1)}, f32[48,1104]{1,0:T(8,128)S(1)}, u32[]{:S(2)}, u32[]{:S(2)}) collective-permute-start(f32[48,1104]{1,0:T(8,128)S(1)} %slice.103), channel_id=1, source_target_pairs={{0,8},{8,16},{16,24},{24,0},{1,9},{9,17},{17,25},{25,1},{2,10},{10... | collective-permute-start | bytes 635912 | tf_op jit(solution)/shard_map/ppermute | solution.py:159
  111.0 8.6 %collective-permute-start.11 = (f32[92,1104]{1,0:T(8,128)S(1)}, f32[92,1104]{1,0:T(8,128)S(1)}, u32[]{:S(2)}, u32[]{:S(2)}) collective-permute-start(f32[92,1104]{1,0:T(8,128)S(1)} %pad_maximum_fusion.2), channel_id=1, source_target_pairs={{0,24},{8,0},{16,8},{24,16},{1,25},{9,1},{17,9},{25,17},{2,26},{10... | collective-permute-start | bytes 1218824 | tf_op jit(solution)/shard_map/ppermute | solution.py:159
  112.5 9.7 %collective-permute-start.9 = (f32[92,1104]{1,0:T(8,128)S(1)}, f32[92,1104]{1,0:T(8,128)S(1)}, u32[]{:S(2)}, u32[]{:S(2)}) collective-permute-start(f32[92,1104]{1,0:T(8,128)S(1)} %pad_maximum_fusion.1), channel_id=1, source_target_pairs={{0,8},{8,16},{16,24},{24,0},{1,9},{9,17},{17,25},{25,1},{2,10},{10... | collective-permute-start | bytes 1218824 | tf_op jit(solution)/shard_map/ppermute | solution.py:159
  122.3 14.1 %collective-permute-start.12 = (bf16[92,1104]{1,0:T(8,128)(2,1)S(1)}, bf16[92,1104]{1,0:T(8,128)(2,1)S(1)}, u32[]{:S(2)}, u32[]{:S(2)}) collective-permute-start(bf16[92,1104]{1,0:T(8,128)(2,1)S(1)} %fusion.1), channel_id=1, source_target_pairs={{0,0},{1,4},{2,8},{3,12},{4,16},{5,20},{6,24},{7,28},{8,1},{9,5},{... | collective-permute-start | bytes 609416 | tf_op jit(solution)/shard_map/ppermute | solution.py:198

commit v2 on v1

--- a/solution.py
+++ b/solution.py
@@ -1,5 +1,3 @@
-import functools
-
 import jax
 import jax.numpy as jnp
 from jax import lax
@@ -7,19 +5,20 @@
 from jax.experimental.pallas import tpu as pltpu
 from jax.sharding import PartitionSpec as P
 
+
 BLK = 23
 LANES = 128
 APAD = 24
 KROW = 32
 SLOTS = 4
 USLOTS = 3
-TILES = 4
 PANEL = 40
 HERE = 5
 GROUP = 8
 CHUNK = 96
 WIDE = 4 * CHUNK
 ROWS = 48
+OFFSETS = (0, 7, 1, 6, 2, 5, 3, 4)
 
 
 def place(z, windows, lane, src, dst):
@@ -34,7 +33,7 @@
     return z
 
 
-def pack_kernel(left_ref, left_cols_ref, right_ref, right_cols_ref, left_out, right_out, left_tmp, right_tmp):
+def pack_kernel(left_ref, right_ref, right_cols_ref, left_out, right_out, left_tmp, right_tmp):
     lane = lax.broadcasted_iota(jnp.int32, (ROWS, LANES), 1)
     for a in range(BLK):
         z = jnp.zeros((ROWS, LANES), jnp.float32)
@@ -47,7 +46,7 @@
                 KROW * s,
             )
         left_tmp[pl.ds(a, ROWS, stride=APAD), :] = z
-    left_tmp[pl.ds(BLK, ROWS, stride=APAD), :] = left_cols_ref[...]
+    left_tmp[pl.ds(BLK, ROWS, stride=APAD), :] = jnp.zeros((ROWS, LANES), jnp.float32)
     for i in range(ROWS):
         left_out[i] = left_tmp[i * APAD : (i + 1) * APAD, :].astype(jnp.bfloat16)
     lane = lax.broadcasted_iota(jnp.int32, (16, LANES), 1)
@@ -65,7 +64,7 @@
     right_tmp[pl.ds(BLK, 16, stride=APAD), :] = right_cols_ref[...]
     for d in range(GROUP):
         for u in range(USLOTS):
-            row = (d // 2) * 4 + u
+            row = (d % 4) * 4 + u
             right_out[d, u] = right_tmp[row * APAD : (row + 1) * APAD, :].astype(jnp.bfloat16)
 
 
@@ -74,33 +73,39 @@
     left = jnp.pad(
         jnp.transpose(left_values[:, 0].astype(jnp.float32), (1, 0, 2)), ((0, 0), (0, 0), (0, wide - BLK * BLK))
     )
-    left_cols = jnp.pad(left_columns[:, 0].astype(jnp.float32), ((0, 0), (0, LANES - SLOTS)))
     right = jnp.pad(
         right_values[0].astype(jnp.float32), ((0, 0), (0, 0), (0, 1), (0, wide - BLK * BLK))
     ).reshape(HERE, 16, wide)
+    left_cols = jnp.pad(left_columns[:, 0].astype(jnp.float32).reshape(2, 96), ((0, 2), (16, 16)))
     right_cols = jnp.pad(
         jnp.transpose(right_columns[0], (1, 2, 0)).astype(jnp.float32), ((0, 0), (0, 1), (0, LANES - HERE))
-    ).reshape(16, LANES)
+    )
+    right_cols = (right_cols + left_cols[None]).reshape(16, LANES)
     return pl.pallas_call(
         pack_kernel,
         out_shape=(
             jax.ShapeDtypeStruct((ROWS, APAD, LANES), jnp.bfloat16),
             jax.ShapeDtypeStruct((GROUP, USLOTS, APAD, LANES), jnp.bfloat16),
         ),
-        in_specs=[pl.BlockSpec(memory_space=pltpu.VMEM)] * 4,
+        in_specs=[pl.BlockSpec(memory_space=pltpu.VMEM)] * 3,
         out_specs=(pl.BlockSpec(memory_space=pltpu.VMEM),) * 2,
         scratch_shapes=[
             pltpu.VMEM((ROWS * APAD, LANES), jnp.float32),
             pltpu.VMEM((16 * APAD, LANES), jnp.float32),
         ],
-    )(left, left_cols, right, right_cols)
-
-
-def product_kernel(lidx_ref, dest_ref, right_ref, *refs):
+    )(left, right, right_cols)
+
+
+def product_kernel(meta_ref, lcol_ref, dest_ref, right_ref, *refs):
     lefts, (out_ref, wide_ref, sum_ref, part_ref) = refs[:GROUP], refs[GROUP:]
     lane = lax.broadcasted_iota(jnp.int32, (APAD, WIDE), 1)
 
+    depth, core = meta_ref[0], meta_ref[1]
+    panels = [(depth + o) % GROUP for o in OFFSETS]
+
     def fill(n, carry):
+        row = 2 * ((n // GROUP) % 4) + lax.bitwise_xor(core, n // 32)
+        base = (n % GROUP) * PANEL + row * HERE
         for k in range(HERE):
             z = jnp.zeros((APAD, WIDE), jnp.float32)
             for u in range(USLOTS):
@@ -112,7 +117,7 @@
             full = jnp.concatenate([z, jnp.zeros((KROW - APAD, WIDE), jnp.float32)], axis=0)
             full = full.astype(jnp.bfloat16)
             for q in range(3):
-                wide_ref[n * HERE + k, q] = full[:, q * LANES : (q + 1) * LANES]
+                wide_ref[base + k, q] = full[:, q * LANES : (q + 1) * LANES]
         return carry
 
     lax.fori_loop(0, 8 * GROUP, fill, 0)
@@ -122,7 +127,11 @@
             i = g * 8 + m
             total = jnp.zeros((APAD, WIDE), jnp.float32)
             for j in range(0, GROUP, 2):
-                at = [lidx_ref[(i * GROUP + j) * SLOTS + s] for s in range(2 * SLOTS)]
+                at = [
+                    panels[h] * PANEL + lcol_ref[panels[h] * (ROWS * SLOTS) + i * SLOTS + s]
+                    for h in (j, j + 1)
+                    for s in range(SLOTS)
+                ]
                 weights = jnp.concatenate(
                     [jnp.concatenate([wide_ref[n, q] for n in at], axis=0) for q in range(3)], axis=1
                 )
@@ -139,11 +148,11 @@
         out_ref[q * LANES : (q + 1) * LANES, :] = turned[:, :count]
 
 
-def product(lidx, dest, right, lefts):
+def product(meta, lcol, dest, right, lefts):
     return pl.pallas_call(
         product_kernel,
         out_shape=jax.ShapeDtypeStruct((WIDE, ROWS * BLK), jnp.float32),
-        in_specs=[pl.BlockSpec(memory_space=pltpu.SMEM)] * 2
+        in_specs=[pl.BlockSpec(memory_space=pltpu.SMEM)] * 3
         + [pl.BlockSpec(memory_space=pltpu.VMEM)] * (1 + GROUP),
         out_specs=pl.BlockSpec(memory_space=pltpu.VMEM),
         scratch_shapes=[
@@ -152,7 +161,7 @@
             pltpu.VMEM((8 * APAD, WIDE), jnp.float32),
         ],
         cost_estimate=pl.CostEstimate(flops=6_000_000_000, bytes_accessed=8_000_000, transcendentals=0),
-    )(lidx, dest, right, *lefts)
+    )(meta, lcol, dest, right, *lefts)
 
 
 def shift(x, axis, by, n):
@@ -166,26 +175,26 @@
     half = ROWS // 2
     f4, b4 = shift(f3[:half], "depth", 1, 8), shift(b3[half:], "depth", -1, 8)
     far = jnp.concatenate([f4, b4], axis=0)
-    return [own, f1, b1, f2, b2, f3, b3, far], (0, -1, 1, -2, 2, -3, 3, 4)
+    return [own, f1, b1, f2, b2, f3, b3, far]
 
 
 def body(left_values, left_columns, right_values, right_columns):
     c, d = lax.axis_index("col"), lax.axis_index("depth")
     left, right = pack(left_values, left_columns, right_values, right_columns)
-    lefts, offsets = gather_depth(left)
+    lefts = gather_depth(left)
     right = lax.all_to_all(right, "depth", 0, 0)
-    first = lax.all_gather(right[:4], "row", axis=1)
-    second = lax.all_gather(right[4:], "row", axis=1)
-    right = jnp.concatenate([first, second], axis=0).reshape(64, USLOTS, APAD, LANES)
+    lcol = right[:, :2, BLK, 16:112].reshape(-1).astype(jnp.int32)
+    mine = lax.all_gather(right, "row", axis=0, axis_index_groups=[[0, 2, 4, 6], [1, 3, 5, 7]])
+    other = lax.ppermute(mine, "row", [(i, i ^ 1) for i in range(8)])
+    right = jnp.concatenate([mine, other], axis=0).reshape(64, USLOTS, APAD, LANES)
     rcol = right[:, :, BLK, :HERE].astype(jnp.int32)
-    local = rcol - 16 * (d % 2)
+    local = rcol - 16 * (d // 4)
+    chunk = lax.bitwise_xor(local // 4, d % 4)
     dest = jnp.where(
-        (local >= 0) & (local < 16), CHUNK * ((local // 4 - c) % 4) + BLK * (local % 4), 4 * LANES
-    )
-    lidx = jnp.stack(
-        [x[:, BLK, :SLOTS].astype(jnp.int32) + PANEL * ((d + o) % 8) for x, o in zip(lefts, offsets)], axis=1
-    )
-    parts = product(lidx.reshape(-1), dest.reshape(-1), right, lefts)
+        (local >= 0) & (local < 16), CHUNK * ((chunk - c) % 4) + BLK * (local % 4), 4 * LANES
+    )
+    meta = jnp.stack([d, lax.axis_index("row") % 2])
+    parts = product(meta, lcol, dest.reshape(-1), right, lefts)
     own, ahead, far, behind = (parts[CHUNK * q : CHUNK * q + 4 * BLK] for q in range(4))
     cut = 48
     from_behind = shift(far[:cut], "col", 1, 4)
@@ -194,7 +203,7 @@
     behind = jnp.concatenate([behind[:cut], behind[cut:] + from_ahead], axis=0)
     total = own + shift(ahead, "col", 1, 4) + shift(behind, "col", -1, 4)
     done = total.astype(jnp.bfloat16)
-    home = [(y * 8 + z, (z // 2) * 8 + (z % 2) * 4 + y) for y in range(4) for z in range(8)]
+    home = [(y * 8 + z, (z % 4) * 8 + (z // 4) * 4 + (y ^ (z % 4))) for y in range(4) for z in range(8)]
     return lax.ppermute(done, ("col", "depth"), home).T
 
 

time: 138 us -> 119 us (0.86)
  blocking collectives: 26.8 us -> 13.9 us
  local copies, waits for them, and re-layouts: 10.7 us -> 6.42 us
  waiting for transfers between devices: 47.3 us -> 44.5 us
  other arithmetic: 4.76 us -> 6.84 us
    all_gather x2 -> x1, blocking collectives: 26.8 us -> 13.9 us  [body(): lax.all_gather(right, 'row', axis=0, axis_index_groups=[[0, 2, 4, 6], [1,...]
    ppermute x1, waiting for transfers between devices: 12.2 us -> 7.56 us  [body(): return lax.ppermute(done, ('col', 'depth'), home).T]
    slice x17 -> x0, local copies, waits for them, and re-layouts: 2.88 us -> none  [the longest x16 2.86 us: body(): x[:, BLK, :SLOTS].astype(jnp.int32) + PANEL * ((d + o) % 8)]
  transfers between devices with their start and end apart: 14 -> 15, of which waited for: 9 -> 10; matrix products, arithmetic and copies ran while one was open for 4% -> 4% of each run, Pallas kernels for 0% -> 0%
where the time goes in v2:
time: 119 us
  waiting for transfers between devices  44.5 us (37%)
  starting transfers between devices  25.2 us (21%)
  Pallas kernels  21.9 us (18%)
  blocking collectives  13.9 us (12%)
  other arithmetic  6.84 us (6%)
  local copies, waits for them, and re-layouts  6.42 us (5%)
    ppermute x12, waiting for transfers between devices, shift(): return lax.ppermute(x, axis, [(i, (i + by) % n) for i in range(n)])  30 us
    pallas_call x1, Pallas kernels, product(): pl.pallas_call(product_kernel, out_shape=jax.ShapeDtypeStruct((WIDE, ROWS...  19.1 us
    ppermute x12, starting transfers between devices, shift(): return lax.ppermute(x, axis, [(i, (i + by) % n) for i in range(n)])  14.7 us
    all_gather x1, blocking collectives, body(): lax.all_gather(right, 'row', axis=0, axis_index_groups=[[0, 2, 4, 6], [1,...  13.9 us
    all_to_all x1, starting transfers between devices, body(): right = lax.all_to_all(right, 'depth', 0, 0)  8.47 us
    ppermute x1, waiting for transfers between devices, body(): return lax.ppermute(done, ('col', 'depth'), home).T  7.56 us
    all_to_all x1, waiting for transfers between devices, body(): right = lax.all_to_all(right, 'depth', 0, 0)  6.93 us
    pallas_call x1, Pallas kernels, pack(): pl.pallas_call(pack_kernel, out_shape=(jax.ShapeDtypeStruct((ROWS, APAD,...  2.85 us
  transfers between devices with their start and end apart: 15, of which 10 were waited for; matrix products, arithmetic and copies ran while one was open for 4% of the time, Pallas kernels for 0%

profile of v2, /device:TPU:16, one launch (start us, length us, event | category | flops | bytes accessed | tf_op | source)
XLA Modules:
  0.0 118.9 jit_solution(10276430090992299292)
XLA Ops:
  0.0 0.7 convert_element_type.50
  0.7 0.7 convert_bitcast_fusion
  1.4 0.1 copy.14
  1.5 0.1 convert_element_type.51
  1.6 0.1 pad.23
  1.7 0.6 copy.15
  2.3 0.9 pad_convert_fusion.1
  3.2 0.8 reshape.32.right_ref
  4.0 1.0 copy.17
  5.0 0.8 pad_convert_fusion.left_ref
  5.8 2.9 %shard_map.46 = (bf16[48,24,128]{2,1,0:T(8,128)(2,1)}, bf16[8,3,24,128]{3,2,1,0:T(8,128)(2,1)}) custom-call(f32[4,48,640]{2,1,0:T(8,128)} %pad_convert_fusion.left_ref, f32[5,16,640]{2,1,0:T(8,128)} %reshape.32.right_ref, f32[16,128]{1,0:T(8,128)} %bitcast.25), custom_call_target="tpu_custom_call" | custom-call | tf_op jit(solution)/shard_map/pallas_call | solution.py:84
  8.6 8.5 %all-to-all-start = ((bf16[8,3,24,128]{3,2,1,0:T(8,128)(2,1)}), bf16[8,3,24,128]{3,2,1,0:T(8,128)(2,1)S(1)}, u32[]{:S(2)}, u32[]{:S(2)}) async-start(bf16[8,3,24,128]{3,2,1,0:T(8,128)(2,1)} %get-tuple-element.7), calls=%async_computation | async-start | bytes 294912 | tf_op jit(solution)/shard_map/all_to_all | solution.py:185
  17.1 3.2 %collective-permute-start.2 = (bf16[48,24,128]{2,1,0:T(8,128)(2,1)}, bf16[48,24,128]{2,1,0:T(8,128)(2,1)S(1)}, u32[]{:S(2)}, u32[]{:S(2)}) collective-permute-start(bf16[48,24,128]{2,1,0:T(8,128)(2,1)} %get-tuple-element.8.refs_0_), channel_id=1, source_target_pairs={{0,7},{1,0},{2,1},{3,2},{4,3},{5,4},{6,5},{7,6},{8,15},{9,8},{10,9... | collective-permute-start | bytes 884744 | tf_op jit(solution)/shard_map/ppermute | solution.py:168
  20.3 6.9 %all-to-all-done = bf16[8,3,24,128]{3,2,1,0:T(8,128)(2,1)S(1)} async-done(((bf16[8,3,24,128]{3,2,1,0:T(8,128)(2,1)}), bf16[8,3,24,128]{3,2,1,0:T(8,128)(2,1)S(1)}, u32[]{:S(2)}, u32[]{:S(2)}) %all-to-all-start) | async-done | bytes 147488 | tf_op jit(solution)/shard_map/all_to_all | solution.py:185
  27.3 13.9 %all-gather = bf16[32,3,24,128]{3,2,1,0:T(8,128)(2,1)S(1)} all-gather(bf16[8,3,24,128]{3,2,1,0:T(8,128)(2,1)S(1)} %all-to-all-done), channel_id=2, replica_groups={{0,64,128,192},{32,96,160,224},{1,65,129,193},{33,97,161,225},{2,66,130..., dimensions={0}, use_global_device_ids=true | all-gather | bytes 737280 | tf_op jit(solution)/shard_map/all_gather | solution.py:187
  41.2 0.2 collective-permute-start.4
  41.5 1.9 %collective-permute-start.3 = (bf16[48,24,128]{2,1,0:T(8,128)(2,1)S(1)}, bf16[48,24,128]{2,1,0:T(8,128)(2,1)}, u32[]{:S(2)}, u32[]{:S(2)}) collective-permute-start(bf16[48,24,128]{2,1,0:T(8,128)(2,1)S(1)} %collective-permute-done.1.refs_1_), channel_id=1, source_target_pairs={{0,1},{1,2},{2,3},{3,4},{4,5},{5,6},{6,7},{7,0},{8,9},{9,10},{10,1... | collective-permute-start | bytes 884744 | tf_op jit(solution)/shard_map/ppermute | solution.py:168
  43.3 0.6 pad_add_fusion.1.meta_ref
  43.9 0.1 fusion.4
  44.0 0.7 reshape.33.lcol_ref
  44.7 6.0 %collective-permute-done.4.refs_4_ = bf16[48,24,128]{2,1,0:T(8,128)(2,1)} collective-permute-done((bf16[48,24,128]{2,1,0:T(8,128)(2,1)S(1)}, bf16[48,24,128]{2,1,0:T(8,128)(2,1)}, u32[]{:S(2)}, u32[]{:S(2)}) %collective-permute-start.4) | collective-permute-done | bytes 294944 | tf_op jit(solution)/shard_map/ppermute | solution.py:168
  50.8 1.5 %collective-permute-start.6 = (bf16[48,24,128]{2,1,0:T(8,128)(2,1)}, bf16[48,24,128]{2,1,0:T(8,128)(2,1)S(1)}, u32[]{:S(2)}, u32[]{:S(2)}) collective-permute-start(bf16[48,24,128]{2,1,0:T(8,128)(2,1)} %collective-permute-done.4.refs_4_), channel_id=1, source_target_pairs={{0,7},{1,0},{2,1},{3,2},{4,3},{5,4},{6,5},{7,6},{8,15},{9,8},{10,9... | collective-permute-start | bytes 884744 | tf_op jit(solution)/shard_map/ppermute | solution.py:168
  52.3 0.5 collective-permute-start.5
  52.8 0.1 pad_maximum_fusion
  52.9 0.4 fusion.3
  53.3 0.2 sub.30
  53.5 5.9 %collective-permute-done.6.refs_6_ = bf16[48,24,128]{2,1,0:T(8,128)(2,1)S(1)} collective-permute-done((bf16[48,24,128]{2,1,0:T(8,128)(2,1)}, bf16[48,24,128]{2,1,0:T(8,128)(2,1)S(1)}, u32[]{:S(2)}, u32[]{:S(2)}) %collective-permute-start.6) | collective-permute-done | bytes 294944 | tf_op jit(solution)/shard_map/ppermute | solution.py:168
  59.5 2.9 %collective-permute-start.8 = (bf16[24,24,128]{2,1,0:T(8,128)(2,1)S(1)}, bf16[24,24,128]{2,1,0:T(8,128)(2,1)S(1)}, u32[]{:S(2)}, u32[]{:S(2)}) collective-permute-start(bf16[24,24,128]{2,1,0:T(8,128)(2,1)S(1)} %slice.56), channel_id=1, source_target_pairs={{0,7},{1,0},{2,1},{3,2},{4,3},{5,4},{6,5},{7,6},{8,15},{9,8},{10,9... | collective-permute-start | bytes 442376 | tf_op jit(solution)/shard_map/ppermute | solution.py:168
  62.4 0.1 collective-permute-start.7
  62.5 0.6 fusion.10.dest_ref
  63.1 1.9 %collective-permute-done.8 = bf16[24,24,128]{2,1,0:T(8,128)(2,1)S(1)} collective-permute-done((bf16[24,24,128]{2,1,0:T(8,128)(2,1)S(1)}, bf16[24,24,128]{2,1,0:T(8,128)(2,1)S(1)}, u32[]{:S(2)}, u32[]{:S(2)}) %collective-permute-start.8) | collective-permute-done | bytes 147488 | tf_op jit(solution)/shard_map/ppermute | solution.py:168
  65.1 3.8 %collective-permute-done.7 = bf16[24,24,128]{2,1,0:T(8,128)(2,1)S(1)} collective-permute-done((bf16[24,24,128]{2,1,0:T(8,128)(2,1)S(1)}, bf16[24,24,128]{2,1,0:T(8,128)(2,1)S(1)}, u32[]{:S(2)}, u32[]{:S(2)}) %collective-permute-start.7) | collective-permute-done | bytes 147488 | tf_op jit(solution)/shard_map/ppermute | solution.py:168
  68.8 0.7 pad_maximum_fusion.3.refs_7_
  69.6 19.1 %shard_map.47 = f32[384,1104]{1,0:T(8,128)} custom-call(s32[2]{0:T(128)} %pad_add_fusion.1.meta_ref, s32[1536]{0:T(1024)} %reshape.33.lcol_ref, s32[960]{0:T(1024)} %fusion.10.dest_ref, bf16[64,3,24,128]{3,2,1,0:T(8,128)(2,1)} %bitcast.21, bf16[48,24,128]{2,1,0:T(8,128)(2,1)} %get-tuple-element.8.refs_0_, bf16[48,24,128]{2,1,0:T(8,128)(2,1)} %copy-done.5, ...), custom_call_target="tpu_custom_call" | custom-call | flops 6000000000 | bytes 8000000 | tf_op jit(solution)/shard_map/pallas_call | solution.py:152
  88.7 1.2 %fusion.13 = (f32[44,1104]{1,0:T(8,128)S(1)}, f32[44,1104]{1,0:T(8,128)S(1)}) fusion(f32[384,1104]{1,0:T(8,128)} %shard_map.47), kind=kLoop, calls=%fused_computation.37 | loop fusion | bytes 777216 | tf_op jit(solution)/shard_map/slice | solution.py:202
  89.9 0.5 collective-permute-start.11
  90.4 0.9 slice.59
  91.4 1.7 %collective-permute-start.9 = (f32[48,1104]{1,0:T(8,128)S(1)}, f32[48,1104]{1,0:T(8,128)S(1)}, u32[]{:S(2)}, u32[]{:S(2)}) collective-permute-start(f32[48,1104]{1,0:T(8,128)S(1)} %slice.59), channel_id=1, source_target_pairs={{0,8},{8,16},{16,24},{24,0},{1,9},{9,17},{17,25},{25,1},{2,10},{10... | collective-permute-start | bytes 635912 | tf_op jit(solution)/shard_map/ppermute | solution.py:168
  93.0 2.9 %collective-permute-done.11 = f32[44,1104]{1,0:T(8,128)S(1)} collective-permute-done((f32[44,1104]{1,0:T(8,128)S(1)}, f32[44,1104]{1,0:T(8,128)S(1)}, u32[]{:S(2)}, u32[]{:S(2)}) %collective-permute-start.11) | collective-permute-done | bytes 194336 | tf_op jit(solution)/shard_map/ppermute | solution.py:168
  95.9 1.0 slice_add_fusion.1
  96.9 0.5 collective-permute-done.9
  97.5 1.5 %collective-permute-start.12 = (f32[92,1104]{1,0:T(8,128)S(1)}, f32[92,1104]{1,0:T(8,128)S(1)}, u32[]{:S(2)}, u32[]{:S(2)}) collective-permute-start(f32[92,1104]{1,0:T(8,128)S(1)} %pad_maximum_fusion.2), channel_id=1, source_target_pairs={{0,24},{8,0},{16,8},{24,16},{1,25},{9,1},{17,9},{25,17},{2,26},{10... | collective-permute-start | bytes 1218824 | tf_op jit(solution)/shard_map/ppermute | solution.py:168
  99.0 0.7 collective-permute-start.10
  99.7 6.4 %collective-permute-done.12 = f32[92,1104]{1,0:T(8,128)S(1)} collective-permute-done((f32[92,1104]{1,0:T(8,128)S(1)}, f32[92,1104]{1,0:T(8,128)S(1)}, u32[]{:S(2)}, u32[]{:S(2)}) %collective-permute-start.12) | collective-permute-done | bytes 406304 | tf_op jit(solution)/shard_map/ppermute | solution.py:168
  106.1 2.5 %collective-permute-done.10 = f32[92,1104]{1,0:T(8,128)S(1)} collective-permute-done((f32[92,1104]{1,0:T(8,128)S(1)}, f32[92,1104]{1,0:T(8,128)S(1)}, u32[]{:S(2)}, u32[]{:S(2)}) %collective-permute-start.10) | collective-permute-done | bytes 406304 | tf_op jit(solution)/shard_map/ppermute | solution.py:168
  108.7 2.0 %collective-permute-start.13 = (bf16[92,1104]{1,0:T(8,128)(2,1)S(1)}, bf16[92,1104]{1,0:T(8,128)(2,1)S(1)}, u32[]{:S(2)}, u32[]{:S(2)}) collective-permute-start(bf16[92,1104]{1,0:T(8,128)(2,1)S(1)} %fusion.1), channel_id=1, source_target_pairs={{0,0},{1,9},{2,18},{3,27},{4,4},{5,13},{6,22},{7,31},{8,1},{9,8},{... | collective-permute-start | bytes 609416 | tf_op jit(solution)/shard_map/ppermute | solution.py:207
  110.7 7.6 %collective-permute-done.13 = bf16[92,1104]{1,0:T(8,128)(2,1)S(1)} collective-permute-done((bf16[92,1104]{1,0:T(8,128)(2,1)S(1)}, bf16[92,1104]{1,0:T(8,128)(2,1)S(1)}, u32[]{:S(2)}, u32[]{:S(2)}) %collective-permute-start.13) | collective-permute-done | bytes 203168 | tf_op jit(solution)/shard_map/ppermute | solution.py:207
  118.2 0.7 copy.19
  (27 shorter events, 0.3 us)
Async XLA Ops:
  8.6 18.6 %all-to-all-start = ((bf16[8,3,24,128]{3,2,1,0:T(8,128)(2,1)}), bf16[8,3,24,128]{3,2,1,0:T(8,128)(2,1)S(1)}, u32[]{:S(2)}, u32[]{:S(2)}) async-start(bf16[8,3,24,128]{3,2,1,0:T(8,128)(2,1)} %get-tuple-element.7), calls=%async_computation | async-start | bytes 294912 | tf_op jit(solution)/shard_map/all_to_all | solution.py:185
  17.1 24.1 %collective-permute-start.2 = (bf16[48,24,128]{2,1,0:T(8,128)(2,1)}, bf16[48,24,128]{2,1,0:T(8,128)(2,1)S(1)}, u32[]{:S(2)}, u32[]{:S(2)}) collective-permute-start(bf16[48,24,128]{2,1,0:T(8,128)(2,1)} %get-tuple-element.8.refs_0_), channel_id=1, source_target_pairs={{0,7},{1,0},{2,1},{3,2},{4,3},{5,4},{6,5},{7,6},{8,15},{9,8},{10,9... | collective-permute-start | bytes 884744 | tf_op jit(solution)/shard_map/ppermute | solution.py:168
  20.3 21.1 %collective-permute-start.1 = (bf16[48,24,128]{2,1,0:T(8,128)(2,1)}, bf16[48,24,128]{2,1,0:T(8,128)(2,1)S(1)}, u32[]{:S(2)}, u32[]{:S(2)}) collective-permute-start(bf16[48,24,128]{2,1,0:T(8,128)(2,1)} %get-tuple-element.8.refs_0_), channel_id=1, source_target_pairs={{0,1},{1,2},{2,3},{3,4},{4,5},{5,6},{6,7},{7,0},{8,9},{9,10},{10,1... | collective-permute-start | bytes 884744 | tf_op jit(solution)/shard_map/ppermute | solution.py:168
  41.2 11.6 %collective-permute-start = (bf16[4,8,3,24,128]{4,3,2,1,0:T(8,128)(2,1)S(1)}, bf16[4,8,3,24,128]{4,3,2,1,0:T(8,128)(2,1)S(1)}, u32[]{:S(2)}, u32[]{:S(2)}) collective-permute-start(bf16[4,8,3,24,128]{4,3,2,1,0:T(8,128)(2,1)S(1)} %bitcast.18), channel_id=1, source_target_pairs={{0,32},{32,0},{64,96},{96,64},{128,160},{160,128},{192,224},{224,1... | collective-permute-start | bytes 1769480 | tf_op jit(solution)/shard_map/ppermute | solution.py:188
  41.2 28.4 %copy-start.4 = (bf16[48,24,128]{2,1,0:T(8,128)(2,1)}, bf16[48,24,128]{2,1,0:T(8,128)(2,1)S(1)}, u32[]{:S(2)}) copy-start(bf16[48,24,128]{2,1,0:T(8,128)(2,1)S(1)} %collective-permute-done.2.refs_2_) | copy-start | bytes 884740
  41.2 9.5 %collective-permute-start.4 = (bf16[48,24,128]{2,1,0:T(8,128)(2,1)S(1)}, bf16[48,24,128]{2,1,0:T(8,128)(2,1)}, u32[]{:S(2)}, u32[]{:S(2)}) collective-permute-start(bf16[48,24,128]{2,1,0:T(8,128)(2,1)S(1)} %collective-permute-done.2.refs_2_), channel_id=1, source_target_pairs={{0,7},{1,0},{2,1},{3,2},{4,3},{5,4},{6,5},{7,6},{8,15},{9,8},{10,9... | collective-permute-start | bytes 884744 | tf_op jit(solution)/shard_map/ppermute | solution.py:168
  41.5 28.1 %copy-start.5 = (bf16[48,24,128]{2,1,0:T(8,128)(2,1)}, bf16[48,24,128]{2,1,0:T(8,128)(2,1)S(1)}, u32[]{:S(2)}) copy-start(bf16[48,24,128]{2,1,0:T(8,128)(2,1)S(1)} %collective-permute-done.1.refs_1_) | copy-start | bytes 884740
  41.5 10.8 %collective-permute-start.3 = (bf16[48,24,128]{2,1,0:T(8,128)(2,1)S(1)}, bf16[48,24,128]{2,1,0:T(8,128)(2,1)}, u32[]{:S(2)}, u32[]{:S(2)}) collective-permute-start(bf16[48,24,128]{2,1,0:T(8,128)(2,1)S(1)} %collective-permute-done.1.refs_1_), channel_id=1, source_target_pairs={{0,1},{1,2},{2,3},{3,4},{4,5},{5,6},{6,7},{7,0},{8,9},{9,10},{10,1... | collective-permute-start | bytes 884744 | tf_op jit(solution)/shard_map/ppermute | solution.py:168
  50.8 8.7 %collective-permute-start.6 = (bf16[48,24,128]{2,1,0:T(8,128)(2,1)}, bf16[48,24,128]{2,1,0:T(8,128)(2,1)S(1)}, u32[]{:S(2)}, u32[]{:S(2)}) collective-permute-start(bf16[48,24,128]{2,1,0:T(8,128)(2,1)} %collective-permute-done.4.refs_4_), channel_id=1, source_target_pairs={{0,7},{1,0},{2,1},{3,2},{4,3},{5,4},{6,5},{7,6},{8,15},{9,8},{10,9... | collective-permute-start | bytes 884744 | tf_op jit(solution)/shard_map/ppermute | solution.py:168
  52.3 10.1 %collective-permute-start.5 = (bf16[48,24,128]{2,1,0:T(8,128)(2,1)}, bf16[48,24,128]{2,1,0:T(8,128)(2,1)S(1)}, u32[]{:S(2)}, u32[]{:S(2)}) collective-permute-start(bf16[48,24,128]{2,1,0:T(8,128)(2,1)} %collective-permute-done.3.refs_3_), channel_id=1, source_target_pairs={{0,1},{1,2},{2,3},{3,4},{4,5},{5,6},{6,7},{7,0},{8,9},{9,10},{10,1... | collective-permute-start | bytes 884744 | tf_op jit(solution)/shard_map/ppermute | solution.py:168
  52.9 16.7 %copy-start.1 = (bf16[8,8,3,24,128]{4,3,2,1,0:T(8,128)(2,1)}, bf16[8,8,3,24,128]{4,3,2,1,0:T(8,128)(2,1)S(1)}, u32[]{:S(2)}) copy-start(bf16[8,8,3,24,128]{4,3,2,1,0:T(8,128)(2,1)S(1)} %pad_maximum_fusion) | copy-start | bytes 3538948
  59.5 10.1 %copy-start.2 = (bf16[48,24,128]{2,1,0:T(8,128)(2,1)}, bf16[48,24,128]{2,1,0:T(8,128)(2,1)S(1)}, u32[]{:S(2)}) copy-start(bf16[48,24,128]{2,1,0:T(8,128)(2,1)S(1)} %collective-permute-done.6.refs_6_) | copy-start | bytes 884740
  59.5 5.6 %collective-permute-start.8 = (bf16[24,24,128]{2,1,0:T(8,128)(2,1)S(1)}, bf16[24,24,128]{2,1,0:T(8,128)(2,1)S(1)}, u32[]{:S(2)}, u32[]{:S(2)}) collective-permute-start(bf16[24,24,128]{2,1,0:T(8,128)(2,1)S(1)} %slice.56), channel_id=1, source_target_pairs={{0,7},{1,0},{2,1},{3,2},{4,3},{5,4},{6,5},{7,6},{8,15},{9,8},{10,9... | collective-permute-start | bytes 442376 | tf_op jit(solution)/shard_map/ppermute | solution.py:168
  62.4 7.2 %copy-start.3 = (bf16[48,24,128]{2,1,0:T(8,128)(2,1)}, bf16[48,24,128]{2,1,0:T(8,128)(2,1)S(1)}, u32[]{:S(2)}) copy-start(bf16[48,24,128]{2,1,0:T(8,128)(2,1)S(1)} %collective-permute-done.5.refs_5_) | copy-start | bytes 884740
  62.4 6.4 %collective-permute-start.7 = (bf16[24,24,128]{2,1,0:T(8,128)(2,1)S(1)}, bf16[24,24,128]{2,1,0:T(8,128)(2,1)S(1)}, u32[]{:S(2)}, u32[]{:S(2)}) collective-permute-start(bf16[24,24,128]{2,1,0:T(8,128)(2,1)S(1)} %slice.55), channel_id=1, source_target_pairs={{0,1},{1,2},{2,3},{3,4},{4,5},{5,6},{6,7},{7,0},{8,9},{9,10},{10,1... | collective-permute-start | bytes 442376 | tf_op jit(solution)/shard_map/ppermute | solution.py:168
  88.7 8.7 %copy-start = (f32[384,1104]{1,0:T(8,128)S(1)}, f32[384,1104]{1,0:T(8,128)}, u32[]{:S(2)}) copy-start(f32[384,1104]{1,0:T(8,128)} %shard_map.47) | copy-start | bytes 5087236
  89.9 6.0 %collective-permute-start.11 = (f32[44,1104]{1,0:T(8,128)S(1)}, f32[44,1104]{1,0:T(8,128)S(1)}, u32[]{:S(2)}, u32[]{:S(2)}) collective-permute-start(f32[44,1104]{1,0:T(8,128)S(1)} %get-tuple-element.12), channel_id=1, source_target_pairs={{0,24},{8,0},{16,8},{24,16},{1,25},{9,1},{17,9},{25,17},{2,26},{10... | collective-permute-start | bytes 582920 | tf_op jit(solution)/shard_map/ppermute | solution.py:168
  91.4 6.0 %collective-permute-start.9 = (f32[48,1104]{1,0:T(8,128)S(1)}, f32[48,1104]{1,0:T(8,128)S(1)}, u32[]{:S(2)}, u32[]{:S(2)}) collective-permute-start(f32[48,1104]{1,0:T(8,128)S(1)} %slice.59), channel_id=1, source_target_pairs={{0,8},{8,16},{16,24},{24,0},{1,9},{9,17},{17,25},{25,1},{2,10},{10... | collective-permute-start | bytes 635912 | tf_op jit(solution)/shard_map/ppermute | solution.py:168
  97.5 8.6 %collective-permute-start.12 = (f32[92,1104]{1,0:T(8,128)S(1)}, f32[92,1104]{1,0:T(8,128)S(1)}, u32[]{:S(2)}, u32[]{:S(2)}) collective-permute-start(f32[92,1104]{1,0:T(8,128)S(1)} %pad_maximum_fusion.2), channel_id=1, source_target_pairs={{0,24},{8,0},{16,8},{24,16},{1,25},{9,1},{17,9},{25,17},{2,26},{10... | collective-permute-start | bytes 1218824 | tf_op jit(solution)/shard_map/ppermute | solution.py:168
  99.0 9.6 %collective-permute-start.10 = (f32[92,1104]{1,0:T(8,128)S(1)}, f32[92,1104]{1,0:T(8,128)S(1)}, u32[]{:S(2)}, u32[]{:S(2)}) collective-permute-start(f32[92,1104]{1,0:T(8,128)S(1)} %pad_maximum_fusion.1), channel_id=1, source_target_pairs={{0,8},{8,16},{16,24},{24,0},{1,9},{9,17},{17,25},{25,1},{2,10},{10... | collective-permute-start | bytes 1218824 | tf_op jit(solution)/shard_map/ppermute | solution.py:168
  108.7 9.6 %collective-permute-start.13 = (bf16[92,1104]{1,0:T(8,128)(2,1)S(1)}, bf16[92,1104]{1,0:T(8,128)(2,1)S(1)}, u32[]{:S(2)}, u32[]{:S(2)}) collective-permute-start(bf16[92,1104]{1,0:T(8,128)(2,1)S(1)} %fusion.1), channel_id=1, source_target_pairs={{0,0},{1,9},{2,18},{3,27},{4,4},{5,13},{6,22},{7,31},{8,1},{9,8},{... | collective-permute-start | bytes 609416 | tf_op jit(solution)/shard_map/ppermute | solution.py:207

commit v3 on v0

v3 whole, which is shorter than its diff:
```python
import jax
import jax.numpy as jnp
from jax import lax
from jax.experimental import pallas as pl
from jax.experimental.pallas import tpu as pltpu
from jax.sharding import PartitionSpec as P


BLK = 23
LANES = 128
APAD = 24
KROW = 32
SLOTS = 4
USLOTS = 3
TILES = 4
PANEL = 40
HERE = 5
GROUP = 8
CHUNK = 96
WIDE = 4 * CHUNK
ROWS = 48
SPANS = ((0, 92), (96, 144), (144, 188), (192, 240), (240, 284), (288, 336), (336, 380))
STARTS = (0, 8, 16, 24, 28, 32, 40, 48, 56, 60)
OFFSETS = (0, 7, 1, 6, 2, 5, 3, 4)


def place(z, windows, lane, src, dst):
    first, last = src // LANES, (src + BLK - 1) // LANES
    shift = (dst - src) % LANES
    split = dst + min(BLK, LANES * (first + 1) - src)
    rolled = pltpu.roll(windows(first), shift, 1) if shift else windows(first)
    z = jnp.where((lane >= dst) & (lane < split), rolled, z)
    if last != first:
        rolled = pltpu.roll(windows(last), shift, 1) if shift else windows(last)
        z = jnp.where((lane >= split) & (lane < dst + BLK), rolled, z)
    return z


def pack_left_kernel(left_ref, out_ref, flat_ref, tmp_ref):
    for i in range(ROWS):
        block = left_ref[i].astype(jnp.float32)
        for j in range(5):
            width = min(LANES, BLK * BLK - j * LANES)
            flat_ref[j, i * SLOTS : (i + 1) * SLOTS, 0:width] = block[:, j * LANES : j * LANES + width]
    lane = lax.broadcasted_iota(jnp.int32, (ROWS, LANES), 1)
    for a in range(BLK):
        z = jnp.zeros((ROWS, LANES), jnp.float32)
        for s in range(SLOTS):
            z = place(
                z,
                lambda j, s=s: flat_ref[j, pl.ds(s, ROWS, stride=SLOTS), :],
                lane,
                BLK * a,
                KROW * s,
            )
        tmp_ref[pl.ds(a, ROWS, stride=APAD), :] = z
    tmp_ref[pl.ds(BLK, ROWS, stride=APAD), :] = jnp.zeros((ROWS, LANES), jnp.float32)
    for i in range(ROWS):
        out_ref[i] = tmp_ref[i * APAD : (i + 1) * APAD, :].astype(jnp.bfloat16)


def pack_left(left_values):
    vmem = pl.BlockSpec(memory_space=pltpu.VMEM)
    return pl.pallas_call(
        pack_left_kernel,
        out_shape=jax.ShapeDtypeStruct((ROWS, APAD, LANES), jnp.bfloat16),
        in_specs=[vmem],
        out_specs=vmem,
        scratch_shapes=[
            pltpu.VMEM((5, ROWS * SLOTS, LANES), jnp.float32),
            pltpu.VMEM((ROWS * APAD, LANES), jnp.float32),
        ],
        compiler_params=pltpu.CompilerParams(vmem_limit_bytes=8 * 1024 * 1024),
    )(left_values[:, 0])


def pack_right_kernel(meta_ref, right_ref, right_cols_ref, left_cols_ref, *refs):
    outs, (flat_ref, code_ref, tmp_ref) = refs[:TILES], refs[TILES:]
    for k in range(HERE):
        for u in range(USLOTS):
            n = (k * USLOTS + u) * 8
            flat_ref[n : n + TILES, 0 : BLK * BLK] = right_ref[k, u].astype(jnp.float32)
    code_ref[...] = jnp.zeros((8, LANES), jnp.float32)
    code_ref[0:SLOTS, 0:ROWS] = left_cols_ref[...].astype(jnp.float32)
    codes = code_ref[...]
    lane = lax.broadcasted_iota(jnp.int32, (8, LANES), 1)
    for u in range(USLOTS):
        for a in range(BLK):
            z = jnp.zeros((8, LANES), jnp.float32)
            for k in range(HERE):
                n = (k * USLOTS + u) * 8
                z = place(
                    z,
                    lambda j, n=n: flat_ref[n : n + 8, j * LANES : (j + 1) * LANES],
                    lane,
                    BLK * a,
                    BLK * k,
                )
            tmp_ref[u, pl.ds(a, 8, stride=APAD), :] = z
        code_ref[...] = jnp.zeros((8, LANES), jnp.float32)
        code_ref[0:TILES, 0:HERE] = right_cols_ref[u].astype(jnp.float32)
        z = code_ref[...]
        if u < 2:
            for h in range(2):
                line = codes[2 * u + h : 2 * u + h + 1, :]
                z = z + pltpu.roll(jnp.broadcast_to(line, (8, LANES)), 16 + ROWS * h, 1)
        tmp_ref[u, pl.ds(BLK, 8, stride=APAD), :] = z
    for t in range(TILES):
        tile = (meta_ref[0] + t) % TILES
        for u in range(USLOTS):
            rows = tmp_ref[u, pl.ds(pl.multiple_of(tile * APAD, 8), APAD), :]
            outs[t][u] = rows.astype(jnp.bfloat16)


def pack_right(meta, right_values, right_columns, left_columns):
    vmem = pl.BlockSpec(memory_space=pltpu.VMEM)
    return pl.pallas_call(
        pack_right_kernel,
        out_shape=(jax.ShapeDtypeStruct((USLOTS, APAD, LANES), jnp.bfloat16),) * TILES,
        in_specs=[pl.BlockSpec(memory_space=pltpu.SMEM)] + [vmem] * 3,
        out_specs=(vmem,) * TILES,
        scratch_shapes=[
            pltpu.VMEM((HERE * USLOTS * 8, 5 * LANES), jnp.float32),
            pltpu.VMEM((8, LANES), jnp.float32),
            pltpu.VMEM((USLOTS, 8 * APAD, LANES), jnp.float32),
        ],
        compiler_params=pltpu.CompilerParams(vmem_limit_bytes=8 * 1024 * 1024),
    )(
        meta,
        jnp.transpose(right_values[0], (0, 2, 1, 3)),
        jnp.transpose(right_columns[0], (2, 1, 0)),
        jnp.transpose(left_columns[:, 0], (1, 0)),
    )


def fill_kernel(meta_ref, *refs):
    rights, (wide_ref, table_ref) = refs[:-6], refs[-6:-4]
    right_ref, mixed_ref, codes_ref, sem = refs[-4:]
    depth, core, side, col = (meta_ref[m] for m in range(4))
    for source, piece in enumerate(rights):
        count = 1 if len(piece.shape) == 3 else piece.shape[0]
        start = STARTS[source]
        block = piece[...].reshape(count, USLOTS, APAD, LANES)
        right_ref[start : start + count] = block
        codes = block[:, :, BLK, :].astype(jnp.float32).astype(jnp.int32)
        local = codes - 16 * (depth // 4)
        chunk = lax.bitwise_xor(lax.shift_right_arithmetic(local, 2), depth % 4)
        at = CHUNK * ((chunk - col) & 3) + BLK * (local & 3)
        at = jnp.where((local >= 0) & (local < 16), at, 4 * LANES)
        tiny = lax.broadcasted_iota(jnp.int32, codes.shape, 2) < HERE
        mixed_ref[start * USLOTS : (start + count) * USLOTS] = jnp.where(tiny, at, codes).reshape(-1, LANES)
    copy = pltpu.make_async_copy(mixed_ref, codes_ref, sem)
    copy.start()
    lane = lax.broadcasted_iota(jnp.int32, (8, LANES), 1)
    blank = jnp.zeros((8, LANES), jnp.float32)
    copy.wait()

    def fill(n, carry):
        j = (n // GROUP) % 4
        row = 2 * ((side + jnp.where(j == 1, 3, j - j // 2)) % 4) + lax.bitwise_xor(core, n // 32)
        place_in = n % GROUP
        panel = lax.bitwise_xor(depth // 4, place_in // 4) * 4 + ((depth - place_in) & 3)
        base = panel * PANEL + row * HERE
        blocks = [right_ref[n, u].astype(jnp.float32) for u in range(USLOTS)]
        for k in range(HERE):
            z = [[blank] * 3 for _ in range(3)]
            for u in range(USLOTS):
                at = codes_ref[n * USLOTS + u, k]
                rolled = pltpu.roll(blocks[u], (at + 4 * LANES - BLK * k) % LANES, 1)
                for q in range(3):
                    here = (lane + (q * LANES - at)).astype(jnp.uint32) < BLK
                    for v in range(3):
                        z[q][v] = jnp.where(here, rolled[8 * v : 8 * v + 8], z[q][v])
            for q in range(3):
                wide_ref[base + k, q] = jnp.concatenate(z[q] + [blank], axis=0).astype(jnp.bfloat16)
        return carry

    lax.fori_loop(0, 8 * GROUP, fill, 0, unroll=4)
    table_ref[...] = mixed_ref[0 : GROUP * USLOTS]


def fill(meta, rights):
    vmem = pl.BlockSpec(memory_space=pltpu.VMEM)
    lines = 8 * GROUP * USLOTS
    return pl.pallas_call(
        fill_kernel,
        out_shape=(
            jax.ShapeDtypeStruct((GROUP * PANEL, 3, KROW, LANES), jnp.bfloat16),
            jax.ShapeDtypeStruct((GROUP * USLOTS, LANES), jnp.int32),
        ),
        in_specs=[pl.BlockSpec(memory_space=pltpu.SMEM)] + [vmem] * len(rights),
        out_specs=(vmem, vmem),
        scratch_shapes=[
            pltpu.VMEM((8 * GROUP, USLOTS, APAD, LANES), jnp.bfloat16),
            pltpu.VMEM((lines, LANES), jnp.int32),
            pltpu.SMEM((lines, LANES), jnp.int32),
            pltpu.SemaphoreType.DMA,
        ],
        compiler_params=pltpu.CompilerParams(vmem_limit_bytes=16 * 1024 * 1024),
        cost_estimate=pl.CostEstimate(flops=3_000_000_000, bytes_accessed=8_000_000, transcendentals=0),
    )(meta, *rights)


def product_kernel(meta_ref, table_ref, wide_ref, *refs):
    lefts, outs, (far_ref, sum_ref, part_ref) = refs[:9], refs[9:16], refs[16:]
    depth = meta_ref[0]
    panels = [(depth + o) % GROUP for o in OFFSETS]
    lines = [(lax.bitwise_xor(p // 4, depth // 4) * 4 + ((depth - p) & 3)) * USLOTS for p in panels]
    half = ROWS // 2
    far_ref[:half] = lefts[7][...]
    far_ref[half:] = lefts[8][...]
    lefts = (*lefts[:7], far_ref)

    def step(g, carry):
        for m in range(8):
            i = g * 8 + m
            at = [
                p * PANEL + table_ref[line + s // 2, 16 + ROWS * (s % 2) + i]
                for p, line in zip(panels, lines)
                for s in range(SLOTS)
            ]
            weights = jnp.concatenate(
                [jnp.concatenate([wide_ref[n, q] for n in at], axis=0) for q in range(3)], axis=1
            )
            rows = jnp.concatenate([x[i] for x in lefts], axis=1)
            part_ref[m * BLK : m * BLK + APAD, :] = jnp.dot(rows, weights, preferred_element_type=jnp.float32)
        sum_ref[pl.ds(pl.multiple_of(g * 8 * BLK, 8), 8 * BLK), :] = part_ref[0 : 8 * BLK, :]
        return carry

    lax.fori_loop(0, ROWS // 8, step, 0)
    for q in range(3):
        turned = sum_ref[0:1152, q * LANES : (q + 1) * LANES].T[:, : ROWS * BLK]
        for ref, (first, last) in zip(outs, SPANS):
            low, high = max(first, q * LANES), min(last, (q + 1) * LANES)
            if low < high:
                ref[low - first : high - first, :] = turned[low - q * LANES : high - q * LANES]


def product(meta, table, wide, lefts):
    vmem = pl.BlockSpec(memory_space=pltpu.VMEM)
    smem = pl.BlockSpec(memory_space=pltpu.SMEM)
    return pl.pallas_call(
        product_kernel,
        out_shape=tuple(jax.ShapeDtypeStruct((b - a, ROWS * BLK), jnp.float32) for a, b in SPANS),
        in_specs=[smem, smem, vmem] + [vmem] * len(lefts),
        out_specs=(vmem,) * len(SPANS),
        scratch_shapes=[
            pltpu.VMEM((ROWS, APAD, LANES), jnp.bfloat16),
            pltpu.VMEM((1152, WIDE), jnp.float32),
            pltpu.VMEM((8 * APAD, WIDE), jnp.float32),
        ],
        compiler_params=pltpu.CompilerParams(vmem_limit_bytes=12 * 1024 * 1024),
        cost_estimate=pl.CostEstimate(flops=6_000_000_000, bytes_accessed=8_000_000, transcendentals=0),
    )(meta, table, wide, *lefts)


def shift(x, axis, by, n):
    return lax.ppermute(x, axis, [(i, (i + by) % n) for i in range(n)])


def body(left_values, left_columns, right_values, right_columns):
    c, d = lax.axis_index("col"), lax.axis_index("depth")
    meta = jnp.stack([d, lax.axis_index("row") % 2, lax.axis_index("row") // 2, c])
    tiles = pack_right(meta, right_values, right_columns, left_columns)
    left = pack_left(left_values)
    near = [tiles[0]] + [
        lax.ppermute(tiles[k], "depth", [(z, z // 4 * 4 + (z + k) % 4) for z in range(8)]) for k in (1, 2, 3)
    ]
    up1, down1 = shift(left, "depth", 1, 8), shift(left, "depth", -1, 8)
    half = jnp.stack(near, axis=0)
    other = shift(half, "depth", 4, 8)
    up1, down1, half, other = lax.optimization_barrier((up1, down1, half, other))
    right = jnp.concatenate([half, other], axis=0)
    f1, b1 = shift(right, "row", 2, 8), shift(right, "row", -2, 8)
    up2, down2 = shift(up1, "depth", 1, 8), shift(down1, "depth", -1, 8)
    up2, down2, f1, b1 = lax.optimization_barrier((up2, down2, f1, b1))
    swap = [(i, i ^ 1) for i in range(8)]
    f2, b2 = shift(f1[:4], "row", 2, 8), shift(b1[4:], "row", -2, 8)
    up3, down3 = shift(up2, "depth", 1, 8), shift(down2, "depth", -1, 8)
    others = [lax.ppermute(x, "row", swap) for x in (right, f1, b1)]
    up3, down3, f2, b2 = lax.optimization_barrier((up3, down3, f2, b2))
    others += [lax.ppermute(x, "row", swap) for x in (f2, b2)]
    edge = ROWS // 2
    up4, down4 = shift(up3[:edge], "depth", 1, 8), shift(down3[edge:], "depth", -1, 8)
    lefts = [left, up1, down1, up2, down2, up3, down3, up4, down4]
    wide, table = fill(meta, [right, f1, b1, f2, b2] + others)
    own, ahead_low, ahead_high, far_low, far_high, behind_low, behind_high = product(meta, table, wide, lefts)
    far_low = shift(far_low, "col", 1, 4)
    far_high = shift(far_high, "col", -1, 4)
    ahead_high = shift(ahead_high, "col", 1, 4)
    behind_low = shift(behind_low, "col", -1, 4)
    ahead_low = shift(ahead_low + far_low, "col", 1, 4)
    behind_high = shift(behind_high + far_high, "col", -1, 4)
    low = own[:48] + behind_low + ahead_low
    high = own[48:] + ahead_high + behind_high
    done = jnp.concatenate([low.astype(jnp.bfloat16), high.astype(jnp.bfloat16)], axis=0)
    home = [(y * 8 + z, (z % 4) * 8 + (z // 4) * 4 + (y ^ (z % 4))) for y in range(4) for z in range(8)]
    return lax.ppermute(done, ("col", "depth"), home).T


def solution(mesh):
    placed = (
        P("row", ("col", "depth"), None, None),
        P("row", ("col", "depth"), None),
        P(("col", "depth"), "row", None, None, None),
        P(("col", "depth"), "row", None, None),
    )
    return jax.shard_map(
        body, mesh=mesh, in_specs=placed, out_specs=P("row", ("col", "depth")), check_vma=False
    )
```

time: 359 us -> 103 us (0.29)
  blocking collectives: 176 us -> 0 us
  local copies, waits for them, and re-layouts: 129 us -> 3.96 us
  starting transfers between devices: 5.06 us -> 42 us
  matrix products: 36.2 us -> 0 us
  waiting for transfers between devices: 6.78 us -> 36.8 us
  Pallas kernels: 0 us -> 19.4 us
    unnamed x1 -> x0, blocking collectives: 163 us -> none
    convert_element_type x3 -> x0, local copies, waits for them, and re-layouts: 65.4 us -> none  [the longest x1 41.1 us: dense_right(): filled = jnp.einsum('qrtuc,qrtuab->qratcb', onehot, blocks, preferred_ele...]
    another operation x4 -> x0, local copies, waits for them, and re-layouts: 59.2 us -> none
    ppermute x0 -> x28, starting transfers between devices: none -> 42 us  [the longest x19 33.2 us: shift(): return lax.ppermute(x, axis, [(i, (i + by) % n) for i in range(n)])]
    ppermute x0 -> x28, waiting for transfers between devices: none -> 36.8 us  [the longest x19 25.3 us: shift(): return lax.ppermute(x, axis, [(i, (i + by) % n) for i in range(n)])]
    dot_general x3 -> x0, matrix products: 36.2 us -> none  [the longest x1 17.1 us: dense_right(): jnp.einsum('qrtuc,qrtuab->qratcb', onehot, blocks, preferred_element_type...]
    pallas_call x0 -> x4, Pallas kernels: none -> 19.4 us  [the longest x1 10.2 us: fill(): pl.pallas_call(fill_kernel, out_shape=(jax.ShapeDtypeStruct((GROUP * PANE...]
    all_gather x1 -> x0, blocking collectives: 13.6 us -> none  [in_one_piece(): whole = lax.all_gather(both, axis, axis=dim, tiled=True)]
  transfers between devices with their start and end apart: 2 -> 28, of which waited for: 1 -> 12; matrix products, arithmetic and copies ran while one was open for 0% -> 0% of each run, Pallas kernels for 0% -> 11%
where the time goes in v3:
time: 103 us
  starting transfers between devices  42 us (41%)
  waiting for transfers between devices  36.8 us (36%)
  Pallas kernels  19.4 us (19%)
  local copies, waits for them, and re-layouts  3.96 us (4%)
    ppermute x19, starting transfers between devices, shift(): return lax.ppermute(x, axis, [(i, (i + by) % n) for i in range(n)])  33.2 us
    ppermute x19, waiting for transfers between devices, shift(): return lax.ppermute(x, axis, [(i, (i + by) % n) for i in range(n)])  25.3 us
    pallas_call x1, Pallas kernels, fill(): pl.pallas_call(fill_kernel, out_shape=(jax.ShapeDtypeStruct((GROUP * PANE...  10.2 us
    ppermute x1, waiting for transfers between devices, body(): return lax.ppermute(done, ('col', 'depth'), home).T  9.05 us
    pallas_call x1, Pallas kernels, product(): pl.pallas_call(product_kernel, out_shape=tuple((jax.ShapeDtypeStruct((b -...  7.63 us
    ppermute x1, starting transfers between devices, body(): return lax.ppermute(done, ('col', 'depth'), home).T  4.28 us
    ppermute x3, starting transfers between devices, body(): lax.ppermute(tiles[k], 'depth', [(z, z // 4 * 4 + (z + k) % 4) for z in r...  3.9 us
    unnamed x10, local copies, waits for them, and re-layouts  3.9 us
  transfers between devices with their start and end apart: 28, of which 12 were waited for; matrix products, arithmetic and copies ran while one was open for 0% of the time, Pallas kernels for 11%

profile of v3, /device:TPU:16, one launch (start us, length us, event | category | flops | bytes accessed | tf_op | source)
XLA Modules:
  0.0 102.6 jit_solution(15575817643180708332)
XLA Ops:
  0.0 0.9 copy-done
  0.9 0.5 shard_map.46.refs_0_
  1.5 5.9 %collective-permute-start.1 = (bf16[48,24,128]{2,1,0:T(8,128)(2,1)S(1)}, bf16[48,24,128]{2,1,0:T(8,128)(2,1)S(1)}, u32[]{:S(2)}, u32[]{:S(2)}) collective-permute-start(bf16[48,24,128]{2,1,0:T(8,128)(2,1)S(1)} %shard_map.46.refs_0_), channel_id=1, source_target_pairs={{0,7},{1,0},{2,1},{3,2},{4,3},{5,4},{6,5},{7,6},{8,15},{9,8},{10,9... | collective-permute-start | bytes 884744 | tf_op jit(solution)/shard_map/ppermute | solution.py:258
  7.4 0.0 collective-permute-start
  7.4 0.1 pad_add_fusion.meta_ref
  7.5 0.9 copy-done.1
  8.4 0.7 copy-done.2
  9.0 0.7 copy-done.3
  9.7 1.0 %shard_map.47 = (bf16[3,24,128]{2,1,0:T(8,128)(2,1)S(1)}, bf16[3,24,128]{2,1,0:T(8,128)(2,1)S(1)}, bf16[3,24,128]{2,1,0:T(8,128)(2,1)S(1)}, bf16[3,24,128]{2,1,0:T(8,128)(2,1)S(1)}) custom-call(s32[4]{0:T(128)S(1)} %pad_add_fusion.meta_ref, bf16[5,3,4,529]{3,2,1,0:T(4,128)(2,1)S(1)} %bitcast.20, s32[3,4,5]{2,1,0:T(4,128)S(1)} %bitcast.22, s32[4,48]{1,0:T(4,128)S(1)} %bitcast.23), custom_call_target="tpu_custom_call" | custom-call | tf_op jit(solution)/shard_map/pallas_call | solution.py:117
  10.8 0.1 collective-permute-start.2
  10.9 2.6 %collective-permute-start.3 = (bf16[3,24,128]{2,1,0:T(8,128)(2,1)S(1)}, bf16[3,24,128]{2,1,0:T(8,128)(2,1)S(1)}, u32[]{:S(2)}, u32[]{:S(2)}) collective-permute-start(bf16[3,24,128]{2,1,0:T(8,128)(2,1)S(1)} %get-tuple-element.32), channel_id=1, source_target_pairs={{0,2},{1,3},{2,0},{3,1},{4,6},{5,7},{6,4},{7,5},{8,10},{9,11},{10,... | collective-permute-start | bytes 55304 | tf_op jit(solution)/shard_map/ppermute | solution.py:267
  13.4 1.3 %collective-permute-start.4 = (bf16[3,24,128]{2,1,0:T(8,128)(2,1)S(1)}, bf16[3,24,128]{2,1,0:T(8,128)(2,1)S(1)}, u32[]{:S(2)}, u32[]{:S(2)}) collective-permute-start(bf16[3,24,128]{2,1,0:T(8,128)(2,1)S(1)} %get-tuple-element.33), channel_id=1, source_target_pairs={{0,3},{1,0},{2,1},{3,2},{4,7},{5,4},{6,5},{7,6},{8,11},{9,8},{10,9... | collective-permute-start | bytes 55304 | tf_op jit(solution)/shard_map/ppermute | solution.py:267
  14.7 1.7 %collective-permute-done.2 = bf16[3,24,128]{2,1,0:T(8,128)(2,1)S(1)} collective-permute-done((bf16[3,24,128]{2,1,0:T(8,128)(2,1)S(1)}, bf16[3,24,128]{2,1,0:T(8,128)(2,1)S(1)}, u32[]{:S(2)}, u32[]{:S(2)}) %collective-permute-start.2) | collective-permute-done | bytes 18464 | tf_op jit(solution)/shard_map/ppermute | solution.py:267
  16.4 0.8 collective-permute-done.4
  17.2 4.6 %collective-permute-start.5 = (bf16[4,3,24,128]{3,2,1,0:T(8,128)(2,1)S(1)}, bf16[4,3,24,128]{3,2,1,0:T(8,128)(2,1)S(1)}, u32[]{:S(2)}, u32[]{:S(2)}) collective-permute-start(bf16[4,3,24,128]{3,2,1,0:T(8,128)(2,1)S(1)} %pad_maximum_fusion.1), channel_id=1, source_target_pairs={{0,4},{1,5},{2,6},{3,7},{4,0},{5,1},{6,2},{7,3},{8,12},{9,13},{10,... | collective-permute-start | bytes 221192 | tf_op jit(solution)/shard_map/ppermute | solution.py:258
  21.8 4.0 %collective-permute-done.5 = bf16[4,3,24,128]{3,2,1,0:T(8,128)(2,1)S(1)} collective-permute-done((bf16[4,3,24,128]{3,2,1,0:T(8,128)(2,1)S(1)}, bf16[4,3,24,128]{3,2,1,0:T(8,128)(2,1)S(1)}, u32[]{:S(2)}, u32[]{:S(2)}) %collective-permute-start.5) | collective-permute-done | bytes 73760 | tf_op jit(solution)/shard_map/ppermute | solution.py:258
  25.8 1.7 %collective-permute-start.6 = (bf16[48,24,128]{2,1,0:T(8,128)(2,1)S(1)}, bf16[48,24,128]{2,1,0:T(8,128)(2,1)S(1)}, u32[]{:S(2)}, u32[]{:S(2)}) collective-permute-start(bf16[48,24,128]{2,1,0:T(8,128)(2,1)S(1)} %collective-permute-done.refs_1_), channel_id=1, source_target_pairs={{0,1},{1,2},{2,3},{3,4},{4,5},{5,6},{6,7},{7,0},{8,9},{9,10},{10,1... | collective-permute-start | bytes 884744 | tf_op jit(solution)/shard_map/ppermute | solution.py:258
  27.5 2.9 %collective-permute-start.7 = (bf16[48,24,128]{2,1,0:T(8,128)(2,1)S(1)}, bf16[48,24,128]{2,1,0:T(8,128)(2,1)S(1)}, u32[]{:S(2)}, u32[]{:S(2)}) collective-permute-start(bf16[48,24,128]{2,1,0:T(8,128)(2,1)S(1)} %collective-permute-done.1.refs_2_), channel_id=1, source_target_pairs={{0,7},{1,0},{2,1},{3,2},{4,3},{5,4},{6,5},{7,6},{8,15},{9,8},{10,9... | collective-permute-start | bytes 884744 | tf_op jit(solution)/shard_map/ppermute | solution.py:258
  30.4 2.8 %collective-permute-start.9 = (bf16[8,3,24,128]{3,2,1,0:T(8,128)(2,1)S(1)}, bf16[8,3,24,128]{3,2,1,0:T(8,128)(2,1)S(1)}, u32[]{:S(2)}, u32[]{:S(2)}) collective-permute-start(bf16[8,3,24,128]{3,2,1,0:T(8,128)(2,1)S(1)} %constant_dynamic-update-slice_fusion.refs_0_), channel_id=1, source_target_pairs={{0,192},{32,224},{64,0},{96,32},{128,64},{160,96},{192,128},{224,1... | collective-permute-start | bytes 442376 | tf_op jit(solution)/shard_map/ppermute | solution.py:258
  33.2 2.7 %collective-permute-done.9.refs_2_ = bf16[8,3,24,128]{3,2,1,0:T(8,128)(2,1)S(1)} collective-permute-done((bf16[8,3,24,128]{3,2,1,0:T(8,128)(2,1)S(1)}, bf16[8,3,24,128]{3,2,1,0:T(8,128)(2,1)S(1)}, u32[]{:S(2)}, u32[]{:S(2)}) %collective-permute-start.9) | collective-permute-done | bytes 147488 | tf_op jit(solution)/shard_map/ppermute | solution.py:258
  35.9 3.7 %collective-permute-done.8.refs_1_ = bf16[8,3,24,128]{3,2,1,0:T(8,128)(2,1)S(1)} collective-permute-done((bf16[8,3,24,128]{3,2,1,0:T(8,128)(2,1)S(1)}, bf16[8,3,24,128]{3,2,1,0:T(8,128)(2,1)S(1)}, u32[]{:S(2)}, u32[]{:S(2)}) %collective-permute-start.8) | collective-permute-done | bytes 147488 | tf_op jit(solution)/shard_map/ppermute | solution.py:258
  39.6 3.2 %collective-permute-start.11 = (bf16[48,24,128]{2,1,0:T(8,128)(2,1)S(1)}, bf16[48,24,128]{2,1,0:T(8,128)(2,1)S(1)}, u32[]{:S(2)}, u32[]{:S(2)}) collective-permute-start(bf16[48,24,128]{2,1,0:T(8,128)(2,1)S(1)} %collective-permute-done.7.refs_4_), channel_id=1, source_target_pairs={{0,7},{1,0},{2,1},{3,2},{4,3},{5,4},{6,5},{7,6},{8,15},{9,8},{10,9... | collective-permute-start | bytes 884744 | tf_op jit(solution)/shard_map/ppermute | solution.py:258
  42.8 0.2 collective-permute-start.13
  43.0 2.0 %collective-permute-start.12 = (bf16[4,3,24,128]{3,2,1,0:T(8,128)(2,1)S(1)}, bf16[4,3,24,128]{3,2,1,0:T(8,128)(2,1)S(1)}, u32[]{:S(2)}, u32[]{:S(2)}) collective-permute-start(bf16[4,3,24,128]{3,2,1,0:T(8,128)(2,1)S(1)} %slice.18), channel_id=1, source_target_pairs={{0,64},{32,96},{64,128},{96,160},{128,192},{160,224},{192,0},{224,... | collective-permute-start | bytes 221192 | tf_op jit(solution)/shard_map/ppermute | solution.py:258
  45.0 2.2 %collective-permute-done.13.refs_4_ = bf16[4,3,24,128]{3,2,1,0:T(8,128)(2,1)S(1)} collective-permute-done((bf16[4,3,24,128]{3,2,1,0:T(8,128)(2,1)S(1)}, bf16[4,3,24,128]{3,2,1,0:T(8,128)(2,1)S(1)}, u32[]{:S(2)}, u32[]{:S(2)}) %collective-permute-start.13) | collective-permute-done | bytes 73760 | tf_op jit(solution)/shard_map/ppermute | solution.py:258
  47.3 0.0 collective-permute-start.15
  47.3 1.4 %collective-permute-done.12.refs_3_ = bf16[4,3,24,128]{3,2,1,0:T(8,128)(2,1)S(1)} collective-permute-done((bf16[4,3,24,128]{3,2,1,0:T(8,128)(2,1)S(1)}, bf16[4,3,24,128]{3,2,1,0:T(8,128)(2,1)S(1)}, u32[]{:S(2)}, u32[]{:S(2)}) %collective-permute-start.12) | collective-permute-done | bytes 73760 | tf_op jit(solution)/shard_map/ppermute | solution.py:258
  48.7 0.5 collective-permute-start.17
  49.2 0.1 collective-permute-start.18
  49.3 2.1 %collective-permute-start.20 = (bf16[24,24,128]{2,1,0:T(8,128)(2,1)S(1)}, bf16[24,24,128]{2,1,0:T(8,128)(2,1)S(1)}, u32[]{:S(2)}, u32[]{:S(2)}) collective-permute-start(bf16[24,24,128]{2,1,0:T(8,128)(2,1)S(1)} %slice.21), channel_id=1, source_target_pairs={{0,7},{1,0},{2,1},{3,2},{4,3},{5,4},{6,5},{7,6},{8,15},{9,8},{10,9... | collective-permute-start | bytes 442376 | tf_op jit(solution)/shard_map/ppermute | solution.py:258
  51.4 0.0 collective-permute-start.19
  51.4 10.2 %shard_map.48 = (bf16[320,3,32,128]{3,2,1,0:T(8,128)(2,1)S(1)}, s32[24,128]{1,0:T(8,128)S(1)}) custom-call(s32[4]{0:T(128)S(1)} %pad_add_fusion.meta_ref, bf16[8,3,24,128]{3,2,1,0:T(8,128)(2,1)S(1)} %constant_dynamic-update-slice_fusion.refs_0_, bf16[8,3,24,128]{3,2,1,0:T(8,128)(2,1)S(1)} %collective-permute-done.8.refs_1_, ...), custom_call_target="tpu_custom_call" | custom-call | flops 3000000000 | bytes 8000000 | tf_op jit(solution)/shard_map/pallas_call | solution.py:185
  61.6 7.6 %shard_map.49 = (f32[92,1104]{1,0:T(8,128)S(1)}, f32[48,1104]{1,0:T(8,128)S(1)}, f32[44,1104]{1,0:T(8,128)S(1)}, f32[48,1104]{1,0:T(8,128)S(1)}, f32[44,1104]{1,...) custom-call(s32[4]{0:T(128)S(1)} %pad_add_fusion.meta_ref, s32[24,128]{1,0:T(8,128)S(1)} %get-tuple-element.44.table_ref, ...), custom_call_target="tpu_custom_call" | custom-call | flops 6000000000 | bytes 8000000 | tf_op jit(solution)/shard_map/pallas_call | solution.py:242
  69.3 0.5 collective-permute-start.25
  69.8 1.6 %collective-permute-start.22 = (f32[48,1104]{1,0:T(8,128)S(1)}, f32[48,1104]{1,0:T(8,128)S(1)}, u32[]{:S(2)}, u32[]{:S(2)}) collective-permute-start(f32[48,1104]{1,0:T(8,128)S(1)} %get-tuple-element.51), channel_id=1, source_target_pairs={{0,8},{8,16},{16,24},{24,0},{1,9},{9,17},{17,25},{25,1},{2,10},{10... | collective-permute-start | bytes 635912 | tf_op jit(solution)/shard_map/ppermute | solution.py:258
  71.4 2.5 %collective-permute-start.24 = (f32[44,1104]{1,0:T(8,128)S(1)}, f32[44,1104]{1,0:T(8,128)S(1)}, u32[]{:S(2)}, u32[]{:S(2)}) collective-permute-start(f32[44,1104]{1,0:T(8,128)S(1)} %get-tuple-element.52), channel_id=1, source_target_pairs={{0,8},{8,16},{16,24},{24,0},{1,9},{9,17},{17,25},{25,1},{2,10},{10... | collective-permute-start | bytes 582920 | tf_op jit(solution)/shard_map/ppermute | solution.py:258
  73.9 2.6 %collective-permute-done.25 = f32[44,1104]{1,0:T(8,128)S(1)} collective-permute-done((f32[44,1104]{1,0:T(8,128)S(1)}, f32[44,1104]{1,0:T(8,128)S(1)}, u32[]{:S(2)}, u32[]{:S(2)}) %collective-permute-start.25) | collective-permute-done | bytes 194336 | tf_op jit(solution)/shard_map/ppermute | solution.py:258
  76.6 0.5 collective-permute-start.26
  77.1 1.0 collective-permute-start.21
  78.1 0.0 collective-permute-done.22
  78.1 1.7 %collective-permute-start.23 = (f32[48,1104]{1,0:T(8,128)S(1)}, f32[48,1104]{1,0:T(8,128)S(1)}, u32[]{:S(2)}, u32[]{:S(2)}) collective-permute-start(f32[48,1104]{1,0:T(8,128)S(1)} %add.25), channel_id=1, source_target_pairs={{0,8},{8,16},{16,24},{24,0},{1,9},{9,17},{17,25},{25,1},{2,10},{10... | collective-permute-start | bytes 635912 | tf_op jit(solution)/shard_map/ppermute | solution.py:258
  79.8 2.1 %collective-permute-done.24 = f32[44,1104]{1,0:T(8,128)S(1)} collective-permute-done((f32[44,1104]{1,0:T(8,128)S(1)}, f32[44,1104]{1,0:T(8,128)S(1)}, u32[]{:S(2)}, u32[]{:S(2)}) %collective-permute-start.24) | collective-permute-done | bytes 194336 | tf_op jit(solution)/shard_map/ppermute | solution.py:258
  81.9 3.5 %collective-permute-done.26 = f32[44,1104]{1,0:T(8,128)S(1)} collective-permute-done((f32[44,1104]{1,0:T(8,128)S(1)}, f32[44,1104]{1,0:T(8,128)S(1)}, u32[]{:S(2)}, u32[]{:S(2)}) %collective-permute-start.26) | collective-permute-done | bytes 194336 | tf_op jit(solution)/shard_map/ppermute | solution.py:258
  85.4 0.1 add_convert_fusion
  85.5 3.0 %collective-permute-done.21 = f32[48,1104]{1,0:T(8,128)S(1)} collective-permute-done((f32[48,1104]{1,0:T(8,128)S(1)}, f32[48,1104]{1,0:T(8,128)S(1)}, u32[]{:S(2)}, u32[]{:S(2)}) %collective-permute-start.21) | collective-permute-done | bytes 212000 | tf_op jit(solution)/shard_map/ppermute | solution.py:258
  88.5 4.3 %collective-permute-start.27 = (bf16[92,1104]{1,0:T(8,128)(2,1)S(1)}, bf16[92,1104]{1,0:T(8,128)(2,1)S(1)}, u32[]{:S(2)}, u32[]{:S(2)}) collective-permute-start(bf16[92,1104]{1,0:T(8,128)(2,1)S(1)} %pad_maximum_fusion), channel_id=1, source_target_pairs={{0,0},{1,9},{2,18},{3,27},{4,4},{5,13},{6,22},{7,31},{8,1},{9,8},{... | collective-permute-start | bytes 609416 | tf_op jit(solution)/shard_map/ppermute | solution.py:298
  92.8 9.1 %collective-permute-done.27 = bf16[92,1104]{1,0:T(8,128)(2,1)S(1)} collective-permute-done((bf16[92,1104]{1,0:T(8,128)(2,1)S(1)}, bf16[92,1104]{1,0:T(8,128)(2,1)S(1)}, u32[]{:S(2)}, u32[]{:S(2)}) %collective-permute-start.27) | collective-permute-done | bytes 203168 | tf_op jit(solution)/shard_map/ppermute | solution.py:298
  101.9 0.7 copy.7
  (34 shorter events, 0.3 us)
Async XLA Ops:
  0.0 0.9 copy-start
  1.5 24.3 %collective-permute-start.1 = (bf16[48,24,128]{2,1,0:T(8,128)(2,1)S(1)}, bf16[48,24,128]{2,1,0:T(8,128)(2,1)S(1)}, u32[]{:S(2)}, u32[]{:S(2)}) collective-permute-start(bf16[48,24,128]{2,1,0:T(8,128)(2,1)S(1)} %shard_map.46.refs_0_), channel_id=1, source_target_pairs={{0,7},{1,0},{2,1},{3,2},{4,3},{5,4},{6,5},{7,6},{8,15},{9,8},{10,9... | collective-permute-start | bytes 884744 | tf_op jit(solution)/shard_map/ppermute | solution.py:258
  7.4 18.4 %collective-permute-start = (bf16[48,24,128]{2,1,0:T(8,128)(2,1)S(1)}, bf16[48,24,128]{2,1,0:T(8,128)(2,1)S(1)}, u32[]{:S(2)}, u32[]{:S(2)}) collective-permute-start(bf16[48,24,128]{2,1,0:T(8,128)(2,1)S(1)} %shard_map.46.refs_0_), channel_id=1, source_target_pairs={{0,1},{1,2},{2,3},{3,4},{4,5},{5,6},{6,7},{7,0},{8,9},{9,10},{10,1... | collective-permute-start | bytes 884744 | tf_op jit(solution)/shard_map/ppermute | solution.py:258
  7.5 0.9 copy-start.1
  8.4 0.7 copy-start.2
  9.0 0.7 copy-start.3
  10.8 5.6 %collective-permute-start.2 = (bf16[3,24,128]{2,1,0:T(8,128)(2,1)S(1)}, bf16[3,24,128]{2,1,0:T(8,128)(2,1)S(1)}, u32[]{:S(2)}, u32[]{:S(2)}) collective-permute-start(bf16[3,24,128]{2,1,0:T(8,128)(2,1)S(1)} %get-tuple-element.31), channel_id=1, source_target_pairs={{0,1},{1,2},{2,3},{3,0},{4,5},{5,6},{6,7},{7,4},{8,9},{9,10},{10,1... | collective-permute-start | bytes 55304 | tf_op jit(solution)/shard_map/ppermute | solution.py:267
  10.9 5.6 %collective-permute-start.3 = (bf16[3,24,128]{2,1,0:T(8,128)(2,1)S(1)}, bf16[3,24,128]{2,1,0:T(8,128)(2,1)S(1)}, u32[]{:S(2)}, u32[]{:S(2)}) collective-permute-start(bf16[3,24,128]{2,1,0:T(8,128)(2,1)S(1)} %get-tuple-element.32), channel_id=1, source_target_pairs={{0,2},{1,3},{2,0},{3,1},{4,6},{5,7},{6,4},{7,5},{8,10},{9,11},{10,... | collective-permute-start | bytes 55304 | tf_op jit(solution)/shard_map/ppermute | solution.py:267
  13.4 3.8 %collective-permute-start.4 = (bf16[3,24,128]{2,1,0:T(8,128)(2,1)S(1)}, bf16[3,24,128]{2,1,0:T(8,128)(2,1)S(1)}, u32[]{:S(2)}, u32[]{:S(2)}) collective-permute-start(bf16[3,24,128]{2,1,0:T(8,128)(2,1)S(1)} %get-tuple-element.33), channel_id=1, source_target_pairs={{0,3},{1,0},{2,1},{3,2},{4,7},{5,4},{6,5},{7,6},{8,11},{9,8},{10,9... | collective-permute-start | bytes 55304 | tf_op jit(solution)/shard_map/ppermute | solution.py:267
  17.2 8.6 %collective-permute-start.5 = (bf16[4,3,24,128]{3,2,1,0:T(8,128)(2,1)S(1)}, bf16[4,3,24,128]{3,2,1,0:T(8,128)(2,1)S(1)}, u32[]{:S(2)}, u32[]{:S(2)}) collective-permute-start(bf16[4,3,24,128]{3,2,1,0:T(8,128)(2,1)S(1)} %pad_maximum_fusion.1), channel_id=1, source_target_pairs={{0,4},{1,5},{2,6},{3,7},{4,0},{5,1},{6,2},{7,3},{8,12},{9,13},{10,... | collective-permute-start | bytes 221192 | tf_op jit(solution)/shard_map/ppermute | solution.py:258
  25.8 13.8 %collective-permute-start.6 = (bf16[48,24,128]{2,1,0:T(8,128)(2,1)S(1)}, bf16[48,24,128]{2,1,0:T(8,128)(2,1)S(1)}, u32[]{:S(2)}, u32[]{:S(2)}) collective-permute-start(bf16[48,24,128]{2,1,0:T(8,128)(2,1)S(1)} %collective-permute-done.refs_1_), channel_id=1, source_target_pairs={{0,1},{1,2},{2,3},{3,4},{4,5},{5,6},{6,7},{7,0},{8,9},{9,10},{10,1... | collective-permute-start | bytes 884744 | tf_op jit(solution)/shard_map/ppermute | solution.py:258
  27.5 12.1 %collective-permute-start.7 = (bf16[48,24,128]{2,1,0:T(8,128)(2,1)S(1)}, bf16[48,24,128]{2,1,0:T(8,128)(2,1)S(1)}, u32[]{:S(2)}, u32[]{:S(2)}) collective-permute-start(bf16[48,24,128]{2,1,0:T(8,128)(2,1)S(1)} %collective-permute-done.1.refs_2_), channel_id=1, source_target_pairs={{0,7},{1,0},{2,1},{3,2},{4,3},{5,4},{6,5},{7,6},{8,15},{9,8},{10,9... | collective-permute-start | bytes 884744 | tf_op jit(solution)/shard_map/ppermute | solution.py:258
  30.4 5.5 %collective-permute-start.9 = (bf16[8,3,24,128]{3,2,1,0:T(8,128)(2,1)S(1)}, bf16[8,3,24,128]{3,2,1,0:T(8,128)(2,1)S(1)}, u32[]{:S(2)}, u32[]{:S(2)}) collective-permute-start(bf16[8,3,24,128]{3,2,1,0:T(8,128)(2,1)S(1)} %constant_dynamic-update-slice_fusion.refs_0_), channel_id=1, source_target_pairs={{0,192},{32,224},{64,0},{96,32},{128,64},{160,96},{192,128},{224,1... | collective-permute-start | bytes 442376 | tf_op jit(solution)/shard_map/ppermute | solution.py:258
  33.2 6.4 %collective-permute-start.8 = (bf16[8,3,24,128]{3,2,1,0:T(8,128)(2,1)S(1)}, bf16[8,3,24,128]{3,2,1,0:T(8,128)(2,1)S(1)}, u32[]{:S(2)}, u32[]{:S(2)}) collective-permute-start(bf16[8,3,24,128]{3,2,1,0:T(8,128)(2,1)S(1)} %constant_dynamic-update-slice_fusion.refs_0_), channel_id=1, source_target_pairs={{0,64},{32,96},{64,128},{96,160},{128,192},{160,224},{192,0},{224,... | collective-permute-start | bytes 442376 | tf_op jit(solution)/shard_map/ppermute | solution.py:258
  39.6 9.1 %collective-permute-start.10 = (bf16[48,24,128]{2,1,0:T(8,128)(2,1)S(1)}, bf16[48,24,128]{2,1,0:T(8,128)(2,1)S(1)}, u32[]{:S(2)}, u32[]{:S(2)}) collective-permute-start(bf16[48,24,128]{2,1,0:T(8,128)(2,1)S(1)} %collective-permute-done.6.refs_3_), channel_id=1, source_target_pairs={{0,1},{1,2},{2,3},{3,4},{4,5},{5,6},{6,7},{7,0},{8,9},{9,10},{10,1... | collective-permute-start | bytes 884744 | tf_op jit(solution)/shard_map/ppermute | solution.py:258
  39.6 9.1 %collective-permute-start.11 = (bf16[48,24,128]{2,1,0:T(8,128)(2,1)S(1)}, bf16[48,24,128]{2,1,0:T(8,128)(2,1)S(1)}, u32[]{:S(2)}, u32[]{:S(2)}) collective-permute-start(bf16[48,24,128]{2,1,0:T(8,128)(2,1)S(1)} %collective-permute-done.7.refs_4_), channel_id=1, source_target_pairs={{0,7},{1,0},{2,1},{3,2},{4,3},{5,4},{6,5},{7,6},{8,15},{9,8},{10,9... | collective-permute-start | bytes 884744 | tf_op jit(solution)/shard_map/ppermute | solution.py:258
  42.8 4.4 %collective-permute-start.13 = (bf16[4,3,24,128]{3,2,1,0:T(8,128)(2,1)S(1)}, bf16[4,3,24,128]{3,2,1,0:T(8,128)(2,1)S(1)}, u32[]{:S(2)}, u32[]{:S(2)}) collective-permute-start(bf16[4,3,24,128]{3,2,1,0:T(8,128)(2,1)S(1)} %slice.19), channel_id=1, source_target_pairs={{0,192},{32,224},{64,0},{96,32},{128,64},{160,96},{192,128},{224,1... | collective-permute-start | bytes 221192 | tf_op jit(solution)/shard_map/ppermute | solution.py:258
  43.0 5.6 %collective-permute-start.12 = (bf16[4,3,24,128]{3,2,1,0:T(8,128)(2,1)S(1)}, bf16[4,3,24,128]{3,2,1,0:T(8,128)(2,1)S(1)}, u32[]{:S(2)}, u32[]{:S(2)}) collective-permute-start(bf16[4,3,24,128]{3,2,1,0:T(8,128)(2,1)S(1)} %slice.18), channel_id=1, source_target_pairs={{0,64},{32,96},{64,128},{96,160},{128,192},{160,224},{192,0},{224,... | collective-permute-start | bytes 221192 | tf_op jit(solution)/shard_map/ppermute | solution.py:258
  45.0 4.3 %collective-permute-start.14 = (bf16[8,3,24,128]{3,2,1,0:T(8,128)(2,1)S(1)}, bf16[8,3,24,128]{3,2,1,0:T(8,128)(2,1)S(1)}, u32[]{:S(2)}, u32[]{:S(2)}) collective-permute-start(bf16[8,3,24,128]{3,2,1,0:T(8,128)(2,1)S(1)} %constant_dynamic-update-slice_fusion.refs_0_), channel_id=1, source_target_pairs={{0,32},{32,0},{64,96},{96,64},{128,160},{160,128},{192,224},{224,1... | collective-permute-start | bytes 442376 | tf_op jit(solution)/shard_map/ppermute | solution.py:280
  47.3 4.1 %collective-permute-start.15 = (bf16[8,3,24,128]{3,2,1,0:T(8,128)(2,1)S(1)}, bf16[8,3,24,128]{3,2,1,0:T(8,128)(2,1)S(1)}, u32[]{:S(2)}, u32[]{:S(2)}) collective-permute-start(bf16[8,3,24,128]{3,2,1,0:T(8,128)(2,1)S(1)} %collective-permute-done.8.refs_1_), channel_id=1, source_target_pairs={{0,32},{32,0},{64,96},{96,64},{128,160},{160,128},{192,224},{224,1... | collective-permute-start | bytes 442376 | tf_op jit(solution)/shard_map/ppermute | solution.py:280
  48.6 2.8 %collective-permute-start.16 = (bf16[8,3,24,128]{3,2,1,0:T(8,128)(2,1)S(1)}, bf16[8,3,24,128]{3,2,1,0:T(8,128)(2,1)S(1)}, u32[]{:S(2)}, u32[]{:S(2)}) collective-permute-start(bf16[8,3,24,128]{3,2,1,0:T(8,128)(2,1)S(1)} %collective-permute-done.9.refs_2_), channel_id=1, source_target_pairs={{0,32},{32,0},{64,96},{96,64},{128,160},{160,128},{192,224},{224,1... | collective-permute-start | bytes 442376 | tf_op jit(solution)/shard_map/ppermute | solution.py:280
  48.7 2.8 %collective-permute-start.17 = (bf16[4,3,24,128]{3,2,1,0:T(8,128)(2,1)S(1)}, bf16[4,3,24,128]{3,2,1,0:T(8,128)(2,1)S(1)}, u32[]{:S(2)}, u32[]{:S(2)}) collective-permute-start(bf16[4,3,24,128]{3,2,1,0:T(8,128)(2,1)S(1)} %collective-permute-done.12.refs_3_), channel_id=1, source_target_pairs={{0,32},{32,0},{64,96},{96,64},{128,160},{160,128},{192,224},{224,1... | collective-permute-start | bytes 221192 | tf_op jit(solution)/shard_map/ppermute | solution.py:282
  49.2 2.3 %collective-permute-start.18 = (bf16[4,3,24,128]{3,2,1,0:T(8,128)(2,1)S(1)}, bf16[4,3,24,128]{3,2,1,0:T(8,128)(2,1)S(1)}, u32[]{:S(2)}, u32[]{:S(2)}) collective-permute-start(bf16[4,3,24,128]{3,2,1,0:T(8,128)(2,1)S(1)} %collective-permute-done.13.refs_4_), channel_id=1, source_target_pairs={{0,32},{32,0},{64,96},{96,64},{128,160},{160,128},{192,224},{224,1... | collective-permute-start | bytes 221192 | tf_op jit(solution)/shard_map/ppermute | solution.py:282
  49.3 12.3 %collective-permute-start.20 = (bf16[24,24,128]{2,1,0:T(8,128)(2,1)S(1)}, bf16[24,24,128]{2,1,0:T(8,128)(2,1)S(1)}, u32[]{:S(2)}, u32[]{:S(2)}) collective-permute-start(bf16[24,24,128]{2,1,0:T(8,128)(2,1)S(1)} %slice.21), channel_id=1, source_target_pairs={{0,7},{1,0},{2,1},{3,2},{4,3},{5,4},{6,5},{7,6},{8,15},{9,8},{10,9... | collective-permute-start | bytes 442376 | tf_op jit(solution)/shard_map/ppermute | solution.py:258
  51.4 10.2 %collective-permute-start.19 = (bf16[24,24,128]{2,1,0:T(8,128)(2,1)S(1)}, bf16[24,24,128]{2,1,0:T(8,128)(2,1)S(1)}, u32[]{:S(2)}, u32[]{:S(2)}) collective-permute-start(bf16[24,24,128]{2,1,0:T(8,128)(2,1)S(1)} %slice.20), channel_id=1, source_target_pairs={{0,1},{1,2},{2,3},{3,4},{4,5},{5,6},{6,7},{7,0},{8,9},{9,10},{10,1... | collective-permute-start | bytes 442376 | tf_op jit(solution)/shard_map/ppermute | solution.py:258
  69.3 7.3 %collective-permute-start.25 = (f32[44,1104]{1,0:T(8,128)S(1)}, f32[44,1104]{1,0:T(8,128)S(1)}, u32[]{:S(2)}, u32[]{:S(2)}) collective-permute-start(f32[44,1104]{1,0:T(8,128)S(1)} %get-tuple-element.54), channel_id=1, source_target_pairs={{0,24},{8,0},{16,8},{24,16},{1,25},{9,1},{17,9},{25,17},{2,26},{10... | collective-permute-start | bytes 582920 | tf_op jit(solution)/shard_map/ppermute | solution.py:258
  69.8 8.3 %collective-permute-start.22 = (f32[48,1104]{1,0:T(8,128)S(1)}, f32[48,1104]{1,0:T(8,128)S(1)}, u32[]{:S(2)}, u32[]{:S(2)}) collective-permute-start(f32[48,1104]{1,0:T(8,128)S(1)} %get-tuple-element.51), channel_id=1, source_target_pairs={{0,8},{8,16},{16,24},{24,0},{1,9},{9,17},{17,25},{25,1},{2,10},{10... | collective-permute-start | bytes 635912 | tf_op jit(solution)/shard_map/ppermute | solution.py:258
  71.4 10.6 %collective-permute-start.24 = (f32[44,1104]{1,0:T(8,128)S(1)}, f32[44,1104]{1,0:T(8,128)S(1)}, u32[]{:S(2)}, u32[]{:S(2)}) collective-permute-start(f32[44,1104]{1,0:T(8,128)S(1)} %get-tuple-element.52), channel_id=1, source_target_pairs={{0,8},{8,16},{16,24},{24,0},{1,9},{9,17},{17,25},{25,1},{2,10},{10... | collective-permute-start | bytes 582920 | tf_op jit(solution)/shard_map/ppermute | solution.py:258
  76.6 8.9 %collective-permute-start.26 = (f32[44,1104]{1,0:T(8,128)S(1)}, f32[44,1104]{1,0:T(8,128)S(1)}, u32[]{:S(2)}, u32[]{:S(2)}) collective-permute-start(f32[44,1104]{1,0:T(8,128)S(1)} %add.28), channel_id=1, source_target_pairs={{0,24},{8,0},{16,8},{24,16},{1,25},{9,1},{17,9},{25,17},{2,26},{10... | collective-permute-start | bytes 582920 | tf_op jit(solution)/shard_map/ppermute | solution.py:258
  77.1 11.4 %collective-permute-start.21 = (f32[48,1104]{1,0:T(8,128)S(1)}, f32[48,1104]{1,0:T(8,128)S(1)}, u32[]{:S(2)}, u32[]{:S(2)}) collective-permute-start(f32[48,1104]{1,0:T(8,128)S(1)} %get-tuple-element.49), channel_id=1, source_target_pairs={{0,24},{8,0},{16,8},{24,16},{1,25},{9,1},{17,9},{25,17},{2,26},{10... | collective-permute-start | bytes 635912 | tf_op jit(solution)/shard_map/ppermute | solution.py:258
  78.1 10.3 %collective-permute-start.23 = (f32[48,1104]{1,0:T(8,128)S(1)}, f32[48,1104]{1,0:T(8,128)S(1)}, u32[]{:S(2)}, u32[]{:S(2)}) collective-permute-start(f32[48,1104]{1,0:T(8,128)S(1)} %add.25), channel_id=1, source_target_pairs={{0,8},{8,16},{16,24},{24,0},{1,9},{9,17},{17,25},{25,1},{2,10},{10... | collective-permute-start | bytes 635912 | tf_op jit(solution)/shard_map/ppermute | solution.py:258
  88.5 13.3 %collective-permute-start.27 = (bf16[92,1104]{1,0:T(8,128)(2,1)S(1)}, bf16[92,1104]{1,0:T(8,128)(2,1)S(1)}, u32[]{:S(2)}, u32[]{:S(2)}) collective-permute-start(bf16[92,1104]{1,0:T(8,128)(2,1)S(1)} %pad_maximum_fusion), channel_id=1, source_target_pairs={{0,0},{1,9},{2,18},{3,27},{4,4},{5,13},{6,22},{7,31},{8,1},{9,8},{... | collective-permute-start | bytes 609416 | tf_op jit(solution)/shard_map/ppermute | solution.py:298

commit v4 on v3

--- a/solution.py
+++ b/solution.py
@@ -134,41 +134,51 @@
 
 
 def fill_kernel(meta_ref, *refs):
-    rights, (wide_ref, table_ref) = refs[:-6], refs[-6:-4]
-    right_ref, mixed_ref, codes_ref, sem = refs[-4:]
+    rights, (wide_ref, table_ref) = refs[:-7], refs[-7:-5]
+    right_ref, mixed_ref, turned_ref, codes_ref, sem = refs[-5:]
     depth, core, side, col = (meta_ref[m] for m in range(4))
     for source, piece in enumerate(rights):
-        count = 1 if len(piece.shape) == 3 else piece.shape[0]
+        count = piece.shape[0]
         start = STARTS[source]
-        block = piece[...].reshape(count, USLOTS, APAD, LANES)
-        right_ref[start : start + count] = block
-        codes = block[:, :, BLK, :].astype(jnp.float32).astype(jnp.int32)
-        local = codes - 16 * (depth // 4)
-        chunk = lax.bitwise_xor(lax.shift_right_arithmetic(local, 2), depth % 4)
-        at = CHUNK * ((chunk - col) & 3) + BLK * (local & 3)
-        at = jnp.where((local >= 0) & (local < 16), at, 4 * LANES)
-        tiny = lax.broadcasted_iota(jnp.int32, codes.shape, 2) < HERE
-        mixed_ref[start * USLOTS : (start + count) * USLOTS] = jnp.where(tiny, at, codes).reshape(-1, LANES)
-    copy = pltpu.make_async_copy(mixed_ref, codes_ref, sem)
+        right_ref[start : start + count] = piece[...]
+        for n in range(count):
+            for u in range(USLOTS):
+                row = (start + n) * USLOTS + u
+                mixed_ref[row : row + 1, :] = piece[n, u, BLK : BLK + 1, :].astype(jnp.float32)
+    codes = jnp.concatenate(
+        [mixed_ref[h * LANES : (h + 1) * LANES, :].T[0:8, :] for h in range(2)], axis=1
+    ).astype(jnp.int32)
+    local = codes - 16 * lax.shift_right_arithmetic(depth, 2)
+    chunk = lax.bitwise_xor(lax.shift_right_arithmetic(local, 2), depth & 3)
+    at = CHUNK * ((chunk - col) & 3) + BLK * (local & 3)
+    at = jnp.where((local >= 0) & (local < 16), at, 4 * LANES)
+    turned_ref[0:8, :] = at
+    turned_ref[8:16, :] = (at + 4 * LANES - BLK * lax.broadcasted_iota(jnp.int32, at.shape, 0)) & (LANES - 1)
+    copy = pltpu.make_async_copy(turned_ref, codes_ref, sem)
     copy.start()
-    lane = lax.broadcasted_iota(jnp.int32, (8, LANES), 1)
+    table_ref[...] = mixed_ref[0 : GROUP * USLOTS, :].astype(jnp.int32)
+    lanes = [lax.broadcasted_iota(jnp.int32, (8, LANES), 1) + q * LANES for q in range(3)]
     blank = jnp.zeros((8, LANES), jnp.float32)
     copy.wait()
 
     def fill(n, carry):
-        j = (n // GROUP) % 4
-        row = 2 * ((side + jnp.where(j == 1, 3, j - j // 2)) % 4) + lax.bitwise_xor(core, n // 32)
-        place_in = n % GROUP
-        panel = lax.bitwise_xor(depth // 4, place_in // 4) * 4 + ((depth - place_in) & 3)
+        j = lax.shift_right_logical(n, 3) & 3
+        x = side + jnp.where(j == 1, 3, j - lax.shift_right_logical(j, 1))
+        row = 2 * (x & 3) + lax.bitwise_xor(core, lax.shift_right_logical(n, 5))
+        spot = n & 7
+        panel = lax.bitwise_xor(lax.shift_right_logical(depth, 2), lax.shift_right_logical(spot, 2)) * 4 + (
+            (depth - spot) & 3
+        )
         base = panel * PANEL + row * HERE
+        first = n * USLOTS
         blocks = [right_ref[n, u].astype(jnp.float32) for u in range(USLOTS)]
         for k in range(HERE):
             z = [[blank] * 3 for _ in range(3)]
             for u in range(USLOTS):
-                at = codes_ref[n * USLOTS + u, k]
-                rolled = pltpu.roll(blocks[u], (at + 4 * LANES - BLK * k) % LANES, 1)
+                at = codes_ref[k, first + u]
+                rolled = pltpu.roll(blocks[u], codes_ref[8 + k, first + u], 1)
                 for q in range(3):
-                    here = (lane + (q * LANES - at)).astype(jnp.uint32) < BLK
+                    here = (lanes[q] - at).astype(jnp.uint32) < BLK
                     for v in range(3):
                         z[q][v] = jnp.where(here, rolled[8 * v : 8 * v + 8], z[q][v])
             for q in range(3):
@@ -176,12 +186,10 @@
         return carry
 
     lax.fori_loop(0, 8 * GROUP, fill, 0, unroll=4)
-    table_ref[...] = mixed_ref[0 : GROUP * USLOTS]
 
 
 def fill(meta, rights):
     vmem = pl.BlockSpec(memory_space=pltpu.VMEM)
-    lines = 8 * GROUP * USLOTS
     return pl.pallas_call(
         fill_kernel,
         out_shape=(
@@ -192,8 +200,9 @@
         out_specs=(vmem, vmem),
         scratch_shapes=[
             pltpu.VMEM((8 * GROUP, USLOTS, APAD, LANES), jnp.bfloat16),
-            pltpu.VMEM((lines, LANES), jnp.int32),
-            pltpu.SMEM((lines, LANES), jnp.int32),
+            pltpu.VMEM((2 * LANES, LANES), jnp.float32),
+            pltpu.VMEM((16, 2 * LANES), jnp.int32),
+            pltpu.SMEM((16, 2 * LANES), jnp.int32),
             pltpu.SemaphoreType.DMA,
         ],
         compiler_params=pltpu.CompilerParams(vmem_limit_bytes=16 * 1024 * 1024),
@@ -201,29 +210,47 @@
     )(meta, *rights)
 
 
-def product_kernel(meta_ref, table_ref, wide_ref, *refs):
-    lefts, outs, (far_ref, sum_ref, part_ref) = refs[:9], refs[9:16], refs[16:]
+def picked(meta_ref, table_ref, wide_ref, offsets, i):
     depth = meta_ref[0]
-    panels = [(depth + o) % GROUP for o in OFFSETS]
-    lines = [(lax.bitwise_xor(p // 4, depth // 4) * 4 + ((depth - p) & 3)) * USLOTS for p in panels]
-    half = ROWS // 2
-    far_ref[:half] = lefts[7][...]
-    far_ref[half:] = lefts[8][...]
-    lefts = (*lefts[:7], far_ref)
+    at = []
+    for o in offsets:
+        panel = (depth + o) & 7
+        line = lax.bitwise_xor(lax.shift_right_logical(panel, 2), lax.shift_right_logical(depth, 2)) * 4 + (
+            (depth - panel) & 3
+        )
+        for s in range(SLOTS):
+            at.append(panel * PANEL + table_ref[line * USLOTS + s // 2, 16 + ROWS * (s % 2) + i])
+    return jnp.concatenate([jnp.concatenate([wide_ref[n, q] for n in at], axis=0) for q in range(3)], axis=1)
+
+
+def early_kernel(meta_ref, table_ref, wide_ref, *refs):
+    lefts, out_ref = refs[:4], refs[4]
 
     def step(g, carry):
         for m in range(8):
             i = g * 8 + m
-            at = [
-                p * PANEL + table_ref[line + s // 2, 16 + ROWS * (s % 2) + i]
-                for p, line in zip(panels, lines)
-                for s in range(SLOTS)
-            ]
-            weights = jnp.concatenate(
-                [jnp.concatenate([wide_ref[n, q] for n in at], axis=0) for q in range(3)], axis=1
-            )
+            weights = picked(meta_ref, table_ref, wide_ref, OFFSETS[:4], i)
             rows = jnp.concatenate([x[i] for x in lefts], axis=1)
-            part_ref[m * BLK : m * BLK + APAD, :] = jnp.dot(rows, weights, preferred_element_type=jnp.float32)
+            out_ref[i] = jnp.dot(rows, weights, preferred_element_type=jnp.float32)
+        return carry
+
+    lax.fori_loop(0, ROWS // 8, step, 0)
+
+
+def late_kernel(meta_ref, table_ref, wide_ref, early_ref, *refs):
+    lefts, outs, (far_ref, sum_ref, part_ref) = refs[:5], refs[5:12], refs[12:]
+    half = ROWS // 2
+    far_ref[:half] = lefts[3][...]
+    far_ref[half:] = lefts[4][...]
+    lefts = (*lefts[:3], far_ref)
+
+    def step(g, carry):
+        for m in range(8):
+            i = g * 8 + m
+            weights = picked(meta_ref, table_ref, wide_ref, OFFSETS[4:], i)
+            rows = jnp.concatenate([x[i] for x in lefts], axis=1)
+            total = early_ref[i] + jnp.dot(rows, weights, preferred_element_type=jnp.float32)
+            part_ref[m * BLK : m * BLK + APAD, :] = total
         sum_ref[pl.ds(pl.multiple_of(g * 8 * BLK, 8), 8 * BLK), :] = part_ref[0 : 8 * BLK, :]
         return carry
 
@@ -239,10 +266,19 @@
 def product(meta, table, wide, lefts):
     vmem = pl.BlockSpec(memory_space=pltpu.VMEM)
     smem = pl.BlockSpec(memory_space=pltpu.SMEM)
+    cost = pl.CostEstimate(flops=3_000_000_000, bytes_accessed=4_000_000, transcendentals=0)
+    early = pl.pallas_call(
+        early_kernel,
+        out_shape=jax.ShapeDtypeStruct((ROWS, APAD, WIDE), jnp.float32),
+        in_specs=[smem, smem, vmem] + [vmem] * 4,
+        out_specs=vmem,
+        compiler_params=pltpu.CompilerParams(vmem_limit_bytes=8 * 1024 * 1024),
+        cost_estimate=cost,
+    )(meta, table, wide, *lefts[:4])
     return pl.pallas_call(
-        product_kernel,
+        late_kernel,
         out_shape=tuple(jax.ShapeDtypeStruct((b - a, ROWS * BLK), jnp.float32) for a, b in SPANS),
-        in_specs=[smem, smem, vmem] + [vmem] * len(lefts),
+        in_specs=[smem, smem, vmem, vmem] + [vmem] * 5,
         out_specs=(vmem,) * len(SPANS),
         scratch_shapes=[
             pltpu.VMEM((ROWS, APAD, LANES), jnp.bfloat16),
@@ -250,8 +286,8 @@
             pltpu.VMEM((8 * APAD, WIDE), jnp.float32),
         ],
         compiler_params=pltpu.CompilerParams(vmem_limit_bytes=12 * 1024 * 1024),
-        cost_estimate=pl.CostEstimate(flops=6_000_000_000, bytes_accessed=8_000_000, transcendentals=0),
-    )(meta, table, wide, *lefts)
+        cost_estimate=cost,
+    )(meta, table, wide, early, *lefts[4:])
 
 
 def shift(x, axis, by, n):
@@ -269,17 +305,14 @@
     up1, down1 = shift(left, "depth", 1, 8), shift(left, "depth", -1, 8)
     half = jnp.stack(near, axis=0)
     other = shift(half, "depth", 4, 8)
-    up1, down1, half, other = lax.optimization_barrier((up1, down1, half, other))
     right = jnp.concatenate([half, other], axis=0)
+    swap = [(i, i ^ 1) for i in range(8)]
     f1, b1 = shift(right, "row", 2, 8), shift(right, "row", -2, 8)
     up2, down2 = shift(up1, "depth", 1, 8), shift(down1, "depth", -1, 8)
-    up2, down2, f1, b1 = lax.optimization_barrier((up2, down2, f1, b1))
-    swap = [(i, i ^ 1) for i in range(8)]
     f2, b2 = shift(f1[:4], "row", 2, 8), shift(b1[4:], "row", -2, 8)
+    others = [lax.ppermute(x, "row", swap) for x in (right, f1, b1)]
+    others += [lax.ppermute(x, "row", swap) for x in (f2, b2)]
     up3, down3 = shift(up2, "depth", 1, 8), shift(down2, "depth", -1, 8)
-    others = [lax.ppermute(x, "row", swap) for x in (right, f1, b1)]
-    up3, down3, f2, b2 = lax.optimization_barrier((up3, down3, f2, b2))
-    others += [lax.ppermute(x, "row", swap) for x in (f2, b2)]
     edge = ROWS // 2
     up4, down4 = shift(up3[:edge], "depth", 1, 8), shift(down3[edge:], "depth", -1, 8)
     lefts = [left, up1, down1, up2, down2, up3, down3, up4, down4]

time: 103 us -> 96.3 us (0.935)
  waiting for transfers between devices: 36.8 us -> 30.7 us
  Pallas kernels: 19.4 us -> 16.5 us
  starting transfers between devices: 42 us -> 44.4 us
    ppermute x19, waiting for transfers between devices: 25.3 us -> 19.4 us  [shift(): return lax.ppermute(x, axis, [(i, (i + by) % n) for i in range(n)])]
    pallas_call x1, Pallas kernels: 10.2 us -> 5.58 us  [fill(): pl.pallas_call(fill_kernel, out_shape=(jax.ShapeDtypeStruct((GROUP * PANE...]
    ppermute x19, starting transfers between devices: 33.2 us -> 36.8 us  [shift(): return lax.ppermute(x, axis, [(i, (i + by) % n) for i in range(n)])]
    pallas_call x1 -> x2, Pallas kernels: 7.63 us -> 9.37 us  [the longest x1 5.08 us: product(): pl.pallas_call(late_kernel, out_shape=tuple((jax.ShapeDtypeStruct((b - a,...]
    ppermute x1, starting transfers between devices: 4.28 us -> 3.04 us  [body(): return lax.ppermute(done, ('col', 'depth'), home).T]
    unnamed x10 -> x13, local copies, waits for them, and re-layouts: 3.9 us -> 3.92 us
  transfers between devices with their start and end apart: 28 -> 28, of which waited for: 12 -> 13; matrix products, arithmetic and copies ran while one was open for 0% -> 0% of each run, Pallas kernels for 11% -> 11%
where the time goes in v4:
time: 96.3 us; the launch traced here: 96 us
  starting transfers between devices  44.4 us (46%)
  waiting for transfers between devices  30.7 us (32%)
  Pallas kernels  16.5 us (17%)
  local copies, waits for them, and re-layouts  3.98 us (4%)
    ppermute x19, starting transfers between devices, shift(): return lax.ppermute(x, axis, [(i, (i + by) % n) for i in range(n)])  36.8 us
    ppermute x19, waiting for transfers between devices, shift(): return lax.ppermute(x, axis, [(i, (i + by) % n) for i in range(n)])  19.4 us
    ppermute x1, waiting for transfers between devices, body(): return lax.ppermute(done, ('col', 'depth'), home).T  8.8 us
    pallas_call x1, Pallas kernels, fill(): pl.pallas_call(fill_kernel, out_shape=(jax.ShapeDtypeStruct((GROUP * PANE...  5.58 us
    pallas_call x1, Pallas kernels, product(): pl.pallas_call(late_kernel, out_shape=tuple((jax.ShapeDtypeStruct((b - a,...  5.08 us
    pallas_call x1, Pallas kernels, product(): pl.pallas_call(early_kernel, out_shape=jax.ShapeDtypeStruct((ROWS, APAD,...  4.29 us
    unnamed x13, local copies, waits for them, and re-layouts  3.92 us
    ppermute x3, starting transfers between devices, body(): lax.ppermute(tiles[k], 'depth', [(z, z // 4 * 4 + (z + k) % 4) for z in r...  3.9 us
  transfers between devices with their start and end apart: 28, of which 13 were waited for; matrix products, arithmetic and copies ran while one was open for 0% of the time, Pallas kernels for 11%

profile of v4, /device:TPU:16, one launch (start us, length us, event | category | flops | bytes accessed | tf_op | source)
XLA Modules:
  0.0 96.0 jit_solution(17908566009918301863)
XLA Ops:
  0.0 0.9 copy-done
  0.9 0.5 shard_map.48.refs_0_
  1.5 5.9 %collective-permute-start.14 = (bf16[48,24,128]{2,1,0:T(8,128)(2,1)S(1)}, bf16[48,24,128]{2,1,0:T(8,128)(2,1)S(1)}, u32[]{:S(2)}, u32[]{:S(2)}) collective-permute-start(bf16[48,24,128]{2,1,0:T(8,128)(2,1)S(1)} %shard_map.48.refs_0_), channel_id=1, source_target_pairs={{0,7},{1,0},{2,1},{3,2},{4,3},{5,4},{6,5},{7,6},{8,15},{9,8},{10,9... | collective-permute-start | bytes 884744 | tf_op jit(solution)/shard_map/ppermute | solution.py:294
  7.4 0.0 collective-permute-start.13
  7.4 0.1 pad_add_fusion.meta_ref
  7.5 0.9 copy-done.1
  8.4 0.7 copy-done.2
  9.0 0.7 copy-done.3
  9.7 1.0 %shard_map.46 = (bf16[3,24,128]{2,1,0:T(8,128)(2,1)S(1)}, bf16[3,24,128]{2,1,0:T(8,128)(2,1)S(1)}, bf16[3,24,128]{2,1,0:T(8,128)(2,1)S(1)}, bf16[3,24,128]{2,1,0:T(8,128)(2,1)S(1)}) custom-call(s32[4]{0:T(128)S(1)} %pad_add_fusion.meta_ref, bf16[5,3,4,529]{3,2,1,0:T(4,128)(2,1)S(1)} %bitcast.24, s32[3,4,5]{2,1,0:T(4,128)S(1)} %bitcast.26, s32[4,48]{1,0:T(4,128)S(1)} %bitcast.27), custom_call_target="tpu_custom_call" | custom-call | tf_op jit(solution)/shard_map/pallas_call | solution.py:117
  10.8 0.1 collective-permute-start
  10.9 2.6 %collective-permute-start.1 = (bf16[3,24,128]{2,1,0:T(8,128)(2,1)S(1)}, bf16[3,24,128]{2,1,0:T(8,128)(2,1)S(1)}, u32[]{:S(2)}, u32[]{:S(2)}) collective-permute-start(bf16[3,24,128]{2,1,0:T(8,128)(2,1)S(1)} %get-tuple-element.20), channel_id=1, source_target_pairs={{0,2},{1,3},{2,0},{3,1},{4,6},{5,7},{6,4},{7,5},{8,10},{9,11},{10,... | collective-permute-start | bytes 55304 | tf_op jit(solution)/shard_map/ppermute | solution.py:303
  13.4 1.3 %collective-permute-start.2 = (bf16[3,24,128]{2,1,0:T(8,128)(2,1)S(1)}, bf16[3,24,128]{2,1,0:T(8,128)(2,1)S(1)}, u32[]{:S(2)}, u32[]{:S(2)}) collective-permute-start(bf16[3,24,128]{2,1,0:T(8,128)(2,1)S(1)} %get-tuple-element.21), channel_id=1, source_target_pairs={{0,3},{1,0},{2,1},{3,2},{4,7},{5,4},{6,5},{7,6},{8,11},{9,8},{10,9... | collective-permute-start | bytes 55304 | tf_op jit(solution)/shard_map/ppermute | solution.py:303
  14.7 1.7 %collective-permute-done = bf16[3,24,128]{2,1,0:T(8,128)(2,1)S(1)} collective-permute-done((bf16[3,24,128]{2,1,0:T(8,128)(2,1)S(1)}, bf16[3,24,128]{2,1,0:T(8,128)(2,1)S(1)}, u32[]{:S(2)}, u32[]{:S(2)}) %collective-permute-start) | collective-permute-done | bytes 18464 | tf_op jit(solution)/shard_map/ppermute | solution.py:303
  16.4 0.0 collective-permute-done.1
  16.4 0.8 collective-permute-done.2
  17.2 4.6 %collective-permute-start.3 = (bf16[4,3,24,128]{3,2,1,0:T(8,128)(2,1)S(1)}, bf16[4,3,24,128]{3,2,1,0:T(8,128)(2,1)S(1)}, u32[]{:S(2)}, u32[]{:S(2)}) collective-permute-start(bf16[4,3,24,128]{3,2,1,0:T(8,128)(2,1)S(1)} %pad_maximum_fusion.1), channel_id=1, source_target_pairs={{0,4},{1,5},{2,6},{3,7},{4,0},{5,1},{6,2},{7,3},{8,12},{9,13},{10,... | collective-permute-start | bytes 221192 | tf_op jit(solution)/shard_map/ppermute | solution.py:294
  21.8 4.0 %collective-permute-done.3 = bf16[4,3,24,128]{3,2,1,0:T(8,128)(2,1)S(1)} collective-permute-done((bf16[4,3,24,128]{3,2,1,0:T(8,128)(2,1)S(1)}, bf16[4,3,24,128]{3,2,1,0:T(8,128)(2,1)S(1)}, u32[]{:S(2)}, u32[]{:S(2)}) %collective-permute-start.3) | collective-permute-done | bytes 73760 | tf_op jit(solution)/shard_map/ppermute | solution.py:294
  25.8 2.8 %collective-permute-start.5 = (bf16[8,3,24,128]{3,2,1,0:T(8,128)(2,1)S(1)}, bf16[8,3,24,128]{3,2,1,0:T(8,128)(2,1)S(1)}, u32[]{:S(2)}, u32[]{:S(2)}) collective-permute-start(bf16[8,3,24,128]{3,2,1,0:T(8,128)(2,1)S(1)} %constant_dynamic-update-slice_fusion.refs_0_), channel_id=1, source_target_pairs={{0,192},{32,224},{64,0},{96,32},{128,64},{160,96},{192,128},{224,1... | collective-permute-start | bytes 442376 | tf_op jit(solution)/shard_map/ppermute | solution.py:294
  28.6 4.3 %collective-permute-start.16 = (bf16[48,24,128]{2,1,0:T(8,128)(2,1)S(1)}, bf16[48,24,128]{2,1,0:T(8,128)(2,1)S(1)}, u32[]{:S(2)}, u32[]{:S(2)}) collective-permute-start(bf16[48,24,128]{2,1,0:T(8,128)(2,1)S(1)} %collective-permute-done.14.refs_2_), channel_id=1, source_target_pairs={{0,7},{1,0},{2,1},{3,2},{4,3},{5,4},{6,5},{7,6},{8,15},{9,8},{10,9... | collective-permute-start | bytes 884744 | tf_op jit(solution)/shard_map/ppermute | solution.py:294
  33.0 3.3 %collective-permute-start.7 = (bf16[4,3,24,128]{3,2,1,0:T(8,128)(2,1)S(1)}, bf16[4,3,24,128]{3,2,1,0:T(8,128)(2,1)S(1)}, u32[]{:S(2)}, u32[]{:S(2)}) collective-permute-start(bf16[4,3,24,128]{3,2,1,0:T(8,128)(2,1)S(1)} %slice.25), channel_id=1, source_target_pairs={{0,192},{32,224},{64,0},{96,32},{128,64},{160,96},{192,128},{224,1... | collective-permute-start | bytes 221192 | tf_op jit(solution)/shard_map/ppermute | solution.py:294
  36.3 0.2 collective-permute-start.10
  36.5 0.1 collective-permute-start.6
  36.6 1.9 %collective-permute-done.7.refs_4_ = bf16[4,3,24,128]{3,2,1,0:T(8,128)(2,1)S(1)} collective-permute-done((bf16[4,3,24,128]{3,2,1,0:T(8,128)(2,1)S(1)}, bf16[4,3,24,128]{3,2,1,0:T(8,128)(2,1)S(1)}, u32[]{:S(2)}, u32[]{:S(2)}) %collective-permute-start.7) | collective-permute-done | bytes 73760 | tf_op jit(solution)/shard_map/ppermute | solution.py:294
  38.5 3.8 %collective-permute-done.6.refs_3_ = bf16[4,3,24,128]{3,2,1,0:T(8,128)(2,1)S(1)} collective-permute-done((bf16[4,3,24,128]{3,2,1,0:T(8,128)(2,1)S(1)}, bf16[4,3,24,128]{3,2,1,0:T(8,128)(2,1)S(1)}, u32[]{:S(2)}, u32[]{:S(2)}) %collective-permute-start.6) | collective-permute-done | bytes 73760 | tf_op jit(solution)/shard_map/ppermute | solution.py:294
  42.3 0.5 collective-permute-start.11
  42.8 3.2 %collective-permute-start.18 = (bf16[48,24,128]{2,1,0:T(8,128)(2,1)S(1)}, bf16[48,24,128]{2,1,0:T(8,128)(2,1)S(1)}, u32[]{:S(2)}, u32[]{:S(2)}) collective-permute-start(bf16[48,24,128]{2,1,0:T(8,128)(2,1)S(1)} %collective-permute-done.16.refs_0_), channel_id=1, source_target_pairs={{0,7},{1,0},{2,1},{3,2},{4,3},{5,4},{6,5},{7,6},{8,15},{9,8},{10,9... | collective-permute-start | bytes 884744 | tf_op jit(solution)/shard_map/ppermute | solution.py:294
  46.0 5.6 %shard_map.47 = (bf16[320,3,32,128]{3,2,1,0:T(8,128)(2,1)S(1)}, s32[24,128]{1,0:T(8,128)S(1)}) custom-call(s32[4]{0:T(128)S(1)} %pad_add_fusion.meta_ref, bf16[8,3,24,128]{3,2,1,0:T(8,128)(2,1)S(1)} %constant_dynamic-update-slice_fusion.refs_0_, bf16[8,3,24,128]{3,2,1,0:T(8,128)(2,1)S(1)} %collective-permute-done.4.refs_1_, ...), custom_call_target="tpu_custom_call" | custom-call | flops 3000000000 | bytes 8000000 | tf_op jit(solution)/shard_map/pallas_call | solution.py:193
  51.6 0.9 collective-permute-done.18.refs_2_
  52.5 3.8 %collective-permute-start.20 = (bf16[24,24,128]{2,1,0:T(8,128)(2,1)S(1)}, bf16[24,24,128]{2,1,0:T(8,128)(2,1)S(1)}, u32[]{:S(2)}, u32[]{:S(2)}) collective-permute-start(bf16[24,24,128]{2,1,0:T(8,128)(2,1)S(1)} %slice.27), channel_id=1, source_target_pairs={{0,7},{1,0},{2,1},{3,2},{4,3},{5,4},{6,5},{7,6},{8,15},{9,8},{10,9... | collective-permute-start | bytes 442376 | tf_op jit(solution)/shard_map/ppermute | solution.py:294
  56.3 0.1 collective-permute-start.19
  56.4 4.3 %shard_map.49.early_ref = f32[48,24,384]{2,1,0:T(8,128)S(1)} custom-call(s32[4]{0:T(128)S(1)} %pad_add_fusion.meta_ref, s32[24,128]{1,0:T(8,128)S(1)} %get-tuple-element.22.table_ref, bf16[320,3,32,128]{3,2,1,0:T(8,128)(2,1)S(1)} %get-tuple-element.23.wide_ref, bf16[48,24,128]{2,1,0:T(8,128)(2,1)S(1)} %shard_map.48.refs_0_, ...), custom_call_target="tpu_custom_call" | custom-call | flops 3000000000 | bytes 4000000 | tf_op jit(solution)/shard_map/pallas_call | solution.py:270
  60.7 2.0 %collective-permute-done.19.refs_3_ = bf16[24,24,128]{2,1,0:T(8,128)(2,1)S(1)} collective-permute-done((bf16[24,24,128]{2,1,0:T(8,128)(2,1)S(1)}, bf16[24,24,128]{2,1,0:T(8,128)(2,1)S(1)}, u32[]{:S(2)}, u32[]{:S(2)}) %collective-permute-start.19) | collective-permute-done | bytes 147488 | tf_op jit(solution)/shard_map/ppermute | solution.py:294
  62.8 5.1 %shard_map.50 = (f32[92,1104]{1,0:T(8,128)S(1)}, f32[48,1104]{1,0:T(8,128)S(1)}, f32[44,1104]{1,0:T(8,128)S(1)}, f32[48,1104]{1,0:T(8,128)S(1)}, f32[44,1104]{1,...) custom-call(s32[4]{0:T(128)S(1)} %pad_add_fusion.meta_ref, s32[24,128]{1,0:T(8,128)S(1)} %get-tuple-element.22.table_ref, ...), custom_call_target="tpu_custom_call" | custom-call | flops 3000000000 | bytes 4000000 | tf_op jit(solution)/shard_map/pallas_call | solution.py:278
  67.8 0.5 collective-permute-start.25
  68.4 1.6 %collective-permute-start.22 = (f32[48,1104]{1,0:T(8,128)S(1)}, f32[48,1104]{1,0:T(8,128)S(1)}, u32[]{:S(2)}, u32[]{:S(2)}) collective-permute-start(f32[48,1104]{1,0:T(8,128)S(1)} %get-tuple-element.27), channel_id=1, source_target_pairs={{0,8},{8,16},{16,24},{24,0},{1,9},{9,17},{17,25},{25,1},{2,10},{10... | collective-permute-start | bytes 635912 | tf_op jit(solution)/shard_map/ppermute | solution.py:294
  70.0 2.5 %collective-permute-start.24 = (f32[44,1104]{1,0:T(8,128)S(1)}, f32[44,1104]{1,0:T(8,128)S(1)}, u32[]{:S(2)}, u32[]{:S(2)}) collective-permute-start(f32[44,1104]{1,0:T(8,128)S(1)} %get-tuple-element.28), channel_id=1, source_target_pairs={{0,8},{8,16},{16,24},{24,0},{1,9},{9,17},{17,25},{25,1},{2,10},{10... | collective-permute-start | bytes 582920 | tf_op jit(solution)/shard_map/ppermute | solution.py:294
  72.5 1.4 %collective-permute-done.25 = f32[44,1104]{1,0:T(8,128)S(1)} collective-permute-done((f32[44,1104]{1,0:T(8,128)S(1)}, f32[44,1104]{1,0:T(8,128)S(1)}, u32[]{:S(2)}, u32[]{:S(2)}) %collective-permute-start.25) | collective-permute-done | bytes 194336 | tf_op jit(solution)/shard_map/ppermute | solution.py:294
  73.9 1.2 %collective-permute-start.26 = (f32[44,1104]{1,0:T(8,128)S(1)}, f32[44,1104]{1,0:T(8,128)S(1)}, u32[]{:S(2)}, u32[]{:S(2)}) collective-permute-start(f32[44,1104]{1,0:T(8,128)S(1)} %add.28), channel_id=1, source_target_pairs={{0,24},{8,0},{16,8},{24,16},{1,25},{9,1},{17,9},{25,17},{2,26},{10... | collective-permute-start | bytes 582920 | tf_op jit(solution)/shard_map/ppermute | solution.py:294
  75.1 0.3 collective-permute-start.21
  75.4 0.4 collective-permute-done.22
  75.8 2.6 %collective-permute-start.23 = (f32[48,1104]{1,0:T(8,128)S(1)}, f32[48,1104]{1,0:T(8,128)S(1)}, u32[]{:S(2)}, u32[]{:S(2)}) collective-permute-start(f32[48,1104]{1,0:T(8,128)S(1)} %add.25), channel_id=1, source_target_pairs={{0,8},{8,16},{16,24},{24,0},{1,9},{9,17},{17,25},{25,1},{2,10},{10... | collective-permute-start | bytes 635912 | tf_op jit(solution)/shard_map/ppermute | solution.py:294
  78.4 1.4 %collective-permute-done.24 = f32[44,1104]{1,0:T(8,128)S(1)} collective-permute-done((f32[44,1104]{1,0:T(8,128)S(1)}, f32[44,1104]{1,0:T(8,128)S(1)}, u32[]{:S(2)}, u32[]{:S(2)}) %collective-permute-start.24) | collective-permute-done | bytes 194336 | tf_op jit(solution)/shard_map/ppermute | solution.py:294
  79.8 1.3 %collective-permute-done.26 = f32[44,1104]{1,0:T(8,128)S(1)} collective-permute-done((f32[44,1104]{1,0:T(8,128)S(1)}, f32[44,1104]{1,0:T(8,128)S(1)}, u32[]{:S(2)}, u32[]{:S(2)}) %collective-permute-start.26) | collective-permute-done | bytes 194336 | tf_op jit(solution)/shard_map/ppermute | solution.py:294
  81.1 0.1 add_convert_fusion
  81.1 2.3 %collective-permute-done.21 = f32[48,1104]{1,0:T(8,128)S(1)} collective-permute-done((f32[48,1104]{1,0:T(8,128)S(1)}, f32[48,1104]{1,0:T(8,128)S(1)}, u32[]{:S(2)}, u32[]{:S(2)}) %collective-permute-start.21) | collective-permute-done | bytes 212000 | tf_op jit(solution)/shard_map/ppermute | solution.py:294
  83.5 3.0 %collective-permute-start.27 = (bf16[92,1104]{1,0:T(8,128)(2,1)S(1)}, bf16[92,1104]{1,0:T(8,128)(2,1)S(1)}, u32[]{:S(2)}, u32[]{:S(2)}) collective-permute-start(bf16[92,1104]{1,0:T(8,128)(2,1)S(1)} %pad_maximum_fusion), channel_id=1, source_target_pairs={{0,0},{1,9},{2,18},{3,27},{4,4},{5,13},{6,22},{7,31},{8,1},{9,8},{... | collective-permute-start | bytes 609416 | tf_op jit(solution)/shard_map/ppermute | solution.py:331
  86.6 8.8 %collective-permute-done.27 = bf16[92,1104]{1,0:T(8,128)(2,1)S(1)} collective-permute-done((bf16[92,1104]{1,0:T(8,128)(2,1)S(1)}, bf16[92,1104]{1,0:T(8,128)(2,1)S(1)}, u32[]{:S(2)}, u32[]{:S(2)}) %collective-permute-start.27) | collective-permute-done | bytes 203168 | tf_op jit(solution)/shard_map/ppermute | solution.py:331
  95.4 0.7 copy.10
  (38 shorter events, 0.3 us)
Async XLA Ops:
  0.0 0.9 copy-start
  1.5 27.2 %collective-permute-start.14 = (bf16[48,24,128]{2,1,0:T(8,128)(2,1)S(1)}, bf16[48,24,128]{2,1,0:T(8,128)(2,1)S(1)}, u32[]{:S(2)}, u32[]{:S(2)}) collective-permute-start(bf16[48,24,128]{2,1,0:T(8,128)(2,1)S(1)} %shard_map.48.refs_0_), channel_id=1, source_target_pairs={{0,7},{1,0},{2,1},{3,2},{4,3},{5,4},{6,5},{7,6},{8,15},{9,8},{10,9... | collective-permute-start | bytes 884744 | tf_op jit(solution)/shard_map/ppermute | solution.py:294
  7.4 25.5 %collective-permute-start.13 = (bf16[48,24,128]{2,1,0:T(8,128)(2,1)S(1)}, bf16[48,24,128]{2,1,0:T(8,128)(2,1)S(1)}, u32[]{:S(2)}, u32[]{:S(2)}) collective-permute-start(bf16[48,24,128]{2,1,0:T(8,128)(2,1)S(1)} %shard_map.48.refs_0_), channel_id=1, source_target_pairs={{0,1},{1,2},{2,3},{3,4},{4,5},{5,6},{6,7},{7,0},{8,9},{9,10},{10,1... | collective-permute-start | bytes 884744 | tf_op jit(solution)/shard_map/ppermute | solution.py:294
  7.5 0.9 copy-start.1
  8.4 0.7 copy-start.2
  9.0 0.7 copy-start.3
  10.8 5.6 %collective-permute-start = (bf16[3,24,128]{2,1,0:T(8,128)(2,1)S(1)}, bf16[3,24,128]{2,1,0:T(8,128)(2,1)S(1)}, u32[]{:S(2)}, u32[]{:S(2)}) collective-permute-start(bf16[3,24,128]{2,1,0:T(8,128)(2,1)S(1)} %get-tuple-element.19), channel_id=1, source_target_pairs={{0,1},{1,2},{2,3},{3,0},{4,5},{5,6},{6,7},{7,4},{8,9},{9,10},{10,1... | collective-permute-start | bytes 55304 | tf_op jit(solution)/shard_map/ppermute | solution.py:303
  10.9 5.6 %collective-permute-start.1 = (bf16[3,24,128]{2,1,0:T(8,128)(2,1)S(1)}, bf16[3,24,128]{2,1,0:T(8,128)(2,1)S(1)}, u32[]{:S(2)}, u32[]{:S(2)}) collective-permute-start(bf16[3,24,128]{2,1,0:T(8,128)(2,1)S(1)} %get-tuple-element.20), channel_id=1, source_target_pairs={{0,2},{1,3},{2,0},{3,1},{4,6},{5,7},{6,4},{7,5},{8,10},{9,11},{10,... | collective-permute-start | bytes 55304 | tf_op jit(solution)/shard_map/ppermute | solution.py:303
  13.4 3.8 %collective-permute-start.2 = (bf16[3,24,128]{2,1,0:T(8,128)(2,1)S(1)}, bf16[3,24,128]{2,1,0:T(8,128)(2,1)S(1)}, u32[]{:S(2)}, u32[]{:S(2)}) collective-permute-start(bf16[3,24,128]{2,1,0:T(8,128)(2,1)S(1)} %get-tuple-element.21), channel_id=1, source_target_pairs={{0,3},{1,0},{2,1},{3,2},{4,7},{5,4},{6,5},{7,6},{8,11},{9,8},{10,9... | collective-permute-start | bytes 55304 | tf_op jit(solution)/shard_map/ppermute | solution.py:303
  17.2 8.6 %collective-permute-start.3 = (bf16[4,3,24,128]{3,2,1,0:T(8,128)(2,1)S(1)}, bf16[4,3,24,128]{3,2,1,0:T(8,128)(2,1)S(1)}, u32[]{:S(2)}, u32[]{:S(2)}) collective-permute-start(bf16[4,3,24,128]{3,2,1,0:T(8,128)(2,1)S(1)} %pad_maximum_fusion.1), channel_id=1, source_target_pairs={{0,4},{1,5},{2,6},{3,7},{4,0},{5,1},{6,2},{7,3},{8,12},{9,13},{10,... | collective-permute-start | bytes 221192 | tf_op jit(solution)/shard_map/ppermute | solution.py:294
  25.8 7.1 %collective-permute-start.5 = (bf16[8,3,24,128]{3,2,1,0:T(8,128)(2,1)S(1)}, bf16[8,3,24,128]{3,2,1,0:T(8,128)(2,1)S(1)}, u32[]{:S(2)}, u32[]{:S(2)}) collective-permute-start(bf16[8,3,24,128]{3,2,1,0:T(8,128)(2,1)S(1)} %constant_dynamic-update-slice_fusion.refs_0_), channel_id=1, source_target_pairs={{0,192},{32,224},{64,0},{96,32},{128,64},{160,96},{192,128},{224,1... | collective-permute-start | bytes 442376 | tf_op jit(solution)/shard_map/ppermute | solution.py:294
  28.6 7.6 %collective-permute-start.4 = (bf16[8,3,24,128]{3,2,1,0:T(8,128)(2,1)S(1)}, bf16[8,3,24,128]{3,2,1,0:T(8,128)(2,1)S(1)}, u32[]{:S(2)}, u32[]{:S(2)}) collective-permute-start(bf16[8,3,24,128]{3,2,1,0:T(8,128)(2,1)S(1)} %constant_dynamic-update-slice_fusion.refs_0_), channel_id=1, source_target_pairs={{0,64},{32,96},{64,128},{96,160},{128,192},{160,224},{192,0},{224,... | collective-permute-start | bytes 442376 | tf_op jit(solution)/shard_map/ppermute | solution.py:294
  28.6 14.1 %collective-permute-start.16 = (bf16[48,24,128]{2,1,0:T(8,128)(2,1)S(1)}, bf16[48,24,128]{2,1,0:T(8,128)(2,1)S(1)}, u32[]{:S(2)}, u32[]{:S(2)}) collective-permute-start(bf16[48,24,128]{2,1,0:T(8,128)(2,1)S(1)} %collective-permute-done.14.refs_2_), channel_id=1, source_target_pairs={{0,7},{1,0},{2,1},{3,2},{4,3},{5,4},{6,5},{7,6},{8,15},{9,8},{10,9... | collective-permute-start | bytes 884744 | tf_op jit(solution)/shard_map/ppermute | solution.py:294
  32.9 13.1 %collective-permute-start.15 = (bf16[48,24,128]{2,1,0:T(8,128)(2,1)S(1)}, bf16[48,24,128]{2,1,0:T(8,128)(2,1)S(1)}, u32[]{:S(2)}, u32[]{:S(2)}) collective-permute-start(bf16[48,24,128]{2,1,0:T(8,128)(2,1)S(1)} %collective-permute-done.13.refs_1_), channel_id=1, source_target_pairs={{0,1},{1,2},{2,3},{3,4},{4,5},{5,6},{6,7},{7,0},{8,9},{9,10},{10,1... | collective-permute-start | bytes 884744 | tf_op jit(solution)/shard_map/ppermute | solution.py:294
  32.9 3.6 %collective-permute-start.8 = (bf16[8,3,24,128]{3,2,1,0:T(8,128)(2,1)S(1)}, bf16[8,3,24,128]{3,2,1,0:T(8,128)(2,1)S(1)}, u32[]{:S(2)}, u32[]{:S(2)}) collective-permute-start(bf16[8,3,24,128]{3,2,1,0:T(8,128)(2,1)S(1)} %constant_dynamic-update-slice_fusion.refs_0_), channel_id=1, source_target_pairs={{0,32},{32,0},{64,96},{96,64},{128,160},{160,128},{192,224},{224,1... | collective-permute-start | bytes 442376 | tf_op jit(solution)/shard_map/ppermute | solution.py:313
  33.0 5.5 %collective-permute-start.7 = (bf16[4,3,24,128]{3,2,1,0:T(8,128)(2,1)S(1)}, bf16[4,3,24,128]{3,2,1,0:T(8,128)(2,1)S(1)}, u32[]{:S(2)}, u32[]{:S(2)}) collective-permute-start(bf16[4,3,24,128]{3,2,1,0:T(8,128)(2,1)S(1)} %slice.25), channel_id=1, source_target_pairs={{0,192},{32,224},{64,0},{96,32},{128,64},{160,96},{192,128},{224,1... | collective-permute-start | bytes 221192 | tf_op jit(solution)/shard_map/ppermute | solution.py:294
  36.3 6.0 %collective-permute-start.10 = (bf16[8,3,24,128]{3,2,1,0:T(8,128)(2,1)S(1)}, bf16[8,3,24,128]{3,2,1,0:T(8,128)(2,1)S(1)}, u32[]{:S(2)}, u32[]{:S(2)}) collective-permute-start(bf16[8,3,24,128]{3,2,1,0:T(8,128)(2,1)S(1)} %collective-permute-done.5.refs_2_), channel_id=1, source_target_pairs={{0,32},{32,0},{64,96},{96,64},{128,160},{160,128},{192,224},{224,1... | collective-permute-start | bytes 442376 | tf_op jit(solution)/shard_map/ppermute | solution.py:313
  36.5 5.8 %collective-permute-start.6 = (bf16[4,3,24,128]{3,2,1,0:T(8,128)(2,1)S(1)}, bf16[4,3,24,128]{3,2,1,0:T(8,128)(2,1)S(1)}, u32[]{:S(2)}, u32[]{:S(2)}) collective-permute-start(bf16[4,3,24,128]{3,2,1,0:T(8,128)(2,1)S(1)} %slice.24), channel_id=1, source_target_pairs={{0,64},{32,96},{64,128},{96,160},{128,192},{160,224},{192,0},{224,... | collective-permute-start | bytes 221192 | tf_op jit(solution)/shard_map/ppermute | solution.py:294
  38.5 7.6 %collective-permute-start.9 = (bf16[8,3,24,128]{3,2,1,0:T(8,128)(2,1)S(1)}, bf16[8,3,24,128]{3,2,1,0:T(8,128)(2,1)S(1)}, u32[]{:S(2)}, u32[]{:S(2)}) collective-permute-start(bf16[8,3,24,128]{3,2,1,0:T(8,128)(2,1)S(1)} %collective-permute-done.4.refs_1_), channel_id=1, source_target_pairs={{0,32},{32,0},{64,96},{96,64},{128,160},{160,128},{192,224},{224,1... | collective-permute-start | bytes 442376 | tf_op jit(solution)/shard_map/ppermute | solution.py:313
  42.3 3.7 %collective-permute-start.12 = (bf16[4,3,24,128]{3,2,1,0:T(8,128)(2,1)S(1)}, bf16[4,3,24,128]{3,2,1,0:T(8,128)(2,1)S(1)}, u32[]{:S(2)}, u32[]{:S(2)}) collective-permute-start(bf16[4,3,24,128]{3,2,1,0:T(8,128)(2,1)S(1)} %collective-permute-done.7.refs_4_), channel_id=1, source_target_pairs={{0,32},{32,0},{64,96},{96,64},{128,160},{160,128},{192,224},{224,1... | collective-permute-start | bytes 221192 | tf_op jit(solution)/shard_map/ppermute | solution.py:314
  42.3 3.8 %collective-permute-start.11 = (bf16[4,3,24,128]{3,2,1,0:T(8,128)(2,1)S(1)}, bf16[4,3,24,128]{3,2,1,0:T(8,128)(2,1)S(1)}, u32[]{:S(2)}, u32[]{:S(2)}) collective-permute-start(bf16[4,3,24,128]{3,2,1,0:T(8,128)(2,1)S(1)} %collective-permute-done.6.refs_3_), channel_id=1, source_target_pairs={{0,32},{32,0},{64,96},{96,64},{128,160},{160,128},{192,224},{224,1... | collective-permute-start | bytes 221192 | tf_op jit(solution)/shard_map/ppermute | solution.py:314
  42.8 9.7 %collective-permute-start.18 = (bf16[48,24,128]{2,1,0:T(8,128)(2,1)S(1)}, bf16[48,24,128]{2,1,0:T(8,128)(2,1)S(1)}, u32[]{:S(2)}, u32[]{:S(2)}) collective-permute-start(bf16[48,24,128]{2,1,0:T(8,128)(2,1)S(1)} %collective-permute-done.16.refs_0_), channel_id=1, source_target_pairs={{0,7},{1,0},{2,1},{3,2},{4,3},{5,4},{6,5},{7,6},{8,15},{9,8},{10,9... | collective-permute-start | bytes 884744 | tf_op jit(solution)/shard_map/ppermute | solution.py:294
  46.0 10.3 %collective-permute-start.17 = (bf16[48,24,128]{2,1,0:T(8,128)(2,1)S(1)}, bf16[48,24,128]{2,1,0:T(8,128)(2,1)S(1)}, u32[]{:S(2)}, u32[]{:S(2)}) collective-permute-start(bf16[48,24,128]{2,1,0:T(8,128)(2,1)S(1)} %collective-permute-done.15.refs_3_), channel_id=1, source_target_pairs={{0,1},{1,2},{2,3},{3,4},{4,5},{5,6},{6,7},{7,0},{8,9},{9,10},{10,1... | collective-permute-start | bytes 884744 | tf_op jit(solution)/shard_map/ppermute | solution.py:294
  52.5 8.2 %collective-permute-start.20 = (bf16[24,24,128]{2,1,0:T(8,128)(2,1)S(1)}, bf16[24,24,128]{2,1,0:T(8,128)(2,1)S(1)}, u32[]{:S(2)}, u32[]{:S(2)}) collective-permute-start(bf16[24,24,128]{2,1,0:T(8,128)(2,1)S(1)} %slice.27), channel_id=1, source_target_pairs={{0,7},{1,0},{2,1},{3,2},{4,3},{5,4},{6,5},{7,6},{8,15},{9,8},{10,9... | collective-permute-start | bytes 442376 | tf_op jit(solution)/shard_map/ppermute | solution.py:294
  56.3 6.4 %collective-permute-start.19 = (bf16[24,24,128]{2,1,0:T(8,128)(2,1)S(1)}, bf16[24,24,128]{2,1,0:T(8,128)(2,1)S(1)}, u32[]{:S(2)}, u32[]{:S(2)}) collective-permute-start(bf16[24,24,128]{2,1,0:T(8,128)(2,1)S(1)} %slice.26), channel_id=1, source_target_pairs={{0,1},{1,2},{2,3},{3,4},{4,5},{5,6},{6,7},{7,0},{8,9},{9,10},{10,1... | collective-permute-start | bytes 442376 | tf_op jit(solution)/shard_map/ppermute | solution.py:294
  67.8 6.0 %collective-permute-start.25 = (f32[44,1104]{1,0:T(8,128)S(1)}, f32[44,1104]{1,0:T(8,128)S(1)}, u32[]{:S(2)}, u32[]{:S(2)}) collective-permute-start(f32[44,1104]{1,0:T(8,128)S(1)} %get-tuple-element.30), channel_id=1, source_target_pairs={{0,24},{8,0},{16,8},{24,16},{1,25},{9,1},{17,9},{25,17},{2,26},{10... | collective-permute-start | bytes 582920 | tf_op jit(solution)/shard_map/ppermute | solution.py:294
  68.4 7.4 %collective-permute-start.22 = (f32[48,1104]{1,0:T(8,128)S(1)}, f32[48,1104]{1,0:T(8,128)S(1)}, u32[]{:S(2)}, u32[]{:S(2)}) collective-permute-start(f32[48,1104]{1,0:T(8,128)S(1)} %get-tuple-element.27), channel_id=1, source_target_pairs={{0,8},{8,16},{16,24},{24,0},{1,9},{9,17},{17,25},{25,1},{2,10},{10... | collective-permute-start | bytes 635912 | tf_op jit(solution)/shard_map/ppermute | solution.py:294
  70.0 9.9 %collective-permute-start.24 = (f32[44,1104]{1,0:T(8,128)S(1)}, f32[44,1104]{1,0:T(8,128)S(1)}, u32[]{:S(2)}, u32[]{:S(2)}) collective-permute-start(f32[44,1104]{1,0:T(8,128)S(1)} %get-tuple-element.28), channel_id=1, source_target_pairs={{0,8},{8,16},{16,24},{24,0},{1,9},{9,17},{17,25},{25,1},{2,10},{10... | collective-permute-start | bytes 582920 | tf_op jit(solution)/shard_map/ppermute | solution.py:294
  73.9 7.2 %collective-permute-start.26 = (f32[44,1104]{1,0:T(8,128)S(1)}, f32[44,1104]{1,0:T(8,128)S(1)}, u32[]{:S(2)}, u32[]{:S(2)}) collective-permute-start(f32[44,1104]{1,0:T(8,128)S(1)} %add.28), channel_id=1, source_target_pairs={{0,24},{8,0},{16,8},{24,16},{1,25},{9,1},{17,9},{25,17},{2,26},{10... | collective-permute-start | bytes 582920 | tf_op jit(solution)/shard_map/ppermute | solution.py:294
  75.1 8.4 %collective-permute-start.21 = (f32[48,1104]{1,0:T(8,128)S(1)}, f32[48,1104]{1,0:T(8,128)S(1)}, u32[]{:S(2)}, u32[]{:S(2)}) collective-permute-start(f32[48,1104]{1,0:T(8,128)S(1)} %get-tuple-element.25), channel_id=1, source_target_pairs={{0,24},{8,0},{16,8},{24,16},{1,25},{9,1},{17,9},{25,17},{2,26},{10... | collective-permute-start | bytes 635912 | tf_op jit(solution)/shard_map/ppermute | solution.py:294
  75.8 7.6 %collective-permute-start.23 = (f32[48,1104]{1,0:T(8,128)S(1)}, f32[48,1104]{1,0:T(8,128)S(1)}, u32[]{:S(2)}, u32[]{:S(2)}) collective-permute-start(f32[48,1104]{1,0:T(8,128)S(1)} %add.25), channel_id=1, source_target_pairs={{0,8},{8,16},{16,24},{24,0},{1,9},{9,17},{17,25},{25,1},{2,10},{10... | collective-permute-start | bytes 635912 | tf_op jit(solution)/shard_map/ppermute | solution.py:294
  83.5 11.8 %collective-permute-start.27 = (bf16[92,1104]{1,0:T(8,128)(2,1)S(1)}, bf16[92,1104]{1,0:T(8,128)(2,1)S(1)}, u32[]{:S(2)}, u32[]{:S(2)}) collective-permute-start(bf16[92,1104]{1,0:T(8,128)(2,1)S(1)} %pad_maximum_fusion), channel_id=1, source_target_pairs={{0,0},{1,9},{2,18},{3,27},{4,4},{5,13},{6,22},{7,31},{8,1},{9,8},{... | collective-permute-start | bytes 609416 | tf_op jit(solution)/shard_map/ppermute | solution.py:331

commit v5 on v4

--- a/solution.py
+++ b/solution.py
@@ -1,3 +1,5 @@
+import functools
+
 import jax
 import jax.numpy as jnp
 from jax import lax
@@ -74,8 +76,18 @@
     )(left_values[:, 0])
 
 
-def pack_right_kernel(meta_ref, right_ref, right_cols_ref, left_cols_ref, *refs):
-    outs, (flat_ref, code_ref, tmp_ref) = refs[:TILES], refs[TILES:]
+def pack_right_kernel(meta_ref, right_in, right_cols_in, left_cols_in, *refs):
+    outs, (flat_ref, code_ref, tmp_ref, right_ref, right_cols_ref, left_cols_ref, sems) = refs[:TILES], refs[TILES:]
+    copies = [
+        pltpu.make_async_copy(a, b, sems.at[n])
+        for n, (a, b) in enumerate(
+            ((right_in, right_ref), (right_cols_in, right_cols_ref), (left_cols_in, left_cols_ref))
+        )
+    ]
+    for copy in copies:
+        copy.start()
+    for copy in copies:
+        copy.wait()
     for k in range(HERE):
         for u in range(USLOTS):
             n = (k * USLOTS + u) * 8
@@ -106,7 +118,7 @@
                 z = z + pltpu.roll(jnp.broadcast_to(line, (8, LANES)), 16 + ROWS * h, 1)
         tmp_ref[u, pl.ds(BLK, 8, stride=APAD), :] = z
     for t in range(TILES):
-        tile = (meta_ref[0] + t) % TILES
+        tile = lax.bitwise_xor((meta_ref[0] + t) & 3, 3 * lax.shift_right_logical(meta_ref[0], 2))
         for u in range(USLOTS):
             rows = tmp_ref[u, pl.ds(pl.multiple_of(tile * APAD, 8), APAD), :]
             outs[t][u] = rows.astype(jnp.bfloat16)
@@ -117,14 +129,17 @@
     return pl.pallas_call(
         pack_right_kernel,
         out_shape=(jax.ShapeDtypeStruct((USLOTS, APAD, LANES), jnp.bfloat16),) * TILES,
-        in_specs=[pl.BlockSpec(memory_space=pltpu.SMEM)] + [vmem] * 3,
+        in_specs=[pl.BlockSpec(memory_space=pltpu.SMEM)] + [pl.BlockSpec(memory_space=pl.ANY)] * 3,
         out_specs=(vmem,) * TILES,
         scratch_shapes=[
             pltpu.VMEM((HERE * USLOTS * 8, 5 * LANES), jnp.float32),
             pltpu.VMEM((8, LANES), jnp.float32),
             pltpu.VMEM((USLOTS, 8 * APAD, LANES), jnp.float32),
+            pltpu.VMEM((HERE, USLOTS, TILES, BLK * BLK), jnp.bfloat16),
+            pltpu.VMEM((USLOTS, TILES, HERE), jnp.int32),
+            pltpu.VMEM((SLOTS, ROWS), jnp.int32),
+            pltpu.SemaphoreType.DMA((3,)),
         ],
-        compiler_params=pltpu.CompilerParams(vmem_limit_bytes=8 * 1024 * 1024),
     )(
         meta,
         jnp.transpose(right_values[0], (0, 2, 1, 3)),
@@ -148,8 +163,8 @@
     codes = jnp.concatenate(
         [mixed_ref[h * LANES : (h + 1) * LANES, :].T[0:8, :] for h in range(2)], axis=1
     ).astype(jnp.int32)
-    local = codes - 16 * lax.shift_right_arithmetic(depth, 2)
-    chunk = lax.bitwise_xor(lax.shift_right_arithmetic(local, 2), depth & 3)
+    local = codes - 16 * lax.shift_right_logical(depth, 2)
+    chunk = lax.bitwise_xor(lax.shift_right_arithmetic(local, 2), lax.bitwise_xor(depth, 7 * (depth >> 2)) & 3)
     at = CHUNK * ((chunk - col) & 3) + BLK * (local & 3)
     at = jnp.where((local >= 0) & (local < 16), at, 4 * LANES)
     turned_ref[0:8, :] = at
@@ -166,9 +181,9 @@
         x = side + jnp.where(j == 1, 3, j - lax.shift_right_logical(j, 1))
         row = 2 * (x & 3) + lax.bitwise_xor(core, lax.shift_right_logical(n, 5))
         spot = n & 7
-        panel = lax.bitwise_xor(lax.shift_right_logical(depth, 2), lax.shift_right_logical(spot, 2)) * 4 + (
-            (depth - spot) & 3
-        )
+        other = lax.shift_right_logical(spot, 2)
+        quad = lax.bitwise_xor(lax.shift_right_logical(depth, 2), other)
+        panel = quad * 4 + ((lax.bitwise_xor(depth, 3 * other) - spot) & 3)
         base = panel * PANEL + row * HERE
         first = n * USLOTS
         blocks = [right_ref[n, u].astype(jnp.float32) for u in range(USLOTS)]
@@ -215,79 +230,77 @@
     at = []
     for o in offsets:
         panel = (depth + o) & 7
-        line = lax.bitwise_xor(lax.shift_right_logical(panel, 2), lax.shift_right_logical(depth, 2)) * 4 + (
-            (depth - panel) & 3
-        )
+        other = lax.shift_right_logical(lax.bitwise_xor(panel, depth), 2)
+        line = other * 4 + ((lax.bitwise_xor(depth, 3 * other) - panel) & 3)
         for s in range(SLOTS):
             at.append(panel * PANEL + table_ref[line * USLOTS + s // 2, 16 + ROWS * (s % 2) + i])
     return jnp.concatenate([jnp.concatenate([wide_ref[n, q] for n in at], axis=0) for q in range(3)], axis=1)
 
 
-def early_kernel(meta_ref, table_ref, wide_ref, *refs):
-    lefts, out_ref = refs[:4], refs[4]
-
-    def step(g, carry):
-        for m in range(8):
-            i = g * 8 + m
-            weights = picked(meta_ref, table_ref, wide_ref, OFFSETS[:4], i)
-            rows = jnp.concatenate([x[i] for x in lefts], axis=1)
-            out_ref[i] = jnp.dot(rows, weights, preferred_element_type=jnp.float32)
-        return carry
-
-    lax.fori_loop(0, ROWS // 8, step, 0)
-
-
-def late_kernel(meta_ref, table_ref, wide_ref, early_ref, *refs):
-    lefts, outs, (far_ref, sum_ref, part_ref) = refs[:5], refs[5:12], refs[12:]
-    half = ROWS // 2
-    far_ref[:half] = lefts[3][...]
-    far_ref[half:] = lefts[4][...]
-    lefts = (*lefts[:3], far_ref)
-
-    def step(g, carry):
-        for m in range(8):
-            i = g * 8 + m
-            weights = picked(meta_ref, table_ref, wide_ref, OFFSETS[4:], i)
-            rows = jnp.concatenate([x[i] for x in lefts], axis=1)
-            total = early_ref[i] + jnp.dot(rows, weights, preferred_element_type=jnp.float32)
-            part_ref[m * BLK : m * BLK + APAD, :] = total
-        sum_ref[pl.ds(pl.multiple_of(g * 8 * BLK, 8), 8 * BLK), :] = part_ref[0 : 8 * BLK, :]
-        return carry
-
-    lax.fori_loop(0, ROWS // 8, step, 0)
+def product_kernel(start, count, meta_ref, table_ref, wide_ref, *refs):
+    lefts, outs, (sum_ref, part_ref) = refs[:9], refs[9:16], refs[16:]
+
+    def steps(first, last, far_ref, skip):
+        def step(g, carry):
+            for m in range(8):
+                i = g * 8 + m
+                weights = picked(meta_ref, table_ref, wide_ref, OFFSETS, i)
+                rows = jnp.concatenate([x[i] for x in lefts[:7]] + [far_ref[i - skip]], axis=1)
+                part_ref[m * BLK : m * BLK + APAD, :] = jnp.dot(rows, weights, preferred_element_type=jnp.float32)
+            at = pl.multiple_of((g - start) * 8 * BLK, 8)
+            sum_ref[pl.ds(at, 8 * BLK), :] = part_ref[0 : 8 * BLK, :]
+            return carry
+
+        lax.fori_loop(first, last, step, 0)
+
+    if start < 3:
+        steps(start, min(3, start + count), lefts[7], 0)
+    if start + count > 3:
+        steps(max(3, start), start + count, lefts[8], ROWS // 2)
+    width = count * 8 * BLK
     for q in range(3):
-        turned = sum_ref[0:1152, q * LANES : (q + 1) * LANES].T[:, : ROWS * BLK]
+        turned = sum_ref[:, q * LANES : (q + 1) * LANES].T[:, :width]
         for ref, (first, last) in zip(outs, SPANS):
             low, high = max(first, q * LANES), min(last, (q + 1) * LANES)
             if low < high:
                 ref[low - first : high - first, :] = turned[low - q * LANES : high - q * LANES]
 
 
-def product(meta, table, wide, lefts):
+def product(meta, table, wide, lefts, start, count):
     vmem = pl.BlockSpec(memory_space=pltpu.VMEM)
     smem = pl.BlockSpec(memory_space=pltpu.SMEM)
-    cost = pl.CostEstimate(flops=3_000_000_000, bytes_accessed=4_000_000, transcendentals=0)
-    early = pl.pallas_call(
-        early_kernel,
-        out_shape=jax.ShapeDtypeStruct((ROWS, APAD, WIDE), jnp.float32),
-        in_specs=[smem, smem, vmem] + [vmem] * 4,
-        out_specs=vmem,
-        compiler_params=pltpu.CompilerParams(vmem_limit_bytes=8 * 1024 * 1024),
-        cost_estimate=cost,
-    )(meta, table, wide, *lefts[:4])
+    width = count * 8 * BLK
     return pl.pallas_call(
-        late_kernel,
-        out_shape=tuple(jax.ShapeDtypeStruct((b - a, ROWS * BLK), jnp.float32) for a, b in SPANS),
-        in_specs=[smem, smem, vmem, vmem] + [vmem] * 5,
+        functools.partial(product_kernel, start, count),
+        out_shape=tuple(jax.ShapeDtypeStruct((b - a, width), jnp.float32) for a, b in SPANS),
+        in_specs=[smem, smem, vmem] + [vmem] * len(lefts),
         out_specs=(vmem,) * len(SPANS),
         scratch_shapes=[
-            pltpu.VMEM((ROWS, APAD, LANES), jnp.bfloat16),
-            pltpu.VMEM((1152, WIDE), jnp.float32),
+            pltpu.VMEM((-(-width // LANES) * LANES, WIDE), jnp.float32),
             pltpu.VMEM((8 * APAD, WIDE), jnp.float32),
         ],
-        compiler_params=pltpu.CompilerParams(vmem_limit_bytes=12 * 1024 * 1024),
-        cost_estimate=cost,
-    )(meta, table, wide, early, *lefts[4:])
+        compiler_params=pltpu.CompilerParams(vmem_limit_bytes=8 * 1024 * 1024),
+        cost_estimate=pl.CostEstimate(flops=count * 1_000_000_000, bytes_accessed=8_000_000, transcendentals=0),
+    )(meta, table, wide, *lefts)
+
+
+def summed(parts):
+    own, ahead_low, ahead_high, far_low, far_high, behind_low, behind_high = parts
+    far_low = shift(far_low, "col", 1, 4)
+    far_high = shift(far_high, "col", -1, 4)
+    ahead_high = shift(ahead_high, "col", 1, 4)
+    behind_low = shift(behind_low, "col", -1, 4)
+    ahead_low = shift(ahead_low + far_low, "col", 1, 4)
+    behind_high = shift(behind_high + far_high, "col", -1, 4)
+    low = own[:48] + behind_low + ahead_low
+    high = own[48:] + ahead_high + behind_high
+    done = jnp.concatenate([low.astype(jnp.bfloat16), high.astype(jnp.bfloat16)], axis=0)
+    home = []
+    for y in range(4):
+        for z in range(8):
+            tile = min(z, 7 - z)
+            home.append((y * 8 + z, tile * 8 + z // 4 * 4 + (y ^ tile)))
+    return lax.ppermute(done, ("col", "depth"), home)
 
 
 def shift(x, axis, by, n):
@@ -304,7 +317,7 @@
     ]
     up1, down1 = shift(left, "depth", 1, 8), shift(left, "depth", -1, 8)
     half = jnp.stack(near, axis=0)
-    other = shift(half, "depth", 4, 8)
+    other = lax.ppermute(half, "depth", [(z, 7 - z) for z in range(8)])
     right = jnp.concatenate([half, other], axis=0)
     swap = [(i, i ^ 1) for i in range(8)]
     f1, b1 = shift(right, "row", 2, 8), shift(right, "row", -2, 8)
@@ -317,18 +330,10 @@
     up4, down4 = shift(up3[:edge], "depth", 1, 8), shift(down3[edge:], "depth", -1, 8)
     lefts = [left, up1, down1, up2, down2, up3, down3, up4, down4]
     wide, table = fill(meta, [right, f1, b1, f2, b2] + others)
-    own, ahead_low, ahead_high, far_low, far_high, behind_low, behind_high = product(meta, table, wide, lefts)
-    far_low = shift(far_low, "col", 1, 4)
-    far_high = shift(far_high, "col", -1, 4)
-    ahead_high = shift(ahead_high, "col", 1, 4)
-    behind_low = shift(behind_low, "col", -1, 4)
-    ahead_low = shift(ahead_low + far_low, "col", 1, 4)
-    behind_high = shift(behind_high + far_high, "col", -1, 4)
-    low = own[:48] + behind_low + ahead_low
-    high = own[48:] + ahead_high + behind_high
-    done = jnp.concatenate([low.astype(jnp.bfloat16), high.astype(jnp.bfloat16)], axis=0)
-    home = [(y * 8 + z, (z % 4) * 8 + (z // 4) * 4 + (y ^ (z % 4))) for y in range(4) for z in range(8)]
-    return lax.ppermute(done, ("col", "depth"), home).T
+    first = product(meta, table, wide, lefts, 0, 4)
+    second = product(meta, table, wide, lefts, 4, 2)
+    done = [summed(first), summed(second)]
+    return jnp.concatenate(done, axis=1).T
 
 
 def solution(mesh):

time: 96.3 us -> 96.5 us (level); the launches traced: 96 us -> 94.6 us
  waiting for transfers between devices: 30.7 us -> 19.9 us
  starting transfers between devices: 44.4 us -> 52.9 us
  other arithmetic: 0.27 us -> 2.26 us
  local copies, waits for them, and re-layouts: 3.98 us -> 2.32 us
    ppermute x1 -> x3, starting transfers between devices: 3.04 us -> 10.5 us  [the longest x2 5.96 us: summed(): return lax.ppermute(done, ('col', 'depth'), home)]
    ppermute x19 -> x24, waiting for transfers between devices: 19.4 us -> 12.7 us  [shift(): return lax.ppermute(x, axis, [(i, (i + by) % n) for i in range(n)])]
    ppermute x1 -> x3, waiting for transfers between devices: 8.8 us -> 5.22 us  [the longest x2 4.98 us: summed(): return lax.ppermute(done, ('col', 'depth'), home)]
    unnamed x13 -> x8, local copies, waits for them, and re-layouts: 3.92 us -> 2.26 us
    pallas_call x1, Pallas kernels: 1.05 us -> 2.7 us  [pack_right(): pl.pallas_call(pack_right_kernel, out_shape=(jax.ShapeDtypeStruct((USLOTS...]
    pallas_call x2, Pallas kernels: 9.37 us -> 8.22 us  [product(): pl.pallas_call(functools.partial(product_kernel, start, count), out_shape...]
    ppermute x19 -> x24, starting transfers between devices: 36.8 us -> 37.8 us  [shift(): return lax.ppermute(x, axis, [(i, (i + by) % n) for i in range(n)])]
  transfers between devices with their start and end apart: 28 -> 35, of which waited for: 13 -> 11; matrix products, arithmetic and copies ran while one was open for 0% -> 2% of each run, Pallas kernels for 11% -> 12%
where the time goes in v5:
time: 96.5 us; the launch traced here: 94.6 us
  starting transfers between devices  52.9 us (55%)
  waiting for transfers between devices  19.9 us (21%)
  Pallas kernels  17 us (18%)
  local copies, waits for them, and re-layouts  2.32 us (2%)
  other arithmetic  2.26 us (2%)
    ppermute x24, starting transfers between devices, shift(): return lax.ppermute(x, axis, [(i, (i + by) % n) for i in range(n)])  37.8 us
    ppermute x24, waiting for transfers between devices, shift(): return lax.ppermute(x, axis, [(i, (i + by) % n) for i in range(n)])  12.7 us
    pallas_call x2, Pallas kernels, product(): pl.pallas_call(functools.partial(product_kernel, start, count), out_shape...  8.22 us
    ppermute x2, starting transfers between devices, summed(): return lax.ppermute(done, ('col', 'depth'), home)  5.96 us
    pallas_call x1, Pallas kernels, fill(): pl.pallas_call(fill_kernel, out_shape=(jax.ShapeDtypeStruct((GROUP * PANE...  5.59 us
    ppermute x2, waiting for transfers between devices, summed(): return lax.ppermute(done, ('col', 'depth'), home)  4.98 us
    ppermute x1, starting transfers between devices, body(): other = lax.ppermute(half, 'depth', [(z, 7 - z) for z in range(8)])  4.56 us
    ppermute x3, starting transfers between devices, body(): lax.ppermute(tiles[k], 'depth', [(z, z // 4 * 4 + (z + k) % 4) for z in r...  3.9 us
  transfers between devices with their start and end apart: 35, of which 11 were waited for; matrix products, arithmetic and copies ran while one was open for 2% of the time, Pallas kernels for 12%

profile of v5, /device:TPU:16, one launch (start us, length us, event | category | flops | bytes accessed | tf_op | source)
XLA Modules:
  0.0 94.6 jit_solution(5388918123975662070)
XLA Ops:
  0.0 0.9 copy-done
  0.9 0.5 shard_map.48.refs_0_
  1.5 2.0 %collective-permute-start.13 = (bf16[48,24,128]{2,1,0:T(8,128)(2,1)S(1)}, bf16[48,24,128]{2,1,0:T(8,128)(2,1)S(1)}, u32[]{:S(2)}, u32[]{:S(2)}) collective-permute-start(bf16[48,24,128]{2,1,0:T(8,128)(2,1)S(1)} %shard_map.48.refs_0_), channel_id=1, source_target_pairs={{0,1},{1,2},{2,3},{3,4},{4,5},{5,6},{6,7},{7,0},{8,9},{9,10},{10,1... | collective-permute-start | bytes 884744 | tf_op jit(solution)/shard_map/ppermute | solution.py:307
  3.4 4.0 %collective-permute-start.14 = (bf16[48,24,128]{2,1,0:T(8,128)(2,1)S(1)}, bf16[48,24,128]{2,1,0:T(8,128)(2,1)S(1)}, u32[]{:S(2)}, u32[]{:S(2)}) collective-permute-start(bf16[48,24,128]{2,1,0:T(8,128)(2,1)S(1)} %shard_map.48.refs_0_), channel_id=1, source_target_pairs={{0,7},{1,0},{2,1},{3,2},{4,3},{5,4},{6,5},{7,6},{8,15},{9,8},{10,9... | collective-permute-start | bytes 884744 | tf_op jit(solution)/shard_map/ppermute | solution.py:307
  7.5 0.6 pad_add_fusion.meta_ref
  8.0 2.7 %shard_map.46 = (bf16[3,24,128]{2,1,0:T(8,128)(2,1)}, bf16[3,24,128]{2,1,0:T(8,128)(2,1)}, bf16[3,24,128]{2,1,0:T(8,128)(2,1)}, bf16[3,24,128]{2,1,0:T(8,128)(2,1)}) custom-call(s32[4]{0:T(128)} %pad_add_fusion.meta_ref, bf16[5,3,4,529]{3,2,1,0:T(4,128)(2,1)} %bitcast.25, s32[3,4,5]{2,1,0:T(4,128)} %bitcast.30, s32[4,48]{1,0:T(4,128)} %bitcast.31), custom_call_target="tpu_custom_call" | custom-call | tf_op jit(solution)/shard_map/pallas_call | solution.py:129
  10.8 2.4 %collective-permute-start.1 = (bf16[3,24,128]{2,1,0:T(8,128)(2,1)}, bf16[3,24,128]{2,1,0:T(8,128)(2,1)S(1)}, u32[]{:S(2)}, u32[]{:S(2)}) collective-permute-start(bf16[3,24,128]{2,1,0:T(8,128)(2,1)} %get-tuple-element.27), channel_id=1, source_target_pairs={{0,2},{1,3},{2,0},{3,1},{4,6},{5,7},{6,4},{7,5},{8,10},{9,11},{10,... | collective-permute-start | bytes 55304 | tf_op jit(solution)/shard_map/ppermute | solution.py:316
  13.2 1.5 %collective-permute-start.2 = (bf16[3,24,128]{2,1,0:T(8,128)(2,1)}, bf16[3,24,128]{2,1,0:T(8,128)(2,1)S(1)}, u32[]{:S(2)}, u32[]{:S(2)}) collective-permute-start(bf16[3,24,128]{2,1,0:T(8,128)(2,1)} %get-tuple-element.28), channel_id=1, source_target_pairs={{0,3},{1,0},{2,1},{3,2},{4,7},{5,4},{6,5},{7,6},{8,11},{9,8},{10,9... | collective-permute-start | bytes 55304 | tf_op jit(solution)/shard_map/ppermute | solution.py:316
  14.6 0.7 constant_dynamic-update-slice_fusion.4
  15.4 1.5 %collective-permute-done = bf16[3,24,128]{2,1,0:T(8,128)(2,1)S(1)} collective-permute-done((bf16[3,24,128]{2,1,0:T(8,128)(2,1)}, bf16[3,24,128]{2,1,0:T(8,128)(2,1)S(1)}, u32[]{:S(2)}, u32[]{:S(2)}) %collective-permute-start) | collective-permute-done | bytes 18464 | tf_op jit(solution)/shard_map/ppermute | solution.py:316
  16.8 0.3 collective-permute-done.2
  17.2 0.7 pad_maximum_fusion.1
  17.9 4.6 %collective-permute-start.3 = (bf16[4,3,24,128]{3,2,1,0:T(8,128)(2,1)S(1)}, bf16[4,3,24,128]{3,2,1,0:T(8,128)(2,1)S(1)}, u32[]{:S(2)}, u32[]{:S(2)}) collective-permute-start(bf16[4,3,24,128]{3,2,1,0:T(8,128)(2,1)S(1)} %pad_maximum_fusion.1), channel_id=1, source_target_pairs={{0,7},{1,6},{2,5},{3,4},{4,3},{5,2},{6,1},{7,0},{8,15},{9,14},{10,... | collective-permute-start | bytes 221192 | tf_op jit(solution)/shard_map/ppermute | solution.py:320
  22.5 0.4 collective-permute-start.15
  22.9 2.9 %collective-permute-start.16 = (bf16[48,24,128]{2,1,0:T(8,128)(2,1)S(1)}, bf16[48,24,128]{2,1,0:T(8,128)(2,1)S(1)}, u32[]{:S(2)}, u32[]{:S(2)}) collective-permute-start(bf16[48,24,128]{2,1,0:T(8,128)(2,1)S(1)} %collective-permute-done.14.refs_2_), channel_id=1, source_target_pairs={{0,7},{1,0},{2,1},{3,2},{4,3},{5,4},{6,5},{7,6},{8,15},{9,8},{10,9... | collective-permute-start | bytes 884744 | tf_op jit(solution)/shard_map/ppermute | solution.py:307
  25.8 0.2 collective-permute-done.3
  26.1 1.6 %collective-permute-start.4 = (bf16[8,3,24,128]{3,2,1,0:T(8,128)(2,1)S(1)}, bf16[8,3,24,128]{3,2,1,0:T(8,128)(2,1)S(1)}, u32[]{:S(2)}, u32[]{:S(2)}) collective-permute-start(bf16[8,3,24,128]{3,2,1,0:T(8,128)(2,1)S(1)} %constant_dynamic-update-slice_fusion.refs_0_), channel_id=1, source_target_pairs={{0,64},{32,96},{64,128},{96,160},{128,192},{160,224},{192,0},{224,... | collective-permute-start | bytes 442376 | tf_op jit(solution)/shard_map/ppermute | solution.py:307
  27.6 1.7 %collective-permute-start.5 = (bf16[8,3,24,128]{3,2,1,0:T(8,128)(2,1)S(1)}, bf16[8,3,24,128]{3,2,1,0:T(8,128)(2,1)S(1)}, u32[]{:S(2)}, u32[]{:S(2)}) collective-permute-start(bf16[8,3,24,128]{3,2,1,0:T(8,128)(2,1)S(1)} %constant_dynamic-update-slice_fusion.refs_0_), channel_id=1, source_target_pairs={{0,192},{32,224},{64,0},{96,32},{128,64},{160,96},{192,128},{224,1... | collective-permute-start | bytes 442376 | tf_op jit(solution)/shard_map/ppermute | solution.py:307
  29.4 2.5 %collective-permute-done.15.refs_3_ = bf16[48,24,128]{2,1,0:T(8,128)(2,1)S(1)} collective-permute-done((bf16[48,24,128]{2,1,0:T(8,128)(2,1)S(1)}, bf16[48,24,128]{2,1,0:T(8,128)(2,1)S(1)}, u32[]{:S(2)}, u32[]{:S(2)}) %collective-permute-start.15) | collective-permute-done | bytes 294944 | tf_op jit(solution)/shard_map/ppermute | solution.py:307
  31.8 3.2 %collective-permute-start.18 = (bf16[48,24,128]{2,1,0:T(8,128)(2,1)S(1)}, bf16[48,24,128]{2,1,0:T(8,128)(2,1)S(1)}, u32[]{:S(2)}, u32[]{:S(2)}) collective-permute-start(bf16[48,24,128]{2,1,0:T(8,128)(2,1)S(1)} %collective-permute-done.16.refs_4_), channel_id=1, source_target_pairs={{0,7},{1,0},{2,1},{3,2},{4,3},{5,4},{6,5},{7,6},{8,15},{9,8},{10,9... | collective-permute-start | bytes 884744 | tf_op jit(solution)/shard_map/ppermute | solution.py:307
  35.1 1.6 %collective-permute-start.6 = (bf16[4,3,24,128]{3,2,1,0:T(8,128)(2,1)S(1)}, bf16[4,3,24,128]{3,2,1,0:T(8,128)(2,1)S(1)}, u32[]{:S(2)}, u32[]{:S(2)}) collective-permute-start(bf16[4,3,24,128]{3,2,1,0:T(8,128)(2,1)S(1)} %slice.32), channel_id=1, source_target_pairs={{0,64},{32,96},{64,128},{96,160},{128,192},{160,224},{192,0},{224,... | collective-permute-start | bytes 221192 | tf_op jit(solution)/shard_map/ppermute | solution.py:307
  36.7 1.8 %collective-permute-start.7 = (bf16[4,3,24,128]{3,2,1,0:T(8,128)(2,1)S(1)}, bf16[4,3,24,128]{3,2,1,0:T(8,128)(2,1)S(1)}, u32[]{:S(2)}, u32[]{:S(2)}) collective-permute-start(bf16[4,3,24,128]{3,2,1,0:T(8,128)(2,1)S(1)} %slice.33), channel_id=1, source_target_pairs={{0,192},{32,224},{64,0},{96,32},{128,64},{160,96},{192,128},{224,1... | collective-permute-start | bytes 221192 | tf_op jit(solution)/shard_map/ppermute | solution.py:307
  38.5 2.2 %collective-permute-done.6.refs_3_ = bf16[4,3,24,128]{3,2,1,0:T(8,128)(2,1)S(1)} collective-permute-done((bf16[4,3,24,128]{3,2,1,0:T(8,128)(2,1)S(1)}, bf16[4,3,24,128]{3,2,1,0:T(8,128)(2,1)S(1)}, u32[]{:S(2)}, u32[]{:S(2)}) %collective-permute-start.6) | collective-permute-done | bytes 73760 | tf_op jit(solution)/shard_map/ppermute | solution.py:307
  40.7 0.4 collective-permute-done.7.refs_4_
  41.2 0.4 collective-permute-start.11
  41.9 0.2 collective-permute-done.9.refs_6_
  42.1 3.0 %collective-permute-start.20 = (bf16[24,24,128]{2,1,0:T(8,128)(2,1)S(1)}, bf16[24,24,128]{2,1,0:T(8,128)(2,1)S(1)}, u32[]{:S(2)}, u32[]{:S(2)}) collective-permute-start(bf16[24,24,128]{2,1,0:T(8,128)(2,1)S(1)} %slice.35), channel_id=1, source_target_pairs={{0,7},{1,0},{2,1},{3,2},{4,3},{5,4},{6,5},{7,6},{8,15},{9,8},{10,9... | collective-permute-start | bytes 442376 | tf_op jit(solution)/shard_map/ppermute | solution.py:307
  45.2 0.6 copy-done.1
  45.7 5.6 %shard_map.47 = (bf16[320,3,32,128]{3,2,1,0:T(8,128)(2,1)S(1)}, s32[24,128]{1,0:T(8,128)S(1)}) custom-call(s32[4]{0:T(128)S(1)} %copy-done.1, bf16[8,3,24,128]{3,2,1,0:T(8,128)(2,1)S(1)} %constant_dynamic-update-slice_fusion.refs_0_, bf16[8,3,24,128]{3,2,1,0:T(8,128)(2,1)S(1)} %collective-permute-done.4.refs_1_, ...), custom_call_target="tpu_custom_call" | custom-call | flops 3000000000 | bytes 8000000 | tf_op jit(solution)/shard_map/pallas_call | solution.py:208
  51.3 5.1 %shard_map.49 = (f32[92,736]{1,0:T(8,128)S(1)}, f32[48,736]{1,0:T(8,128)S(1)}, f32[44,736]{1,0:T(8,128)S(1)}, f32[48,736]{1,0:T(8,128)S(1)}, f32[44,736]{1,0:T(8...) custom-call(s32[4]{0:T(128)S(1)} %copy-done.1, s32[24,128]{1,0:T(8,128)S(1)} %get-tuple-element.29.table_ref, ...), custom_call_target="tpu_custom_call" | custom-call | flops 4000000000 | bytes 8000000 | tf_op jit(solution)/shard_map/pallas_call | solution.py:273
  56.5 0.5 collective-permute-start.25
  57.0 3.1 %shard_map.50 = (f32[92,368]{1,0:T(8,128)S(1)}, f32[48,368]{1,0:T(8,128)S(1)}, f32[44,368]{1,0:T(8,128)S(1)}, f32[48,368]{1,0:T(8,128)S(1)}, f32[44,368]{1,0:T(8...) custom-call(s32[4]{0:T(128)S(1)} %copy-done.1, s32[24,128]{1,0:T(8,128)S(1)} %get-tuple-element.29.table_ref, ...), custom_call_target="tpu_custom_call" | custom-call | flops 2000000000 | bytes 8000000 | tf_op jit(solution)/shard_map/pallas_call | solution.py:273
  60.1 0.5 collective-permute-start.32
  60.6 1.6 %collective-permute-start.29 = (f32[48,368]{1,0:T(8,128)S(1)}, f32[48,368]{1,0:T(8,128)S(1)}, u32[]{:S(2)}, u32[]{:S(2)}) collective-permute-start(f32[48,368]{1,0:T(8,128)S(1)} %get-tuple-element.41), channel_id=1, source_target_pairs={{0,8},{8,16},{16,24},{24,0},{1,9},{9,17},{17,25},{25,1},{2,10},{10... | collective-permute-start | bytes 211976 | tf_op jit(solution)/shard_map/ppermute | solution.py:307
  62.2 2.8 %collective-permute-start.31 = (f32[44,368]{1,0:T(8,128)S(1)}, f32[44,368]{1,0:T(8,128)S(1)}, u32[]{:S(2)}, u32[]{:S(2)}) collective-permute-start(f32[44,368]{1,0:T(8,128)S(1)} %get-tuple-element.42), channel_id=1, source_target_pairs={{0,8},{8,16},{16,24},{24,0},{1,9},{9,17},{17,25},{25,1},{2,10},{10... | collective-permute-start | bytes 194312 | tf_op jit(solution)/shard_map/ppermute | solution.py:307
  65.0 0.7 collective-permute-start.33
  65.7 2.4 %collective-permute-start.28 = (f32[48,368]{1,0:T(8,128)S(1)}, f32[48,368]{1,0:T(8,128)S(1)}, u32[]{:S(2)}, u32[]{:S(2)}) collective-permute-start(f32[48,368]{1,0:T(8,128)S(1)} %get-tuple-element.39), channel_id=1, source_target_pairs={{0,24},{8,0},{16,8},{24,16},{1,25},{9,1},{17,9},{25,17},{2,26},{10... | collective-permute-start | bytes 211976 | tf_op jit(solution)/shard_map/ppermute | solution.py:307
  68.1 2.7 %collective-permute-start.22 = (f32[48,736]{1,0:T(8,128)S(1)}, f32[48,736]{1,0:T(8,128)S(1)}, u32[]{:S(2)}, u32[]{:S(2)}) collective-permute-start(f32[48,736]{1,0:T(8,128)S(1)} %get-tuple-element.34), channel_id=1, source_target_pairs={{0,8},{8,16},{16,24},{24,0},{1,9},{9,17},{17,25},{25,1},{2,10},{10... | collective-permute-start | bytes 423944 | tf_op jit(solution)/shard_map/ppermute | solution.py:307
  71.0 2.0 %collective-permute-start.30 = (f32[48,368]{1,0:T(8,128)S(1)}, f32[48,368]{1,0:T(8,128)S(1)}, u32[]{:S(2)}, u32[]{:S(2)}) collective-permute-start(f32[48,368]{1,0:T(8,128)S(1)} %add.49), channel_id=1, source_target_pairs={{0,8},{8,16},{16,24},{24,0},{1,9},{9,17},{17,25},{25,1},{2,10},{10... | collective-permute-start | bytes 211976 | tf_op jit(solution)/shard_map/ppermute | solution.py:307
  73.0 2.8 %collective-permute-done.22 = f32[48,736]{1,0:T(8,128)S(1)} collective-permute-done((f32[48,736]{1,0:T(8,128)S(1)}, f32[48,736]{1,0:T(8,128)S(1)}, u32[]{:S(2)}, u32[]{:S(2)}) %collective-permute-start.22) | collective-permute-done | bytes 141344 | tf_op jit(solution)/shard_map/ppermute | solution.py:307
  75.8 1.7 %collective-permute-start.26 = (f32[44,736]{1,0:T(8,128)S(1)}, f32[44,736]{1,0:T(8,128)S(1)}, u32[]{:S(2)}, u32[]{:S(2)}) collective-permute-start(f32[44,736]{1,0:T(8,128)S(1)} %add.46), channel_id=1, source_target_pairs={{0,24},{8,0},{16,8},{24,16},{1,25},{9,1},{17,9},{25,17},{2,26},{10... | collective-permute-start | bytes 388616 | tf_op jit(solution)/shard_map/ppermute | solution.py:307
  77.6 0.4 collective-permute-start.23
  78.0 3.0 %collective-permute-done.26 = f32[44,736]{1,0:T(8,128)S(1)} collective-permute-done((f32[44,736]{1,0:T(8,128)S(1)}, f32[44,736]{1,0:T(8,128)S(1)}, u32[]{:S(2)}, u32[]{:S(2)}) %collective-permute-start.26) | collective-permute-done | bytes 129568 | tf_op jit(solution)/shard_map/ppermute | solution.py:307
  81.0 1.8 %collective-permute-done.23 = f32[48,736]{1,0:T(8,128)S(1)} collective-permute-done((f32[48,736]{1,0:T(8,128)S(1)}, f32[48,736]{1,0:T(8,128)S(1)}, u32[]{:S(2)}, u32[]{:S(2)}) %collective-permute-start.23) | collective-permute-done | bytes 141344 | tf_op jit(solution)/shard_map/ppermute | solution.py:307
  82.9 3.0 %collective-permute-start.27 = (bf16[92,736]{1,0:T(8,128)(2,1)S(1)}, bf16[92,736]{1,0:T(8,128)(2,1)S(1)}, u32[]{:S(2)}, u32[]{:S(2)}) collective-permute-start(bf16[92,736]{1,0:T(8,128)(2,1)S(1)} %pad_maximum_fusion), channel_id=1, source_target_pairs={{0,0},{1,9},{2,18},{3,27},{4,31},{5,22},{6,13},{7,4},{8,1},{9,8},{... | collective-permute-start | bytes 406280 | tf_op jit(solution)/shard_map/ppermute | solution.py:303
  85.9 3.0 %collective-permute-start.34 = (bf16[92,368]{1,0:T(8,128)(2,1)S(1)}, bf16[92,368]{1,0:T(8,128)(2,1)S(1)}, u32[]{:S(2)}, u32[]{:S(2)}) collective-permute-start(bf16[92,368]{1,0:T(8,128)(2,1)S(1)} %pad_maximum_fusion.2), channel_id=1, source_target_pairs={{0,0},{1,9},{2,18},{3,27},{4,31},{5,22},{6,13},{7,4},{8,1},{9,8},{... | collective-permute-start | bytes 203144 | tf_op jit(solution)/shard_map/ppermute | solution.py:303
  88.9 5.0 %collective-permute-done.34 = bf16[92,368]{1,0:T(8,128)(2,1)S(1)} collective-permute-done((bf16[92,368]{1,0:T(8,128)(2,1)S(1)}, bf16[92,368]{1,0:T(8,128)(2,1)S(1)}, u32[]{:S(2)}, u32[]{:S(2)}) %collective-permute-start.34) | collective-permute-done | bytes 67744 | tf_op jit(solution)/shard_map/ppermute | solution.py:303
  93.9 0.8 maximum_bitcast_fusion
  (53 shorter events, 0.9 us)
Async XLA Ops:
  0.0 0.9 copy-start
  1.5 21.0 %collective-permute-start.13 = (bf16[48,24,128]{2,1,0:T(8,128)(2,1)S(1)}, bf16[48,24,128]{2,1,0:T(8,128)(2,1)S(1)}, u32[]{:S(2)}, u32[]{:S(2)}) collective-permute-start(bf16[48,24,128]{2,1,0:T(8,128)(2,1)S(1)} %shard_map.48.refs_0_), channel_id=1, source_target_pairs={{0,1},{1,2},{2,3},{3,4},{4,5},{5,6},{6,7},{7,0},{8,9},{9,10},{10,1... | collective-permute-start | bytes 884744 | tf_op jit(solution)/shard_map/ppermute | solution.py:307
  3.4 19.4 %collective-permute-start.14 = (bf16[48,24,128]{2,1,0:T(8,128)(2,1)S(1)}, bf16[48,24,128]{2,1,0:T(8,128)(2,1)S(1)}, u32[]{:S(2)}, u32[]{:S(2)}) collective-permute-start(bf16[48,24,128]{2,1,0:T(8,128)(2,1)S(1)} %shard_map.48.refs_0_), channel_id=1, source_target_pairs={{0,7},{1,0},{2,1},{3,2},{4,3},{5,4},{6,5},{7,6},{8,15},{9,8},{10,9... | collective-permute-start | bytes 884744 | tf_op jit(solution)/shard_map/ppermute | solution.py:307
  10.7 6.1 %collective-permute-start = (bf16[3,24,128]{2,1,0:T(8,128)(2,1)}, bf16[3,24,128]{2,1,0:T(8,128)(2,1)S(1)}, u32[]{:S(2)}, u32[]{:S(2)}) collective-permute-start(bf16[3,24,128]{2,1,0:T(8,128)(2,1)} %get-tuple-element.26), channel_id=1, source_target_pairs={{0,1},{1,2},{2,3},{3,0},{4,5},{5,6},{6,7},{7,4},{8,9},{9,10},{10,1... | collective-permute-start | bytes 55304 | tf_op jit(solution)/shard_map/ppermute | solution.py:316
  10.8 6.0 %collective-permute-start.1 = (bf16[3,24,128]{2,1,0:T(8,128)(2,1)}, bf16[3,24,128]{2,1,0:T(8,128)(2,1)S(1)}, u32[]{:S(2)}, u32[]{:S(2)}) collective-permute-start(bf16[3,24,128]{2,1,0:T(8,128)(2,1)} %get-tuple-element.27), channel_id=1, source_target_pairs={{0,2},{1,3},{2,0},{3,1},{4,6},{5,7},{6,4},{7,5},{8,10},{9,11},{10,... | collective-permute-start | bytes 55304 | tf_op jit(solution)/shard_map/ppermute | solution.py:316
  13.2 4.0 %collective-permute-start.2 = (bf16[3,24,128]{2,1,0:T(8,128)(2,1)}, bf16[3,24,128]{2,1,0:T(8,128)(2,1)S(1)}, u32[]{:S(2)}, u32[]{:S(2)}) collective-permute-start(bf16[3,24,128]{2,1,0:T(8,128)(2,1)} %get-tuple-element.28), channel_id=1, source_target_pairs={{0,3},{1,0},{2,1},{3,2},{4,7},{5,4},{6,5},{7,6},{8,11},{9,8},{10,9... | collective-permute-start | bytes 55304 | tf_op jit(solution)/shard_map/ppermute | solution.py:316
  17.9 8.1 %collective-permute-start.3 = (bf16[4,3,24,128]{3,2,1,0:T(8,128)(2,1)S(1)}, bf16[4,3,24,128]{3,2,1,0:T(8,128)(2,1)S(1)}, u32[]{:S(2)}, u32[]{:S(2)}) collective-permute-start(bf16[4,3,24,128]{3,2,1,0:T(8,128)(2,1)S(1)} %pad_maximum_fusion.1), channel_id=1, source_target_pairs={{0,7},{1,6},{2,5},{3,4},{4,3},{5,2},{6,1},{7,0},{8,15},{9,14},{10,... | collective-permute-start | bytes 221192 | tf_op jit(solution)/shard_map/ppermute | solution.py:320
  22.5 9.3 %collective-permute-start.15 = (bf16[48,24,128]{2,1,0:T(8,128)(2,1)S(1)}, bf16[48,24,128]{2,1,0:T(8,128)(2,1)S(1)}, u32[]{:S(2)}, u32[]{:S(2)}) collective-permute-start(bf16[48,24,128]{2,1,0:T(8,128)(2,1)S(1)} %collective-permute-done.13.refs_1_), channel_id=1, source_target_pairs={{0,1},{1,2},{2,3},{3,4},{4,5},{5,6},{6,7},{7,0},{8,9},{9,10},{10,1... | collective-permute-start | bytes 884744 | tf_op jit(solution)/shard_map/ppermute | solution.py:307
  22.9 9.0 %collective-permute-start.16 = (bf16[48,24,128]{2,1,0:T(8,128)(2,1)S(1)}, bf16[48,24,128]{2,1,0:T(8,128)(2,1)S(1)}, u32[]{:S(2)}, u32[]{:S(2)}) collective-permute-start(bf16[48,24,128]{2,1,0:T(8,128)(2,1)S(1)} %collective-permute-done.14.refs_2_), channel_id=1, source_target_pairs={{0,7},{1,0},{2,1},{3,2},{4,3},{5,4},{6,5},{7,6},{8,15},{9,8},{10,9... | collective-permute-start | bytes 884744 | tf_op jit(solution)/shard_map/ppermute | solution.py:307
  26.1 9.0 %collective-permute-start.4 = (bf16[8,3,24,128]{3,2,1,0:T(8,128)(2,1)S(1)}, bf16[8,3,24,128]{3,2,1,0:T(8,128)(2,1)S(1)}, u32[]{:S(2)}, u32[]{:S(2)}) collective-permute-start(bf16[8,3,24,128]{3,2,1,0:T(8,128)(2,1)S(1)} %constant_dynamic-update-slice_fusion.refs_0_), channel_id=1, source_target_pairs={{0,64},{32,96},{64,128},{96,160},{128,192},{160,224},{192,0},{224,... | collective-permute-start | bytes 442376 | tf_op jit(solution)/shard_map/ppermute | solution.py:307
  27.6 9.0 %collective-permute-start.5 = (bf16[8,3,24,128]{3,2,1,0:T(8,128)(2,1)S(1)}, bf16[8,3,24,128]{3,2,1,0:T(8,128)(2,1)S(1)}, u32[]{:S(2)}, u32[]{:S(2)}) collective-permute-start(bf16[8,3,24,128]{3,2,1,0:T(8,128)(2,1)S(1)} %constant_dynamic-update-slice_fusion.refs_0_), channel_id=1, source_target_pairs={{0,192},{32,224},{64,0},{96,32},{128,64},{160,96},{192,128},{224,1... | collective-permute-start | bytes 442376 | tf_op jit(solution)/shard_map/ppermute | solution.py:307
  31.8 9.4 %collective-permute-start.17 = (bf16[48,24,128]{2,1,0:T(8,128)(2,1)S(1)}, bf16[48,24,128]{2,1,0:T(8,128)(2,1)S(1)}, u32[]{:S(2)}, u32[]{:S(2)}) collective-permute-start(bf16[48,24,128]{2,1,0:T(8,128)(2,1)S(1)} %collective-permute-done.15.refs_3_), channel_id=1, source_target_pairs={{0,1},{1,2},{2,3},{3,4},{4,5},{5,6},{6,7},{7,0},{8,9},{9,10},{10,1... | collective-permute-start | bytes 884744 | tf_op jit(solution)/shard_map/ppermute | solution.py:307
  31.8 9.8 %collective-permute-start.18 = (bf16[48,24,128]{2,1,0:T(8,128)(2,1)S(1)}, bf16[48,24,128]{2,1,0:T(8,128)(2,1)S(1)}, u32[]{:S(2)}, u32[]{:S(2)}) collective-permute-start(bf16[48,24,128]{2,1,0:T(8,128)(2,1)S(1)} %collective-permute-done.16.refs_4_), channel_id=1, source_target_pairs={{0,7},{1,0},{2,1},{3,2},{4,3},{5,4},{6,5},{7,6},{8,15},{9,8},{10,9... | collective-permute-start | bytes 884744 | tf_op jit(solution)/shard_map/ppermute | solution.py:307
  35.1 5.6 %collective-permute-start.6 = (bf16[4,3,24,128]{3,2,1,0:T(8,128)(2,1)S(1)}, bf16[4,3,24,128]{3,2,1,0:T(8,128)(2,1)S(1)}, u32[]{:S(2)}, u32[]{:S(2)}) collective-permute-start(bf16[4,3,24,128]{3,2,1,0:T(8,128)(2,1)S(1)} %slice.32), channel_id=1, source_target_pairs={{0,64},{32,96},{64,128},{96,160},{128,192},{160,224},{192,0},{224,... | collective-permute-start | bytes 221192 | tf_op jit(solution)/shard_map/ppermute | solution.py:307
  36.7 4.4 %collective-permute-start.7 = (bf16[4,3,24,128]{3,2,1,0:T(8,128)(2,1)S(1)}, bf16[4,3,24,128]{3,2,1,0:T(8,128)(2,1)S(1)}, u32[]{:S(2)}, u32[]{:S(2)}) collective-permute-start(bf16[4,3,24,128]{3,2,1,0:T(8,128)(2,1)S(1)} %slice.33), channel_id=1, source_target_pairs={{0,192},{32,224},{64,0},{96,32},{128,64},{160,96},{192,128},{224,1... | collective-permute-start | bytes 221192 | tf_op jit(solution)/shard_map/ppermute | solution.py:307
  38.5 3.3 %collective-permute-start.8 = (bf16[8,3,24,128]{3,2,1,0:T(8,128)(2,1)S(1)}, bf16[8,3,24,128]{3,2,1,0:T(8,128)(2,1)S(1)}, u32[]{:S(2)}, u32[]{:S(2)}) collective-permute-start(bf16[8,3,24,128]{3,2,1,0:T(8,128)(2,1)S(1)} %constant_dynamic-update-slice_fusion.refs_0_), channel_id=1, source_target_pairs={{0,32},{32,0},{64,96},{96,64},{128,160},{160,128},{192,224},{224,1... | collective-permute-start | bytes 442376 | tf_op jit(solution)/shard_map/ppermute | solution.py:326
  40.7 1.4 %collective-permute-start.9 = (bf16[8,3,24,128]{3,2,1,0:T(8,128)(2,1)S(1)}, bf16[8,3,24,128]{3,2,1,0:T(8,128)(2,1)S(1)}, u32[]{:S(2)}, u32[]{:S(2)}) collective-permute-start(bf16[8,3,24,128]{3,2,1,0:T(8,128)(2,1)S(1)} %collective-permute-done.4.refs_1_), channel_id=1, source_target_pairs={{0,32},{32,0},{64,96},{96,64},{128,160},{160,128},{192,224},{224,1... | collective-permute-start | bytes 442376 | tf_op jit(solution)/shard_map/ppermute | solution.py:326
  41.1 4.0 %collective-permute-start.10 = (bf16[8,3,24,128]{3,2,1,0:T(8,128)(2,1)S(1)}, bf16[8,3,24,128]{3,2,1,0:T(8,128)(2,1)S(1)}, u32[]{:S(2)}, u32[]{:S(2)}) collective-permute-start(bf16[8,3,24,128]{3,2,1,0:T(8,128)(2,1)S(1)} %collective-permute-done.5.refs_2_), channel_id=1, source_target_pairs={{0,32},{32,0},{64,96},{96,64},{128,160},{160,128},{192,224},{224,1... | collective-permute-start | bytes 442376 | tf_op jit(solution)/shard_map/ppermute | solution.py:326
  41.2 3.9 %collective-permute-start.11 = (bf16[4,3,24,128]{3,2,1,0:T(8,128)(2,1)S(1)}, bf16[4,3,24,128]{3,2,1,0:T(8,128)(2,1)S(1)}, u32[]{:S(2)}, u32[]{:S(2)}) collective-permute-start(bf16[4,3,24,128]{3,2,1,0:T(8,128)(2,1)S(1)} %collective-permute-done.6.refs_3_), channel_id=1, source_target_pairs={{0,32},{32,0},{64,96},{96,64},{128,160},{160,128},{192,224},{224,1... | collective-permute-start | bytes 221192 | tf_op jit(solution)/shard_map/ppermute | solution.py:327
  41.6 3.5 %collective-permute-start.12 = (bf16[4,3,24,128]{3,2,1,0:T(8,128)(2,1)S(1)}, bf16[4,3,24,128]{3,2,1,0:T(8,128)(2,1)S(1)}, u32[]{:S(2)}, u32[]{:S(2)}) collective-permute-start(bf16[4,3,24,128]{3,2,1,0:T(8,128)(2,1)S(1)} %collective-permute-done.7.refs_4_), channel_id=1, source_target_pairs={{0,32},{32,0},{64,96},{96,64},{128,160},{160,128},{192,224},{224,1... | collective-permute-start | bytes 221192 | tf_op jit(solution)/shard_map/ppermute | solution.py:327
  41.8 9.5 %collective-permute-start.19 = (bf16[24,24,128]{2,1,0:T(8,128)(2,1)S(1)}, bf16[24,24,128]{2,1,0:T(8,128)(2,1)S(1)}, u32[]{:S(2)}, u32[]{:S(2)}) collective-permute-start(bf16[24,24,128]{2,1,0:T(8,128)(2,1)S(1)} %slice.34), channel_id=1, source_target_pairs={{0,1},{1,2},{2,3},{3,4},{4,5},{5,6},{6,7},{7,0},{8,9},{9,10},{10,1... | collective-permute-start | bytes 442376 | tf_op jit(solution)/shard_map/ppermute | solution.py:307
  42.1 9.2 %collective-permute-start.20 = (bf16[24,24,128]{2,1,0:T(8,128)(2,1)S(1)}, bf16[24,24,128]{2,1,0:T(8,128)(2,1)S(1)}, u32[]{:S(2)}, u32[]{:S(2)}) collective-permute-start(bf16[24,24,128]{2,1,0:T(8,128)(2,1)S(1)} %slice.35), channel_id=1, source_target_pairs={{0,7},{1,0},{2,1},{3,2},{4,3},{5,4},{6,5},{7,6},{8,15},{9,8},{10,9... | collective-permute-start | bytes 442376 | tf_op jit(solution)/shard_map/ppermute | solution.py:307
  45.1 0.6 copy-start.1
  56.5 11.6 %collective-permute-start.25 = (f32[44,736]{1,0:T(8,128)S(1)}, f32[44,736]{1,0:T(8,128)S(1)}, u32[]{:S(2)}, u32[]{:S(2)}) collective-permute-start(f32[44,736]{1,0:T(8,128)S(1)} %get-tuple-element.37), channel_id=1, source_target_pairs={{0,24},{8,0},{16,8},{24,16},{1,25},{9,1},{17,9},{25,17},{2,26},{10... | collective-permute-start | bytes 388616 | tf_op jit(solution)/shard_map/ppermute | solution.py:307
  60.1 4.9 %collective-permute-start.32 = (f32[44,368]{1,0:T(8,128)S(1)}, f32[44,368]{1,0:T(8,128)S(1)}, u32[]{:S(2)}, u32[]{:S(2)}) collective-permute-start(f32[44,368]{1,0:T(8,128)S(1)} %get-tuple-element.44), channel_id=1, source_target_pairs={{0,24},{8,0},{16,8},{24,16},{1,25},{9,1},{17,9},{25,17},{2,26},{10... | collective-permute-start | bytes 194312 | tf_op jit(solution)/shard_map/ppermute | solution.py:307
  60.6 7.5 %collective-permute-start.29 = (f32[48,368]{1,0:T(8,128)S(1)}, f32[48,368]{1,0:T(8,128)S(1)}, u32[]{:S(2)}, u32[]{:S(2)}) collective-permute-start(f32[48,368]{1,0:T(8,128)S(1)} %get-tuple-element.41), channel_id=1, source_target_pairs={{0,8},{8,16},{16,24},{24,0},{1,9},{9,17},{17,25},{25,1},{2,10},{10... | collective-permute-start | bytes 211976 | tf_op jit(solution)/shard_map/ppermute | solution.py:307
  62.2 8.7 %collective-permute-start.31 = (f32[44,368]{1,0:T(8,128)S(1)}, f32[44,368]{1,0:T(8,128)S(1)}, u32[]{:S(2)}, u32[]{:S(2)}) collective-permute-start(f32[44,368]{1,0:T(8,128)S(1)} %get-tuple-element.42), channel_id=1, source_target_pairs={{0,8},{8,16},{16,24},{24,0},{1,9},{9,17},{17,25},{25,1},{2,10},{10... | collective-permute-start | bytes 194312 | tf_op jit(solution)/shard_map/ppermute | solution.py:307
  65.0 6.0 %collective-permute-start.33 = (f32[44,368]{1,0:T(8,128)S(1)}, f32[44,368]{1,0:T(8,128)S(1)}, u32[]{:S(2)}, u32[]{:S(2)}) collective-permute-start(f32[44,368]{1,0:T(8,128)S(1)} %add.52), channel_id=1, source_target_pairs={{0,24},{8,0},{16,8},{24,16},{1,25},{9,1},{17,9},{25,17},{2,26},{10... | collective-permute-start | bytes 194312 | tf_op jit(solution)/shard_map/ppermute | solution.py:307
  65.7 11.9 %collective-permute-start.28 = (f32[48,368]{1,0:T(8,128)S(1)}, f32[48,368]{1,0:T(8,128)S(1)}, u32[]{:S(2)}, u32[]{:S(2)}) collective-permute-start(f32[48,368]{1,0:T(8,128)S(1)} %get-tuple-element.39), channel_id=1, source_target_pairs={{0,24},{8,0},{16,8},{24,16},{1,25},{9,1},{17,9},{25,17},{2,26},{10... | collective-permute-start | bytes 211976 | tf_op jit(solution)/shard_map/ppermute | solution.py:307
  68.1 9.9 %collective-permute-start.24 = (f32[44,736]{1,0:T(8,128)S(1)}, f32[44,736]{1,0:T(8,128)S(1)}, u32[]{:S(2)}, u32[]{:S(2)}) collective-permute-start(f32[44,736]{1,0:T(8,128)S(1)} %get-tuple-element.35), channel_id=1, source_target_pairs={{0,8},{8,16},{16,24},{24,0},{1,9},{9,17},{17,25},{25,1},{2,10},{10... | collective-permute-start | bytes 388616 | tf_op jit(solution)/shard_map/ppermute | solution.py:307
  68.1 7.7 %collective-permute-start.22 = (f32[48,736]{1,0:T(8,128)S(1)}, f32[48,736]{1,0:T(8,128)S(1)}, u32[]{:S(2)}, u32[]{:S(2)}) collective-permute-start(f32[48,736]{1,0:T(8,128)S(1)} %get-tuple-element.34), channel_id=1, source_target_pairs={{0,8},{8,16},{16,24},{24,0},{1,9},{9,17},{17,25},{25,1},{2,10},{10... | collective-permute-start | bytes 423944 | tf_op jit(solution)/shard_map/ppermute | solution.py:307
  70.9 10.1 %collective-permute-start.21 = (f32[48,736]{1,0:T(8,128)S(1)}, f32[48,736]{1,0:T(8,128)S(1)}, u32[]{:S(2)}, u32[]{:S(2)}) collective-permute-start(f32[48,736]{1,0:T(8,128)S(1)} %get-tuple-element.32), channel_id=1, source_target_pairs={{0,24},{8,0},{16,8},{24,16},{1,25},{9,1},{17,9},{25,17},{2,26},{10... | collective-permute-start | bytes 423944 | tf_op jit(solution)/shard_map/ppermute | solution.py:307
  71.0 7.0 %collective-permute-start.30 = (f32[48,368]{1,0:T(8,128)S(1)}, f32[48,368]{1,0:T(8,128)S(1)}, u32[]{:S(2)}, u32[]{:S(2)}) collective-permute-start(f32[48,368]{1,0:T(8,128)S(1)} %add.49), channel_id=1, source_target_pairs={{0,8},{8,16},{16,24},{24,0},{1,9},{9,17},{17,25},{25,1},{2,10},{10... | collective-permute-start | bytes 211976 | tf_op jit(solution)/shard_map/ppermute | solution.py:307
  75.8 5.1 %collective-permute-start.26 = (f32[44,736]{1,0:T(8,128)S(1)}, f32[44,736]{1,0:T(8,128)S(1)}, u32[]{:S(2)}, u32[]{:S(2)}) collective-permute-start(f32[44,736]{1,0:T(8,128)S(1)} %add.46), channel_id=1, source_target_pairs={{0,24},{8,0},{16,8},{24,16},{1,25},{9,1},{17,9},{25,17},{2,26},{10... | collective-permute-start | bytes 388616 | tf_op jit(solution)/shard_map/ppermute | solution.py:307
  77.6 5.2 %collective-permute-start.23 = (f32[48,736]{1,0:T(8,128)S(1)}, f32[48,736]{1,0:T(8,128)S(1)}, u32[]{:S(2)}, u32[]{:S(2)}) collective-permute-start(f32[48,736]{1,0:T(8,128)S(1)} %add.43), channel_id=1, source_target_pairs={{0,8},{8,16},{16,24},{24,0},{1,9},{9,17},{17,25},{25,1},{2,10},{10... | collective-permute-start | bytes 423944 | tf_op jit(solution)/shard_map/ppermute | solution.py:307
  82.9 11.0 %collective-permute-start.27 = (bf16[92,736]{1,0:T(8,128)(2,1)S(1)}, bf16[92,736]{1,0:T(8,128)(2,1)S(1)}, u32[]{:S(2)}, u32[]{:S(2)}) collective-permute-start(bf16[92,736]{1,0:T(8,128)(2,1)S(1)} %pad_maximum_fusion), channel_id=1, source_target_pairs={{0,0},{1,9},{2,18},{3,27},{4,31},{5,22},{6,13},{7,4},{8,1},{9,8},{... | collective-permute-start | bytes 406280 | tf_op jit(solution)/shard_map/ppermute | solution.py:303
  85.9 7.9 %collective-permute-start.34 = (bf16[92,368]{1,0:T(8,128)(2,1)S(1)}, bf16[92,368]{1,0:T(8,128)(2,1)S(1)}, u32[]{:S(2)}, u32[]{:S(2)}) collective-permute-start(bf16[92,368]{1,0:T(8,128)(2,1)S(1)} %pad_maximum_fusion.2), channel_id=1, source_target_pairs={{0,0},{1,9},{2,18},{3,27},{4,31},{5,22},{6,13},{7,4},{8,1},{9,8},{... | collective-permute-start | bytes 203144 | tf_op jit(solution)/shard_map/ppermute | solution.py:303

commit v6 on v5

--- a/solution.py
+++ b/solution.py
@@ -22,7 +22,7 @@
 WIDE = 4 * CHUNK
 ROWS = 48
 SPANS = ((0, 92), (96, 144), (144, 188), (192, 240), (240, 284), (288, 336), (336, 380))
-STARTS = (0, 8, 16, 24, 28, 32, 40, 48, 56, 60)
+STARTS = (0, 8, 16, 24, 32, 40, 48, 56)
 OFFSETS = (0, 7, 1, 6, 2, 5, 3, 4)
 
 
@@ -76,8 +76,8 @@
     )(left_values[:, 0])
 
 
-def pack_right_kernel(meta_ref, right_in, right_cols_in, left_cols_in, *refs):
-    outs, (flat_ref, code_ref, tmp_ref, right_ref, right_cols_ref, left_cols_ref, sems) = refs[:TILES], refs[TILES:]
+def pack_right_kernel(right_in, right_cols_in, left_cols_in, *refs):
+    outs, (flat_ref, code_ref, tmp_ref, right_ref, right_cols_ref, left_cols_ref, sems) = refs[:1], refs[1:]
     copies = [
         pltpu.make_async_copy(a, b, sems.at[n])
         for n, (a, b) in enumerate(
@@ -117,20 +117,19 @@
                 line = codes[2 * u + h : 2 * u + h + 1, :]
                 z = z + pltpu.roll(jnp.broadcast_to(line, (8, LANES)), 16 + ROWS * h, 1)
         tmp_ref[u, pl.ds(BLK, 8, stride=APAD), :] = z
-    for t in range(TILES):
-        tile = lax.bitwise_xor((meta_ref[0] + t) & 3, 3 * lax.shift_right_logical(meta_ref[0], 2))
+    for d in range(GROUP):
+        tile = min(d, 7 - d)
         for u in range(USLOTS):
-            rows = tmp_ref[u, pl.ds(pl.multiple_of(tile * APAD, 8), APAD), :]
-            outs[t][u] = rows.astype(jnp.bfloat16)
-
-
-def pack_right(meta, right_values, right_columns, left_columns):
+            outs[0][d, u] = tmp_ref[u, tile * APAD : (tile + 1) * APAD, :].astype(jnp.bfloat16)
+
+
+def pack_right(right_values, right_columns, left_columns):
     vmem = pl.BlockSpec(memory_space=pltpu.VMEM)
     return pl.pallas_call(
         pack_right_kernel,
-        out_shape=(jax.ShapeDtypeStruct((USLOTS, APAD, LANES), jnp.bfloat16),) * TILES,
-        in_specs=[pl.BlockSpec(memory_space=pltpu.SMEM)] + [pl.BlockSpec(memory_space=pl.ANY)] * 3,
-        out_specs=(vmem,) * TILES,
+        out_shape=jax.ShapeDtypeStruct((GROUP, USLOTS, APAD, LANES), jnp.bfloat16),
+        in_specs=[pl.BlockSpec(memory_space=pl.ANY)] * 3,
+        out_specs=vmem,
         scratch_shapes=[
             pltpu.VMEM((HERE * USLOTS * 8, 5 * LANES), jnp.float32),
             pltpu.VMEM((8, LANES), jnp.float32),
@@ -141,7 +140,6 @@
             pltpu.SemaphoreType.DMA((3,)),
         ],
     )(
-        meta,
         jnp.transpose(right_values[0], (0, 2, 1, 3)),
         jnp.transpose(right_columns[0], (2, 1, 0)),
         jnp.transpose(left_columns[:, 0], (1, 0)),
@@ -165,7 +163,7 @@
     ).astype(jnp.int32)
     local = codes - 16 * lax.shift_right_logical(depth, 2)
     chunk = lax.bitwise_xor(lax.shift_right_arithmetic(local, 2), lax.bitwise_xor(depth, 7 * (depth >> 2)) & 3)
-    at = CHUNK * ((chunk - col) & 3) + BLK * (local & 3)
+    at = CHUNK * (((chunk - col) * (1 - 2 * core)) & 3) + BLK * (local & 3)
     at = jnp.where((local >= 0) & (local < 16), at, 4 * LANES)
     turned_ref[0:8, :] = at
     turned_ref[8:16, :] = (at + 4 * LANES - BLK * lax.broadcasted_iota(jnp.int32, at.shape, 0)) & (LANES - 1)
@@ -178,13 +176,11 @@
 
     def fill(n, carry):
         j = lax.shift_right_logical(n, 3) & 3
-        x = side + jnp.where(j == 1, 3, j - lax.shift_right_logical(j, 1))
-        row = 2 * (x & 3) + lax.bitwise_xor(core, lax.shift_right_logical(n, 5))
+        owner = lax.bitwise_xor(core, lax.shift_right_logical(n, 5))
+        x = side + (1 - 2 * owner) * jnp.where(j == 1, 3, j - lax.shift_right_logical(j, 1))
+        row = 2 * (x & 3) + owner
         spot = n & 7
-        other = lax.shift_right_logical(spot, 2)
-        quad = lax.bitwise_xor(lax.shift_right_logical(depth, 2), other)
-        panel = quad * 4 + ((lax.bitwise_xor(depth, 3 * other) - spot) & 3)
-        base = panel * PANEL + row * HERE
+        base = spot * PANEL + row * HERE
         first = n * USLOTS
         blocks = [right_ref[n, u].astype(jnp.float32) for u in range(USLOTS)]
         for k in range(HERE):
@@ -229,9 +225,8 @@
     depth = meta_ref[0]
     at = []
     for o in offsets:
-        panel = (depth + o) & 7
-        other = lax.shift_right_logical(lax.bitwise_xor(panel, depth), 2)
-        line = other * 4 + ((lax.bitwise_xor(depth, 3 * other) - panel) & 3)
+        panel = (depth + o * (1 - 2 * meta_ref[1])) & 7
+        line = panel
         for s in range(SLOTS):
             at.append(panel * PANEL + table_ref[line * USLOTS + s // 2, 16 + ROWS * (s % 2) + i])
     return jnp.concatenate([jnp.concatenate([wide_ref[n, q] for n in at], axis=0) for q in range(3)], axis=1)
@@ -304,36 +299,37 @@
 
 
 def shift(x, axis, by, n):
-    return lax.ppermute(x, axis, [(i, (i + by) % n) for i in range(n)])
+    pairs = []
+    for r in range(8):
+        way = by if r % 2 == 0 else -by
+        if axis == "row":
+            pairs.append((r, (r + way) % n))
+        else:
+            pairs += [(r * n + i, r * n + (i + way) % n) for i in range(n)]
+    return lax.ppermute(x, axis if axis == "row" else ("row", axis), pairs)
 
 
 def body(left_values, left_columns, right_values, right_columns):
     c, d = lax.axis_index("col"), lax.axis_index("depth")
     meta = jnp.stack([d, lax.axis_index("row") % 2, lax.axis_index("row") // 2, c])
-    tiles = pack_right(meta, right_values, right_columns, left_columns)
+    tiles = pack_right(right_values, right_columns, left_columns)
     left = pack_left(left_values)
-    near = [tiles[0]] + [
-        lax.ppermute(tiles[k], "depth", [(z, z // 4 * 4 + (z + k) % 4) for z in range(8)]) for k in (1, 2, 3)
-    ]
+    right = lax.all_to_all(tiles, "depth", 0, 0)
     up1, down1 = shift(left, "depth", 1, 8), shift(left, "depth", -1, 8)
-    half = jnp.stack(near, axis=0)
-    other = lax.ppermute(half, "depth", [(z, 7 - z) for z in range(8)])
-    right = jnp.concatenate([half, other], axis=0)
+    up1, down1, right = lax.optimization_barrier((up1, down1, right))
     swap = [(i, i ^ 1) for i in range(8)]
+    f2 = shift(right, "row", 4, 8)
     f1, b1 = shift(right, "row", 2, 8), shift(right, "row", -2, 8)
     up2, down2 = shift(up1, "depth", 1, 8), shift(down1, "depth", -1, 8)
-    f2, b2 = shift(f1[:4], "row", 2, 8), shift(b1[4:], "row", -2, 8)
     others = [lax.ppermute(x, "row", swap) for x in (right, f1, b1)]
-    others += [lax.ppermute(x, "row", swap) for x in (f2, b2)]
+    others += [lax.ppermute(f2, "row", swap)]
     up3, down3 = shift(up2, "depth", 1, 8), shift(down2, "depth", -1, 8)
     edge = ROWS // 2
     up4, down4 = shift(up3[:edge], "depth", 1, 8), shift(down3[edge:], "depth", -1, 8)
     lefts = [left, up1, down1, up2, down2, up3, down3, up4, down4]
-    wide, table = fill(meta, [right, f1, b1, f2, b2] + others)
-    first = product(meta, table, wide, lefts, 0, 4)
-    second = product(meta, table, wide, lefts, 4, 2)
-    done = [summed(first), summed(second)]
-    return jnp.concatenate(done, axis=1).T
+    wide, table = fill(meta, [right, f1, b1, f2] + others)
+    parts = product(meta, table, wide, lefts, 0, 6)
+    return summed(parts).T
 
 
 def solution(mesh):

time: 96.5 us -> 94.3 us (0.977); the launches traced: 94.6 us -> 93.9 us
  starting transfers between devices: 52.9 us -> 30.8 us
  blocking collectives: 0 us -> 14.7 us
  waiting for transfers between devices: 19.9 us -> 30.7 us
  other arithmetic: 2.26 us -> 0.24 us
  Pallas kernels: 17 us -> 15.6 us
    ppermute x30 -> x18, starting transfers between devices: 46.8 us -> 28.4 us  [the longest x17 28.4 us: shift(): return lax.ppermute(x, axis if axis == 'row' else ('row', axis), pairs)]
    all_to_all x0 -> x1, blocking collectives: none -> 14.7 us  [body(): right = lax.all_to_all(tiles, 'depth', 0, 0)]
    ppermute x30 -> x18, waiting for transfers between devices: 14.7 us -> 21.6 us  [the longest x17 21.6 us: shift(): return lax.ppermute(x, axis if axis == 'row' else ('row', axis), pairs)]
    ppermute x2 -> x1, waiting for transfers between devices: 4.98 us -> 9.17 us  [summed(): return lax.ppermute(done, ('col', 'depth'), home)]
    ppermute x2 -> x1, starting transfers between devices: 5.96 us -> 1.92 us  [summed(): return lax.ppermute(done, ('col', 'depth'), home)]
    pallas_call x2 -> x1, Pallas kernels: 8.22 us -> 7.44 us  [product(): pl.pallas_call(functools.partial(product_kernel, start, count), out_shape...]
    unnamed x8 -> x3, local copies, waits for them, and re-layouts: 2.26 us -> 1.63 us
  transfers between devices with their start and end apart: 35 -> 22, of which waited for: 11 -> 9; matrix products, arithmetic and copies ran while one was open for 2% -> 0% of each run, Pallas kernels for 12% -> 8%
where the time goes in v6:
time: 94.3 us; the launch traced here: 93.9 us
  starting transfers between devices  30.8 us (33%)
  waiting for transfers between devices  30.7 us (33%)
  Pallas kernels  15.6 us (17%)
  blocking collectives  14.7 us (16%)
  local copies, waits for them, and re-layouts  1.66 us (2%)
    ppermute x17, starting transfers between devices, shift(): return lax.ppermute(x, axis if axis == 'row' else ('row', axis), pairs)  28.4 us
    ppermute x17, waiting for transfers between devices, shift(): return lax.ppermute(x, axis if axis == 'row' else ('row', axis), pairs)  21.6 us
    all_to_all x1, blocking collectives, body(): right = lax.all_to_all(tiles, 'depth', 0, 0)  14.7 us
    ppermute x1, waiting for transfers between devices, summed(): return lax.ppermute(done, ('col', 'depth'), home)  9.17 us
    pallas_call x1, Pallas kernels, product(): pl.pallas_call(functools.partial(product_kernel, start, count), out_shape...  7.44 us
    pallas_call x1, Pallas kernels, fill(): pl.pallas_call(fill_kernel, out_shape=(jax.ShapeDtypeStruct((GROUP * PANE...  5.62 us
    pallas_call x1, Pallas kernels, pack_right(): pl.pallas_call(pack_right_kernel, out_shape=jax.ShapeDtypeStruct((GROUP,...  2.09 us
    ppermute x1, starting transfers between devices, summed(): return lax.ppermute(done, ('col', 'depth'), home)  1.92 us
  transfers between devices with their start and end apart: 22, of which 9 were waited for; matrix products, arithmetic and copies ran while one was open for 0% of the time, Pallas kernels for 8%

profile of v6, /device:TPU:16, one launch (start us, length us, event | category | flops | bytes accessed | tf_op | source)
XLA Modules:
  0.0 93.9 jit_solution(13403231838606574989)
XLA Ops:
  0.0 0.9 %copy-done = bf16[48,1,4,529]{3,2,1,0:T(4,128)(2,1)S(1)} copy-done((bf16[48,1,4,529]{3,2,1,0:T(4,128)(2,1)S(1)}, bf16[48,1,4,529]{3,2,1,0:T(4,128)(2,1)}, u32[]{:S(2)}) %copy-start) | copy-done | bytes 203160
  0.9 0.5 shard_map.46.refs_0_
  1.5 5.9 %collective-permute-start.1 = (bf16[48,24,128]{2,1,0:T(8,128)(2,1)S(1)}, bf16[48,24,128]{2,1,0:T(8,128)(2,1)S(1)}, u32[]{:S(2)}, u32[]{:S(2)}) collective-permute-start(bf16[48,24,128]{2,1,0:T(8,128)(2,1)S(1)} %shard_map.46.refs_0_), channel_id=1, source_target_pairs={{0,7},{1,0},{2,1},{3,2},{4,3},{5,4},{6,5},{7,6},{32,33},{33,34},{3... | collective-permute-start | bytes 884744 | tf_op jit(solution)/shard_map/ppermute | solution.py:309
  7.4 2.1 %shard_map.47 = bf16[8,3,24,128]{3,2,1,0:T(8,128)(2,1)} custom-call(bf16[5,3,4,529]{3,2,1,0:T(4,128)(2,1)} %bitcast.17, s32[3,4,5]{2,1,0:T(4,128)} %bitcast.18, s32[4,48]{1,0:T(4,128)} %bitcast.19), custom_call_target="tpu_custom_call" | custom-call | tf_op jit(solution)/shard_map/pallas_call | solution.py:128
  9.5 14.7 %all_to_all.5.refs_0_ = bf16[8,3,24,128]{3,2,1,0:T(8,128)(2,1)S(1)} all-to-all(bf16[8,3,24,128]{3,2,1,0:T(8,128)(2,1)} %shard_map.47), channel_id=1, replica_groups=mesh['row'=8,'col'=4,'depth'=8] {'depth'}, dimensions={0} | all-to-all | bytes 294912 | tf_op jit(solution)/shard_map/all_to_all | solution.py:317
  24.2 0.0 collective-permute-done.1.refs_2_
  24.2 0.0 collective-permute-done.refs_1_
  24.2 0.5 collective-permute-start.9
  24.7 2.7 %collective-permute-start.10 = (bf16[48,24,128]{2,1,0:T(8,128)(2,1)S(1)}, bf16[48,24,128]{2,1,0:T(8,128)(2,1)S(1)}, u32[]{:S(2)}, u32[]{:S(2)}) collective-permute-start(bf16[48,24,128]{2,1,0:T(8,128)(2,1)S(1)} %collective-permute-done.1.refs_2_), channel_id=1, source_target_pairs={{0,7},{1,0},{2,1},{3,2},{4,3},{5,4},{6,5},{7,6},{32,33},{33,34},{3... | collective-permute-start | bytes 884744 | tf_op jit(solution)/shard_map/ppermute | solution.py:309
  27.4 5.9 %collective-permute-done.9.refs_3_ = bf16[48,24,128]{2,1,0:T(8,128)(2,1)S(1)} collective-permute-done((bf16[48,24,128]{2,1,0:T(8,128)(2,1)S(1)}, bf16[48,24,128]{2,1,0:T(8,128)(2,1)S(1)}, u32[]{:S(2)}, u32[]{:S(2)}) %collective-permute-start.9) | collective-permute-done | bytes 294944 | tf_op jit(solution)/shard_map/ppermute | solution.py:309
  33.4 0.5 collective-permute-start.11
  33.8 3.0 %collective-permute-start.4 = (bf16[8,3,24,128]{3,2,1,0:T(8,128)(2,1)S(1)}, bf16[8,3,24,128]{3,2,1,0:T(8,128)(2,1)S(1)}, u32[]{:S(2)}, u32[]{:S(2)}) collective-permute-start(bf16[8,3,24,128]{3,2,1,0:T(8,128)(2,1)S(1)} %all_to_all.5.refs_0_), channel_id=1, source_target_pairs={{0,128},{32,160},{64,192},{96,224},{128,0},{160,32},{192,64},{224,... | collective-permute-start | bytes 442376 | tf_op jit(solution)/shard_map/ppermute | solution.py:309
  36.8 2.8 %collective-permute-start.12 = (bf16[48,24,128]{2,1,0:T(8,128)(2,1)S(1)}, bf16[48,24,128]{2,1,0:T(8,128)(2,1)S(1)}, u32[]{:S(2)}, u32[]{:S(2)}) collective-permute-start(bf16[48,24,128]{2,1,0:T(8,128)(2,1)S(1)} %collective-permute-done.10.refs_4_), channel_id=1, source_target_pairs={{0,7},{1,0},{2,1},{3,2},{4,3},{5,4},{6,5},{7,6},{32,33},{33,34},{3... | collective-permute-start | bytes 884744 | tf_op jit(solution)/shard_map/ppermute | solution.py:309
  39.6 1.1 %collective-permute-start.3 = (bf16[8,3,24,128]{3,2,1,0:T(8,128)(2,1)S(1)}, bf16[8,3,24,128]{3,2,1,0:T(8,128)(2,1)S(1)}, u32[]{:S(2)}, u32[]{:S(2)}) collective-permute-start(bf16[8,3,24,128]{3,2,1,0:T(8,128)(2,1)S(1)} %all_to_all.5.refs_0_), channel_id=1, source_target_pairs={{0,192},{32,96},{64,0},{96,160},{128,64},{160,224},{192,128},{224,... | collective-permute-start | bytes 442376 | tf_op jit(solution)/shard_map/ppermute | solution.py:309
  40.8 0.9 collective-permute-start.2
  41.6 0.0 collective-permute-done.4.refs_3_
  41.6 0.0 collective-permute-start.5
  41.6 3.1 %collective-permute-done.3.refs_2_ = bf16[8,3,24,128]{3,2,1,0:T(8,128)(2,1)S(1)} collective-permute-done((bf16[8,3,24,128]{3,2,1,0:T(8,128)(2,1)S(1)}, bf16[8,3,24,128]{3,2,1,0:T(8,128)(2,1)S(1)}, u32[]{:S(2)}, u32[]{:S(2)}) %collective-permute-start.3) | collective-permute-done | bytes 147488 | tf_op jit(solution)/shard_map/ppermute | solution.py:309
  44.8 2.3 %collective-permute-done.2.refs_1_ = bf16[8,3,24,128]{3,2,1,0:T(8,128)(2,1)S(1)} collective-permute-done((bf16[8,3,24,128]{3,2,1,0:T(8,128)(2,1)S(1)}, bf16[8,3,24,128]{3,2,1,0:T(8,128)(2,1)S(1)}, u32[]{:S(2)}, u32[]{:S(2)}) %collective-permute-start.2) | collective-permute-done | bytes 147488 | tf_op jit(solution)/shard_map/ppermute | solution.py:309
  47.1 0.0 collective-permute-start.7
  47.1 0.0 collective-permute-done.11.refs_5_
  47.1 0.5 collective-permute-start.6
  47.6 0.1 pad_add_fusion.meta_ref
  47.7 0.0 collective-permute-done.12.refs_6_
  47.7 0.1 collective-permute-start.13
  47.8 0.0 collective-permute-done.5.refs_4_
  47.9 3.5 %collective-permute-start.14 = (bf16[24,24,128]{2,1,0:T(8,128)(2,1)S(1)}, bf16[24,24,128]{2,1,0:T(8,128)(2,1)S(1)}, u32[]{:S(2)}, u32[]{:S(2)}) collective-permute-start(bf16[24,24,128]{2,1,0:T(8,128)(2,1)S(1)} %slice.17), channel_id=1, source_target_pairs={{0,7},{1,0},{2,1},{3,2},{4,3},{5,4},{6,5},{7,6},{32,33},{33,34},{3... | collective-permute-start | bytes 442376 | tf_op jit(solution)/shard_map/ppermute | solution.py:309
  51.3 0.0 collective-permute-done.8.refs_7_
  51.3 0.0 collective-permute-done.7.refs_6_
  51.3 0.0 collective-permute-done.6.refs_5_
  51.3 5.6 %shard_map.48 = (bf16[320,3,32,128]{3,2,1,0:T(8,128)(2,1)S(1)}, s32[24,128]{1,0:T(8,128)S(1)}) custom-call(s32[4]{0:T(128)S(1)} %pad_add_fusion.meta_ref, bf16[8,3,24,128]{3,2,1,0:T(8,128)(2,1)S(1)} %all_to_all.5.refs_0_, bf16[8,3,24,128]{3,2,1,0:T(8,128)(2,1)S(1)} %collective-permute-done.2.refs_1_, ...), custom_call_target="tpu_custom_call" | custom-call | flops 3000000000 | bytes 8000000 | tf_op jit(solution)/shard_map/pallas_call | solution.py:204
  57.0 0.0 collective-permute-done.14.refs_8_
  57.0 7.4 %shard_map.49 = (f32[92,1104]{1,0:T(8,128)S(1)}, f32[48,1104]{1,0:T(8,128)S(1)}, f32[44,1104]{1,0:T(8,128)S(1)}, f32[48,1104]{1,0:T(8,128)S(1)}, f32[44,1104]{1,...) custom-call(s32[4]{0:T(128)S(1)} %pad_add_fusion.meta_ref, s32[24,128]{1,0:T(8,128)S(1)} %get-tuple-element.18.table_ref, ...), custom_call_target="tpu_custom_call" | custom-call | flops 6000000000 | bytes 8000000 | tf_op jit(solution)/shard_map/pallas_call | solution.py:268
  64.4 0.5 collective-permute-start.19
  65.0 1.6 %collective-permute-start.16 = (f32[48,1104]{1,0:T(8,128)S(1)}, f32[48,1104]{1,0:T(8,128)S(1)}, u32[]{:S(2)}, u32[]{:S(2)}) collective-permute-start(f32[48,1104]{1,0:T(8,128)S(1)} %get-tuple-element.25), channel_id=1, source_target_pairs={{0,8},{8,16},{16,24},{24,0},{32,56},{40,32},{48,40},{56,48},{64,72... | collective-permute-start | bytes 635912 | tf_op jit(solution)/shard_map/ppermute | solution.py:309
  66.5 2.5 %collective-permute-start.18 = (f32[44,1104]{1,0:T(8,128)S(1)}, f32[44,1104]{1,0:T(8,128)S(1)}, u32[]{:S(2)}, u32[]{:S(2)}) collective-permute-start(f32[44,1104]{1,0:T(8,128)S(1)} %get-tuple-element.26), channel_id=1, source_target_pairs={{0,8},{8,16},{16,24},{24,0},{32,56},{40,32},{48,40},{56,48},{64,72... | collective-permute-start | bytes 582920 | tf_op jit(solution)/shard_map/ppermute | solution.py:309
  69.0 3.8 %collective-permute-done.19 = f32[44,1104]{1,0:T(8,128)S(1)} collective-permute-done((f32[44,1104]{1,0:T(8,128)S(1)}, f32[44,1104]{1,0:T(8,128)S(1)}, u32[]{:S(2)}, u32[]{:S(2)}) %collective-permute-start.19) | collective-permute-done | bytes 194336 | tf_op jit(solution)/shard_map/ppermute | solution.py:309
  72.8 0.5 collective-permute-start.20
  73.4 1.0 %collective-permute-start.15 = (f32[48,1104]{1,0:T(8,128)S(1)}, f32[48,1104]{1,0:T(8,128)S(1)}, u32[]{:S(2)}, u32[]{:S(2)}) collective-permute-start(f32[48,1104]{1,0:T(8,128)S(1)} %get-tuple-element.23), channel_id=1, source_target_pairs={{0,24},{8,0},{16,8},{24,16},{32,40},{40,48},{48,56},{56,32},{64,88... | collective-permute-start | bytes 635912 | tf_op jit(solution)/shard_map/ppermute | solution.py:309
  74.4 1.3 %collective-permute-start.17 = (f32[48,1104]{1,0:T(8,128)S(1)}, f32[48,1104]{1,0:T(8,128)S(1)}, u32[]{:S(2)}, u32[]{:S(2)}) collective-permute-start(f32[48,1104]{1,0:T(8,128)S(1)} %add.25), channel_id=1, source_target_pairs={{0,8},{8,16},{16,24},{24,0},{32,56},{40,32},{48,40},{56,48},{64,72... | collective-permute-start | bytes 635912 | tf_op jit(solution)/shard_map/ppermute | solution.py:309
  75.6 0.7 collective-permute-done.18
  76.3 3.0 %collective-permute-done.20 = f32[44,1104]{1,0:T(8,128)S(1)} collective-permute-done((f32[44,1104]{1,0:T(8,128)S(1)}, f32[44,1104]{1,0:T(8,128)S(1)}, u32[]{:S(2)}, u32[]{:S(2)}) %collective-permute-start.20) | collective-permute-done | bytes 194336 | tf_op jit(solution)/shard_map/ppermute | solution.py:309
  79.3 0.1 add_convert_fusion
  79.4 2.3 %collective-permute-done.15 = f32[48,1104]{1,0:T(8,128)S(1)} collective-permute-done((f32[48,1104]{1,0:T(8,128)S(1)}, f32[48,1104]{1,0:T(8,128)S(1)}, u32[]{:S(2)}, u32[]{:S(2)}) %collective-permute-start.15) | collective-permute-done | bytes 212000 | tf_op jit(solution)/shard_map/ppermute | solution.py:309
  81.7 0.4 collective-permute-done.17
  82.1 1.9 %collective-permute-start.21 = (bf16[92,1104]{1,0:T(8,128)(2,1)S(1)}, bf16[92,1104]{1,0:T(8,128)(2,1)S(1)}, u32[]{:S(2)}, u32[]{:S(2)}) collective-permute-start(bf16[92,1104]{1,0:T(8,128)(2,1)S(1)} %pad_maximum_fusion), channel_id=1, source_target_pairs={{0,0},{1,9},{2,18},{3,27},{4,31},{5,22},{6,13},{7,4},{8,1},{9,8},{... | collective-permute-start | bytes 609416 | tf_op jit(solution)/shard_map/ppermute | solution.py:298
  84.0 9.2 %collective-permute-done.21 = bf16[92,1104]{1,0:T(8,128)(2,1)S(1)} collective-permute-done((bf16[92,1104]{1,0:T(8,128)(2,1)S(1)}, bf16[92,1104]{1,0:T(8,128)(2,1)S(1)}, u32[]{:S(2)}, u32[]{:S(2)}) %collective-permute-start.21) | collective-permute-done | bytes 203168 | tf_op jit(solution)/shard_map/ppermute | solution.py:298
  93.2 0.7 copy.6
  (12 shorter events, 0.2 us)
Async XLA Ops:
  0.0 0.9 %copy-start = (bf16[48,1,4,529]{3,2,1,0:T(4,128)(2,1)S(1)}, bf16[48,1,4,529]{3,2,1,0:T(4,128)(2,1)}, u32[]{:S(2)}) copy-start(bf16[48,1,4,529]{3,2,1,0:T(4,128)(2,1)} %param.4) | copy-start | bytes 609412
  1.5 22.7 %collective-permute-start.1 = (bf16[48,24,128]{2,1,0:T(8,128)(2,1)S(1)}, bf16[48,24,128]{2,1,0:T(8,128)(2,1)S(1)}, u32[]{:S(2)}, u32[]{:S(2)}) collective-permute-start(bf16[48,24,128]{2,1,0:T(8,128)(2,1)S(1)} %shard_map.46.refs_0_), channel_id=1, source_target_pairs={{0,7},{1,0},{2,1},{3,2},{4,3},{5,4},{6,5},{7,6},{32,33},{33,34},{3... | collective-permute-start | bytes 884744 | tf_op jit(solution)/shard_map/ppermute | solution.py:309
  7.4 16.8 %collective-permute-start = (bf16[48,24,128]{2,1,0:T(8,128)(2,1)S(1)}, bf16[48,24,128]{2,1,0:T(8,128)(2,1)S(1)}, u32[]{:S(2)}, u32[]{:S(2)}) collective-permute-start(bf16[48,24,128]{2,1,0:T(8,128)(2,1)S(1)} %shard_map.46.refs_0_), channel_id=1, source_target_pairs={{0,1},{1,2},{2,3},{3,4},{4,5},{5,6},{6,7},{7,0},{32,39},{33,32},{3... | collective-permute-start | bytes 884744 | tf_op jit(solution)/shard_map/ppermute | solution.py:309
  24.2 9.1 %collective-permute-start.9 = (bf16[48,24,128]{2,1,0:T(8,128)(2,1)S(1)}, bf16[48,24,128]{2,1,0:T(8,128)(2,1)S(1)}, u32[]{:S(2)}, u32[]{:S(2)}) collective-permute-start(bf16[48,24,128]{2,1,0:T(8,128)(2,1)S(1)} %collective-permute-done.refs_1_), channel_id=1, source_target_pairs={{0,1},{1,2},{2,3},{3,4},{4,5},{5,6},{6,7},{7,0},{32,39},{33,32},{3... | collective-permute-start | bytes 884744 | tf_op jit(solution)/shard_map/ppermute | solution.py:309
  24.7 12.1 %collective-permute-start.10 = (bf16[48,24,128]{2,1,0:T(8,128)(2,1)S(1)}, bf16[48,24,128]{2,1,0:T(8,128)(2,1)S(1)}, u32[]{:S(2)}, u32[]{:S(2)}) collective-permute-start(bf16[48,24,128]{2,1,0:T(8,128)(2,1)S(1)} %collective-permute-done.1.refs_2_), channel_id=1, source_target_pairs={{0,7},{1,0},{2,1},{3,2},{4,3},{5,4},{6,5},{7,6},{32,33},{33,34},{3... | collective-permute-start | bytes 884744 | tf_op jit(solution)/shard_map/ppermute | solution.py:309
  33.4 13.8 %collective-permute-start.11 = (bf16[48,24,128]{2,1,0:T(8,128)(2,1)S(1)}, bf16[48,24,128]{2,1,0:T(8,128)(2,1)S(1)}, u32[]{:S(2)}, u32[]{:S(2)}) collective-permute-start(bf16[48,24,128]{2,1,0:T(8,128)(2,1)S(1)} %collective-permute-done.9.refs_3_), channel_id=1, source_target_pairs={{0,1},{1,2},{2,3},{3,4},{4,5},{5,6},{6,7},{7,0},{32,39},{33,32},{3... | collective-permute-start | bytes 884744 | tf_op jit(solution)/shard_map/ppermute | solution.py:309
  33.8 7.8 %collective-permute-start.4 = (bf16[8,3,24,128]{3,2,1,0:T(8,128)(2,1)S(1)}, bf16[8,3,24,128]{3,2,1,0:T(8,128)(2,1)S(1)}, u32[]{:S(2)}, u32[]{:S(2)}) collective-permute-start(bf16[8,3,24,128]{3,2,1,0:T(8,128)(2,1)S(1)} %all_to_all.5.refs_0_), channel_id=1, source_target_pairs={{0,128},{32,160},{64,192},{96,224},{128,0},{160,32},{192,64},{224,... | collective-permute-start | bytes 442376 | tf_op jit(solution)/shard_map/ppermute | solution.py:309
  36.8 10.9 %collective-permute-start.12 = (bf16[48,24,128]{2,1,0:T(8,128)(2,1)S(1)}, bf16[48,24,128]{2,1,0:T(8,128)(2,1)S(1)}, u32[]{:S(2)}, u32[]{:S(2)}) collective-permute-start(bf16[48,24,128]{2,1,0:T(8,128)(2,1)S(1)} %collective-permute-done.10.refs_4_), channel_id=1, source_target_pairs={{0,7},{1,0},{2,1},{3,2},{4,3},{5,4},{6,5},{7,6},{32,33},{33,34},{3... | collective-permute-start | bytes 884744 | tf_op jit(solution)/shard_map/ppermute | solution.py:309
  39.6 5.1 %collective-permute-start.3 = (bf16[8,3,24,128]{3,2,1,0:T(8,128)(2,1)S(1)}, bf16[8,3,24,128]{3,2,1,0:T(8,128)(2,1)S(1)}, u32[]{:S(2)}, u32[]{:S(2)}) collective-permute-start(bf16[8,3,24,128]{3,2,1,0:T(8,128)(2,1)S(1)} %all_to_all.5.refs_0_), channel_id=1, source_target_pairs={{0,192},{32,96},{64,0},{96,160},{128,64},{160,224},{192,128},{224,... | collective-permute-start | bytes 442376 | tf_op jit(solution)/shard_map/ppermute | solution.py:309
  40.8 6.4 %collective-permute-start.2 = (bf16[8,3,24,128]{3,2,1,0:T(8,128)(2,1)S(1)}, bf16[8,3,24,128]{3,2,1,0:T(8,128)(2,1)S(1)}, u32[]{:S(2)}, u32[]{:S(2)}) collective-permute-start(bf16[8,3,24,128]{3,2,1,0:T(8,128)(2,1)S(1)} %all_to_all.5.refs_0_), channel_id=1, source_target_pairs={{0,64},{32,224},{64,128},{96,32},{128,192},{160,96},{192,0},{224,1... | collective-permute-start | bytes 442376 | tf_op jit(solution)/shard_map/ppermute | solution.py:309
  41.6 6.2 %collective-permute-start.5 = (bf16[8,3,24,128]{3,2,1,0:T(8,128)(2,1)S(1)}, bf16[8,3,24,128]{3,2,1,0:T(8,128)(2,1)S(1)}, u32[]{:S(2)}, u32[]{:S(2)}) collective-permute-start(bf16[8,3,24,128]{3,2,1,0:T(8,128)(2,1)S(1)} %all_to_all.5.refs_0_), channel_id=1, source_target_pairs={{0,32},{32,0},{64,96},{96,64},{128,160},{160,128},{192,224},{224,1... | collective-permute-start | bytes 442376 | tf_op jit(solution)/shard_map/ppermute | solution.py:324
  44.8 6.6 %collective-permute-start.8 = (bf16[8,3,24,128]{3,2,1,0:T(8,128)(2,1)S(1)}, bf16[8,3,24,128]{3,2,1,0:T(8,128)(2,1)S(1)}, u32[]{:S(2)}, u32[]{:S(2)}) collective-permute-start(bf16[8,3,24,128]{3,2,1,0:T(8,128)(2,1)S(1)} %collective-permute-done.4.refs_3_), channel_id=1, source_target_pairs={{0,32},{32,0},{64,96},{96,64},{128,160},{160,128},{192,224},{224,1... | collective-permute-start | bytes 442376 | tf_op jit(solution)/shard_map/ppermute | solution.py:325
  47.1 4.2 %collective-permute-start.7 = (bf16[8,3,24,128]{3,2,1,0:T(8,128)(2,1)S(1)}, bf16[8,3,24,128]{3,2,1,0:T(8,128)(2,1)S(1)}, u32[]{:S(2)}, u32[]{:S(2)}) collective-permute-start(bf16[8,3,24,128]{3,2,1,0:T(8,128)(2,1)S(1)} %collective-permute-done.3.refs_2_), channel_id=1, source_target_pairs={{0,32},{32,0},{64,96},{96,64},{128,160},{160,128},{192,224},{224,1... | collective-permute-start | bytes 442376 | tf_op jit(solution)/shard_map/ppermute | solution.py:324
  47.1 4.2 %collective-permute-start.6 = (bf16[8,3,24,128]{3,2,1,0:T(8,128)(2,1)S(1)}, bf16[8,3,24,128]{3,2,1,0:T(8,128)(2,1)S(1)}, u32[]{:S(2)}, u32[]{:S(2)}) collective-permute-start(bf16[8,3,24,128]{3,2,1,0:T(8,128)(2,1)S(1)} %collective-permute-done.2.refs_1_), channel_id=1, source_target_pairs={{0,32},{32,0},{64,96},{96,64},{128,160},{160,128},{192,224},{224,1... | collective-permute-start | bytes 442376 | tf_op jit(solution)/shard_map/ppermute | solution.py:324
  47.7 9.2 %collective-permute-start.13 = (bf16[24,24,128]{2,1,0:T(8,128)(2,1)S(1)}, bf16[24,24,128]{2,1,0:T(8,128)(2,1)S(1)}, u32[]{:S(2)}, u32[]{:S(2)}) collective-permute-start(bf16[24,24,128]{2,1,0:T(8,128)(2,1)S(1)} %slice.16), channel_id=1, source_target_pairs={{0,1},{1,2},{2,3},{3,4},{4,5},{5,6},{6,7},{7,0},{32,39},{33,32},{3... | collective-permute-start | bytes 442376 | tf_op jit(solution)/shard_map/ppermute | solution.py:309
  47.9 9.1 %collective-permute-start.14 = (bf16[24,24,128]{2,1,0:T(8,128)(2,1)S(1)}, bf16[24,24,128]{2,1,0:T(8,128)(2,1)S(1)}, u32[]{:S(2)}, u32[]{:S(2)}) collective-permute-start(bf16[24,24,128]{2,1,0:T(8,128)(2,1)S(1)} %slice.17), channel_id=1, source_target_pairs={{0,7},{1,0},{2,1},{3,2},{4,3},{5,4},{6,5},{7,6},{32,33},{33,34},{3... | collective-permute-start | bytes 442376 | tf_op jit(solution)/shard_map/ppermute | solution.py:309
  64.4 8.4 %collective-permute-start.19 = (f32[44,1104]{1,0:T(8,128)S(1)}, f32[44,1104]{1,0:T(8,128)S(1)}, u32[]{:S(2)}, u32[]{:S(2)}) collective-permute-start(f32[44,1104]{1,0:T(8,128)S(1)} %get-tuple-element.28), channel_id=1, source_target_pairs={{0,24},{8,0},{16,8},{24,16},{32,40},{40,48},{48,56},{56,32},{64,88... | collective-permute-start | bytes 582920 | tf_op jit(solution)/shard_map/ppermute | solution.py:309
  65.0 9.4 %collective-permute-start.16 = (f32[48,1104]{1,0:T(8,128)S(1)}, f32[48,1104]{1,0:T(8,128)S(1)}, u32[]{:S(2)}, u32[]{:S(2)}) collective-permute-start(f32[48,1104]{1,0:T(8,128)S(1)} %get-tuple-element.25), channel_id=1, source_target_pairs={{0,8},{8,16},{16,24},{24,0},{32,56},{40,32},{48,40},{56,48},{64,72... | collective-permute-start | bytes 635912 | tf_op jit(solution)/shard_map/ppermute | solution.py:309
  66.5 9.8 %collective-permute-start.18 = (f32[44,1104]{1,0:T(8,128)S(1)}, f32[44,1104]{1,0:T(8,128)S(1)}, u32[]{:S(2)}, u32[]{:S(2)}) collective-permute-start(f32[44,1104]{1,0:T(8,128)S(1)} %get-tuple-element.26), channel_id=1, source_target_pairs={{0,8},{8,16},{16,24},{24,0},{32,56},{40,32},{48,40},{56,48},{64,72... | collective-permute-start | bytes 582920 | tf_op jit(solution)/shard_map/ppermute | solution.py:309
  72.8 6.5 %collective-permute-start.20 = (f32[44,1104]{1,0:T(8,128)S(1)}, f32[44,1104]{1,0:T(8,128)S(1)}, u32[]{:S(2)}, u32[]{:S(2)}) collective-permute-start(f32[44,1104]{1,0:T(8,128)S(1)} %add.28), channel_id=1, source_target_pairs={{0,24},{8,0},{16,8},{24,16},{32,40},{40,48},{48,56},{56,32},{64,88... | collective-permute-start | bytes 582920 | tf_op jit(solution)/shard_map/ppermute | solution.py:309
  73.4 8.3 %collective-permute-start.15 = (f32[48,1104]{1,0:T(8,128)S(1)}, f32[48,1104]{1,0:T(8,128)S(1)}, u32[]{:S(2)}, u32[]{:S(2)}) collective-permute-start(f32[48,1104]{1,0:T(8,128)S(1)} %get-tuple-element.23), channel_id=1, source_target_pairs={{0,24},{8,0},{16,8},{24,16},{32,40},{40,48},{48,56},{56,32},{64,88... | collective-permute-start | bytes 635912 | tf_op jit(solution)/shard_map/ppermute | solution.py:309
  74.4 7.7 %collective-permute-start.17 = (f32[48,1104]{1,0:T(8,128)S(1)}, f32[48,1104]{1,0:T(8,128)S(1)}, u32[]{:S(2)}, u32[]{:S(2)}) collective-permute-start(f32[48,1104]{1,0:T(8,128)S(1)} %add.25), channel_id=1, source_target_pairs={{0,8},{8,16},{16,24},{24,0},{32,56},{40,32},{48,40},{56,48},{64,72... | collective-permute-start | bytes 635912 | tf_op jit(solution)/shard_map/ppermute | solution.py:309
  82.1 11.1 %collective-permute-start.21 = (bf16[92,1104]{1,0:T(8,128)(2,1)S(1)}, bf16[92,1104]{1,0:T(8,128)(2,1)S(1)}, u32[]{:S(2)}, u32[]{:S(2)}) collective-permute-start(bf16[92,1104]{1,0:T(8,128)(2,1)S(1)} %pad_maximum_fusion), channel_id=1, source_target_pairs={{0,0},{1,9},{2,18},{3,27},{4,31},{5,22},{6,13},{7,4},{8,1},{9,8},{... | collective-permute-start | bytes 609416 | tf_op jit(solution)/shard_map/ppermute | solution.py:298

commit v7 on v6

--- a/solution.py
+++ b/solution.py
@@ -22,7 +22,6 @@
 WIDE = 4 * CHUNK
 ROWS = 48
 SPANS = ((0, 92), (96, 144), (144, 188), (192, 240), (240, 284), (288, 336), (336, 380))
-STARTS = (0, 8, 16, 24, 32, 40, 48, 56)
 OFFSETS = (0, 7, 1, 6, 2, 5, 3, 4)
 
 
@@ -146,21 +145,21 @@
     )
 
 
-def fill_kernel(meta_ref, *refs):
-    rights, (wide_ref, table_ref) = refs[:-7], refs[-7:-5]
+def fill_kernel(theirs, meta_ref, *refs):
+    rights, refs = refs[:4], refs[4 + theirs :]
+    wide_ref, refs = refs[0], refs[1:]
     right_ref, mixed_ref, turned_ref, codes_ref, sem = refs[-5:]
     depth, core, side, col = (meta_ref[m] for m in range(4))
+    owner = lax.bitwise_xor(core, theirs)
     for source, piece in enumerate(rights):
         count = piece.shape[0]
-        start = STARTS[source]
+        start = source * GROUP
         right_ref[start : start + count] = piece[...]
         for n in range(count):
             for u in range(USLOTS):
                 row = (start + n) * USLOTS + u
                 mixed_ref[row : row + 1, :] = piece[n, u, BLK : BLK + 1, :].astype(jnp.float32)
-    codes = jnp.concatenate(
-        [mixed_ref[h * LANES : (h + 1) * LANES, :].T[0:8, :] for h in range(2)], axis=1
-    ).astype(jnp.int32)
+    codes = mixed_ref[...].T[0:8, :].astype(jnp.int32)
     local = codes - 16 * lax.shift_right_logical(depth, 2)
     chunk = lax.bitwise_xor(lax.shift_right_arithmetic(local, 2), lax.bitwise_xor(depth, 7 * (depth >> 2)) & 3)
     at = CHUNK * (((chunk - col) * (1 - 2 * core)) & 3) + BLK * (local & 3)
@@ -169,14 +168,14 @@
     turned_ref[8:16, :] = (at + 4 * LANES - BLK * lax.broadcasted_iota(jnp.int32, at.shape, 0)) & (LANES - 1)
     copy = pltpu.make_async_copy(turned_ref, codes_ref, sem)
     copy.start()
-    table_ref[...] = mixed_ref[0 : GROUP * USLOTS, :].astype(jnp.int32)
+    if not theirs:
+        refs[0][...] = mixed_ref[0 : GROUP * USLOTS, :].astype(jnp.int32)
     lanes = [lax.broadcasted_iota(jnp.int32, (8, LANES), 1) + q * LANES for q in range(3)]
     blank = jnp.zeros((8, LANES), jnp.float32)
     copy.wait()
 
     def fill(n, carry):
-        j = lax.shift_right_logical(n, 3) & 3
-        owner = lax.bitwise_xor(core, lax.shift_right_logical(n, 5))
+        j = lax.shift_right_logical(n, 3)
         x = side + (1 - 2 * owner) * jnp.where(j == 1, 3, j - lax.shift_right_logical(j, 1))
         row = 2 * (x & 3) + owner
         spot = n & 7
@@ -196,29 +195,32 @@
                 wide_ref[base + k, q] = jnp.concatenate(z[q] + [blank], axis=0).astype(jnp.bfloat16)
         return carry
 
-    lax.fori_loop(0, 8 * GROUP, fill, 0, unroll=4)
-
-
-def fill(meta, rights):
+    lax.fori_loop(0, 4 * GROUP, fill, 0, unroll=8)
+
+
+def fill(meta, rights, wide=None):
     vmem = pl.BlockSpec(memory_space=pltpu.VMEM)
+    theirs = 0 if wide is None else 1
+    shapes = (
+        jax.ShapeDtypeStruct((GROUP * PANEL, 3, KROW, LANES), jnp.bfloat16),
+        jax.ShapeDtypeStruct((GROUP * USLOTS, LANES), jnp.int32),
+    )
     return pl.pallas_call(
-        fill_kernel,
-        out_shape=(
-            jax.ShapeDtypeStruct((GROUP * PANEL, 3, KROW, LANES), jnp.bfloat16),
-            jax.ShapeDtypeStruct((GROUP * USLOTS, LANES), jnp.int32),
-        ),
-        in_specs=[pl.BlockSpec(memory_space=pltpu.SMEM)] + [vmem] * len(rights),
-        out_specs=(vmem, vmem),
+        functools.partial(fill_kernel, theirs),
+        out_shape=shapes[: 2 - theirs],
+        in_specs=[pl.BlockSpec(memory_space=pltpu.SMEM)] + [vmem] * (4 + theirs),
+        out_specs=(vmem, vmem)[: 2 - theirs],
         scratch_shapes=[
-            pltpu.VMEM((8 * GROUP, USLOTS, APAD, LANES), jnp.bfloat16),
-            pltpu.VMEM((2 * LANES, LANES), jnp.float32),
-            pltpu.VMEM((16, 2 * LANES), jnp.int32),
-            pltpu.SMEM((16, 2 * LANES), jnp.int32),
+            pltpu.VMEM((4 * GROUP, USLOTS, APAD, LANES), jnp.bfloat16),
+            pltpu.VMEM((LANES, LANES), jnp.float32),
+            pltpu.VMEM((16, LANES), jnp.int32),
+            pltpu.SMEM((16, LANES), jnp.int32),
             pltpu.SemaphoreType.DMA,
         ],
-        compiler_params=pltpu.CompilerParams(vmem_limit_bytes=16 * 1024 * 1024),
-        cost_estimate=pl.CostEstimate(flops=3_000_000_000, bytes_accessed=8_000_000, transcendentals=0),
-    )(meta, *rights)
+        input_output_aliases={5: 0} if theirs else {},
+        compiler_params=pltpu.CompilerParams(vmem_limit_bytes=10 * 1024 * 1024),
+        cost_estimate=pl.CostEstimate(flops=1_500_000_000, bytes_accessed=4_000_000, transcendentals=0),
+    )(meta, *rights, *([wide] if theirs else []))
 
 
 def picked(meta_ref, table_ref, wide_ref, offsets, i):
@@ -232,50 +234,41 @@
     return jnp.concatenate([jnp.concatenate([wide_ref[n, q] for n in at], axis=0) for q in range(3)], axis=1)
 
 
-def product_kernel(start, count, meta_ref, table_ref, wide_ref, *refs):
-    lefts, outs, (sum_ref, part_ref) = refs[:9], refs[9:16], refs[16:]
-
-    def steps(first, last, far_ref, skip):
-        def step(g, carry):
-            for m in range(8):
-                i = g * 8 + m
-                weights = picked(meta_ref, table_ref, wide_ref, OFFSETS, i)
-                rows = jnp.concatenate([x[i] for x in lefts[:7]] + [far_ref[i - skip]], axis=1)
-                part_ref[m * BLK : m * BLK + APAD, :] = jnp.dot(rows, weights, preferred_element_type=jnp.float32)
-            at = pl.multiple_of((g - start) * 8 * BLK, 8)
-            sum_ref[pl.ds(at, 8 * BLK), :] = part_ref[0 : 8 * BLK, :]
-            return carry
-
-        lax.fori_loop(first, last, step, 0)
-
-    if start < 3:
-        steps(start, min(3, start + count), lefts[7], 0)
-    if start + count > 3:
-        steps(max(3, start), start + count, lefts[8], ROWS // 2)
-    width = count * 8 * BLK
+def product_kernel(meta_ref, table_ref, wide_ref, *refs):
+    lefts, outs, (sum_ref, part_ref) = refs[:GROUP], refs[GROUP : GROUP + 7], refs[GROUP + 7 :]
+
+    def step(g, carry):
+        for m in range(8):
+            i = g * 8 + m
+            weights = picked(meta_ref, table_ref, wide_ref, OFFSETS, i)
+            rows = jnp.concatenate([x[i] for x in lefts], axis=1)
+            part_ref[m * BLK : m * BLK + APAD, :] = jnp.dot(rows, weights, preferred_element_type=jnp.float32)
+        sum_ref[pl.ds(pl.multiple_of(g * 8 * BLK, 8), 8 * BLK), :] = part_ref[0 : 8 * BLK, :]
+        return carry
+
+    lax.fori_loop(0, ROWS // 8, step, 0)
     for q in range(3):
-        turned = sum_ref[:, q * LANES : (q + 1) * LANES].T[:, :width]
+        turned = sum_ref[:, q * LANES : (q + 1) * LANES].T[:, : ROWS * BLK]
         for ref, (first, last) in zip(outs, SPANS):
             low, high = max(first, q * LANES), min(last, (q + 1) * LANES)
             if low < high:
                 ref[low - first : high - first, :] = turned[low - q * LANES : high - q * LANES]
 
 
-def product(meta, table, wide, lefts, start, count):
+def product(meta, table, wide, lefts):
     vmem = pl.BlockSpec(memory_space=pltpu.VMEM)
     smem = pl.BlockSpec(memory_space=pltpu.SMEM)
-    width = count * 8 * BLK
     return pl.pallas_call(
-        functools.partial(product_kernel, start, count),
-        out_shape=tuple(jax.ShapeDtypeStruct((b - a, width), jnp.float32) for a, b in SPANS),
+        product_kernel,
+        out_shape=tuple(jax.ShapeDtypeStruct((b - a, ROWS * BLK), jnp.float32) for a, b in SPANS),
         in_specs=[smem, smem, vmem] + [vmem] * len(lefts),
         out_specs=(vmem,) * len(SPANS),
         scratch_shapes=[
-            pltpu.VMEM((-(-width // LANES) * LANES, WIDE), jnp.float32),
+            pltpu.VMEM((9 * LANES, WIDE), jnp.float32),
             pltpu.VMEM((8 * APAD, WIDE), jnp.float32),
         ],
         compiler_params=pltpu.CompilerParams(vmem_limit_bytes=8 * 1024 * 1024),
-        cost_estimate=pl.CostEstimate(flops=count * 1_000_000_000, bytes_accessed=8_000_000, transcendentals=0),
+        cost_estimate=pl.CostEstimate(flops=6_000_000_000, bytes_accessed=8_000_000, transcendentals=0),
     )(meta, table, wide, *lefts)
 
 
@@ -324,11 +317,11 @@
     others = [lax.ppermute(x, "row", swap) for x in (right, f1, b1)]
     others += [lax.ppermute(f2, "row", swap)]
     up3, down3 = shift(up2, "depth", 1, 8), shift(down2, "depth", -1, 8)
-    edge = ROWS // 2
-    up4, down4 = shift(up3[:edge], "depth", 1, 8), shift(down3[edge:], "depth", -1, 8)
-    lefts = [left, up1, down1, up2, down2, up3, down3, up4, down4]
-    wide, table = fill(meta, [right, f1, b1, f2] + others)
-    parts = product(meta, table, wide, lefts, 0, 6)
+    up4 = shift(up3, "depth", 1, 8)
+    lefts = [left, up1, down1, up2, down2, up3, down3, up4]
+    wide, table = fill(meta, [right, f1, b1, f2])
+    (wide,) = fill(meta, others, wide)
+    parts = product(meta, table, wide, lefts)
     return summed(parts).T
 
 

time: 94.3 us -> 91.8 us (0.973)
  starting transfers between devices: 30.8 us -> 27.6 us
    ppermute x17 -> x16, starting transfers between devices: 28.4 us -> 23.9 us  [shift(): return lax.ppermute(x, axis if axis == 'row' else ('row', axis), pairs)]
    ppermute x1, waiting for transfers between devices: 9.17 us -> 7.91 us  [summed(): return lax.ppermute(done, ('col', 'depth'), home)]
    ppermute x1, starting transfers between devices: 1.92 us -> 3.18 us  [summed(): return lax.ppermute(done, ('col', 'depth'), home)]
    pallas_call x2 -> x3, Pallas kernels: 13.1 us -> 13.5 us  [the longest x1 7.39 us: product(): pl.pallas_call(product_kernel, out_shape=tuple((jax.ShapeDtypeStruct((b -...]
    ppermute x17 -> x16, waiting for transfers between devices: 21.6 us -> 21.9 us  [shift(): return lax.ppermute(x, axis if axis == 'row' else ('row', axis), pairs)]
  transfers between devices with their start and end apart: 22 -> 21, of which waited for: 9 -> 11; matrix products, arithmetic and copies ran while one was open for 0% -> 0% of each run, Pallas kernels for 8% -> 9%
where the time goes in v7:
time: 91.8 us; the launch traced here: 90.5 us
  waiting for transfers between devices  29.8 us (32%)
  starting transfers between devices  27.6 us (30%)
  Pallas kernels  16.1 us (18%)
  blocking collectives  15 us (16%)
  local copies, waits for them, and re-layouts  1.63 us (2%)
    ppermute x16, starting transfers between devices, shift(): return lax.ppermute(x, axis if axis == 'row' else ('row', axis), pairs)  23.9 us
    ppermute x16, waiting for transfers between devices, shift(): return lax.ppermute(x, axis if axis == 'row' else ('row', axis), pairs)  21.9 us
    all_to_all x1, blocking collectives, body(): right = lax.all_to_all(tiles, 'depth', 0, 0)  15 us
    ppermute x1, waiting for transfers between devices, summed(): return lax.ppermute(done, ('col', 'depth'), home)  7.91 us
    pallas_call x1, Pallas kernels, product(): pl.pallas_call(product_kernel, out_shape=tuple((jax.ShapeDtypeStruct((b -...  7.39 us
    pallas_call x2, Pallas kernels, fill(): pl.pallas_call(functools.partial(fill_kernel, theirs), out_shape=shapes[:...  6.13 us
    ppermute x1, starting transfers between devices, summed(): return lax.ppermute(done, ('col', 'depth'), home)  3.18 us
    pallas_call x1, Pallas kernels, pack_right(): pl.pallas_call(pack_right_kernel, out_shape=jax.ShapeDtypeStruct((GROUP,...  2.09 us
  transfers between devices with their start and end apart: 21, of which 11 were waited for; matrix products, arithmetic and copies ran while one was open for 0% of the time, Pallas kernels for 9%

profile of v7, /device:TPU:16, one launch (start us, length us, event | category | flops | bytes accessed | tf_op | source)
XLA Modules:
  0.0 90.5 jit_solution(2315923409119592734)
XLA Ops:
  0.0 0.9 %copy-done = bf16[48,1,4,529]{3,2,1,0:T(4,128)(2,1)S(1)} copy-done((bf16[48,1,4,529]{3,2,1,0:T(4,128)(2,1)S(1)}, bf16[48,1,4,529]{3,2,1,0:T(4,128)(2,1)}, u32[]{:S(2)}) %copy-start) | copy-done | bytes 203160
  0.9 0.5 shard_map.46.refs_0_
  1.5 2.0 %collective-permute-start = (bf16[48,24,128]{2,1,0:T(8,128)(2,1)S(1)}, bf16[48,24,128]{2,1,0:T(8,128)(2,1)S(1)}, u32[]{:S(2)}, u32[]{:S(2)}) collective-permute-start(bf16[48,24,128]{2,1,0:T(8,128)(2,1)S(1)} %shard_map.46.refs_0_), channel_id=1, source_target_pairs={{0,1},{1,2},{2,3},{3,4},{4,5},{5,6},{6,7},{7,0},{32,39},{33,32},{3... | collective-permute-start | bytes 884744 | tf_op jit(solution)/shard_map/ppermute | solution.py:302
  3.4 4.0 %collective-permute-start.1 = (bf16[48,24,128]{2,1,0:T(8,128)(2,1)S(1)}, bf16[48,24,128]{2,1,0:T(8,128)(2,1)S(1)}, u32[]{:S(2)}, u32[]{:S(2)}) collective-permute-start(bf16[48,24,128]{2,1,0:T(8,128)(2,1)S(1)} %shard_map.46.refs_0_), channel_id=1, source_target_pairs={{0,7},{1,0},{2,1},{3,2},{4,3},{5,4},{6,5},{7,6},{32,33},{33,34},{3... | collective-permute-start | bytes 884744 | tf_op jit(solution)/shard_map/ppermute | solution.py:302
  7.5 2.1 %shard_map.47 = bf16[8,3,24,128]{3,2,1,0:T(8,128)(2,1)} custom-call(bf16[5,3,4,529]{3,2,1,0:T(4,128)(2,1)} %bitcast.17, s32[3,4,5]{2,1,0:T(4,128)} %bitcast.18, s32[4,48]{1,0:T(4,128)} %bitcast.19), custom_call_target="tpu_custom_call" | custom-call | tf_op jit(solution)/shard_map/pallas_call | solution.py:127
  9.6 15.0 %all_to_all.5.refs_0_ = bf16[8,3,24,128]{3,2,1,0:T(8,128)(2,1)S(1)} all-to-all(bf16[8,3,24,128]{3,2,1,0:T(8,128)(2,1)} %shard_map.47), channel_id=1, replica_groups=mesh['row'=8,'col'=4,'depth'=8] {'depth'}, dimensions={0} | all-to-all | bytes 294912 | tf_op jit(solution)/shard_map/all_to_all | solution.py:310
  24.6 0.0 collective-permute-done.refs_1_
  24.6 0.8 collective-permute-start.9
  25.4 1.5 %collective-permute-start.2 = (bf16[8,3,24,128]{3,2,1,0:T(8,128)(2,1)S(1)}, bf16[8,3,24,128]{3,2,1,0:T(8,128)(2,1)S(1)}, u32[]{:S(2)}, u32[]{:S(2)}) collective-permute-start(bf16[8,3,24,128]{3,2,1,0:T(8,128)(2,1)S(1)} %all_to_all.5.refs_0_), channel_id=1, source_target_pairs={{0,64},{32,224},{64,128},{96,32},{128,192},{160,96},{192,0},{224,1... | collective-permute-start | bytes 442376 | tf_op jit(solution)/shard_map/ppermute | solution.py:302
  26.9 2.6 %collective-permute-start.10 = (bf16[48,24,128]{2,1,0:T(8,128)(2,1)S(1)}, bf16[48,24,128]{2,1,0:T(8,128)(2,1)S(1)}, u32[]{:S(2)}, u32[]{:S(2)}) collective-permute-start(bf16[48,24,128]{2,1,0:T(8,128)(2,1)S(1)} %collective-permute-done.1.refs_2_), channel_id=1, source_target_pairs={{0,7},{1,0},{2,1},{3,2},{4,3},{5,4},{6,5},{7,6},{32,33},{33,34},{3... | collective-permute-start | bytes 884744 | tf_op jit(solution)/shard_map/ppermute | solution.py:302
  29.5 4.4 %collective-permute-done.9.refs_3_ = bf16[48,24,128]{2,1,0:T(8,128)(2,1)S(1)} collective-permute-done((bf16[48,24,128]{2,1,0:T(8,128)(2,1)S(1)}, bf16[48,24,128]{2,1,0:T(8,128)(2,1)S(1)}, u32[]{:S(2)}, u32[]{:S(2)}) %collective-permute-start.9) | collective-permute-done | bytes 294944 | tf_op jit(solution)/shard_map/ppermute | solution.py:302
  33.9 0.5 collective-permute-start.11
  34.4 0.9 %collective-permute-start.3 = (bf16[8,3,24,128]{3,2,1,0:T(8,128)(2,1)S(1)}, bf16[8,3,24,128]{3,2,1,0:T(8,128)(2,1)S(1)}, u32[]{:S(2)}, u32[]{:S(2)}) collective-permute-start(bf16[8,3,24,128]{3,2,1,0:T(8,128)(2,1)S(1)} %all_to_all.5.refs_0_), channel_id=1, source_target_pairs={{0,192},{32,96},{64,0},{96,160},{128,64},{160,224},{192,128},{224,... | collective-permute-start | bytes 442376 | tf_op jit(solution)/shard_map/ppermute | solution.py:302
  35.3 1.0 %collective-permute-start.4 = (bf16[8,3,24,128]{3,2,1,0:T(8,128)(2,1)S(1)}, bf16[8,3,24,128]{3,2,1,0:T(8,128)(2,1)S(1)}, u32[]{:S(2)}, u32[]{:S(2)}) collective-permute-start(bf16[8,3,24,128]{3,2,1,0:T(8,128)(2,1)S(1)} %all_to_all.5.refs_0_), channel_id=1, source_target_pairs={{0,128},{32,160},{64,192},{96,224},{128,0},{160,32},{192,64},{224,... | collective-permute-start | bytes 442376 | tf_op jit(solution)/shard_map/ppermute | solution.py:302
  36.3 0.0 collective-permute-done.2.refs_1_
  36.3 0.0 collective-permute-start.5
  36.3 3.2 %collective-permute-done.3.refs_2_ = bf16[8,3,24,128]{3,2,1,0:T(8,128)(2,1)S(1)} collective-permute-done((bf16[8,3,24,128]{3,2,1,0:T(8,128)(2,1)S(1)}, bf16[8,3,24,128]{3,2,1,0:T(8,128)(2,1)S(1)}, u32[]{:S(2)}, u32[]{:S(2)}) %collective-permute-start.3) | collective-permute-done | bytes 147488 | tf_op jit(solution)/shard_map/ppermute | solution.py:302
  39.5 0.0 collective-permute-start.6
  39.5 2.4 %collective-permute-done.4.refs_3_ = bf16[8,3,24,128]{3,2,1,0:T(8,128)(2,1)S(1)} collective-permute-done((bf16[8,3,24,128]{3,2,1,0:T(8,128)(2,1)S(1)}, bf16[8,3,24,128]{3,2,1,0:T(8,128)(2,1)S(1)}, u32[]{:S(2)}, u32[]{:S(2)}) %collective-permute-start.4) | collective-permute-done | bytes 147488 | tf_op jit(solution)/shard_map/ppermute | solution.py:302
  42.0 0.0 collective-permute-start.7
  42.0 0.5 collective-permute-start.8
  42.5 3.2 %collective-permute-start.12 = (bf16[48,24,128]{2,1,0:T(8,128)(2,1)S(1)}, bf16[48,24,128]{2,1,0:T(8,128)(2,1)S(1)}, u32[]{:S(2)}, u32[]{:S(2)}) collective-permute-start(bf16[48,24,128]{2,1,0:T(8,128)(2,1)S(1)} %collective-permute-done.10.refs_4_), channel_id=1, source_target_pairs={{0,7},{1,0},{2,1},{3,2},{4,3},{5,4},{6,5},{7,6},{32,33},{33,34},{3... | collective-permute-start | bytes 884744 | tf_op jit(solution)/shard_map/ppermute | solution.py:302
  45.7 0.0 collective-permute-done.11.refs_5_
  45.7 0.0 collective-permute-start.13
  45.7 0.1 pad_add_fusion.meta_ref
  45.8 3.1 %shard_map.48 = (bf16[320,3,32,128]{3,2,1,0:T(8,128)(2,1)S(1)}, s32[24,128]{1,0:T(8,128)S(1)}) custom-call(s32[4]{0:T(128)S(1)} %pad_add_fusion.meta_ref, bf16[8,3,24,128]{3,2,1,0:T(8,128)(2,1)S(1)} %all_to_all.5.refs_0_, bf16[8,3,24,128]{3,2,1,0:T(8,128)(2,1)S(1)} %collective-permute-done.2.refs_1_, ...), custom_call_target="tpu_custom_call" | custom-call | flops 1500000000 | bytes 4000000 | tf_op jit(solution)/shard_map/pallas_call | solution.py:208
  48.9 0.0 collective-permute-done.7.refs_2_
  48.9 0.0 collective-permute-done.8.refs_3_
  48.9 3.1 %shard_map.49.wide_ref = bf16[320,3,32,128]{3,2,1,0:T(8,128)(2,1)S(1)} custom-call(s32[4]{0:T(128)S(1)} %pad_add_fusion.meta_ref, bf16[8,3,24,128]{3,2,1,0:T(8,128)(2,1)S(1)} %collective-permute-done.5.refs_0_, bf16[8,3,24,128]{3,2,1,0:T(8,128)(2,1)S(1)} %collective-permute-done.6.refs_1_, ...), custom_call_target="tpu_custom_call", output_to_operand_aliasing={{}: (5, {})} | custom-call | flops 1500000000 | bytes 4000000 | tf_op jit(solution)/shard_map/pallas_call | solution.py:208
  52.0 0.5 collective-permute-done.12.refs_6_
  52.5 1.1 %collective-permute-done.13.refs_7_ = bf16[48,24,128]{2,1,0:T(8,128)(2,1)S(1)} collective-permute-done((bf16[48,24,128]{2,1,0:T(8,128)(2,1)S(1)}, bf16[48,24,128]{2,1,0:T(8,128)(2,1)S(1)}, u32[]{:S(2)}, u32[]{:S(2)}) %collective-permute-start.13) | collective-permute-done | bytes 294944 | tf_op jit(solution)/shard_map/ppermute | solution.py:302
  53.7 7.4 %shard_map.50 = (f32[92,1104]{1,0:T(8,128)S(1)}, f32[48,1104]{1,0:T(8,128)S(1)}, f32[44,1104]{1,0:T(8,128)S(1)}, f32[48,1104]{1,0:T(8,128)S(1)}, f32[44,1104]{1,...) custom-call(s32[4]{0:T(128)S(1)} %pad_add_fusion.meta_ref, s32[24,128]{1,0:T(8,128)S(1)} %get-tuple-element.18.table_ref, ...), custom_call_target="tpu_custom_call" | custom-call | flops 6000000000 | bytes 8000000 | tf_op jit(solution)/shard_map/pallas_call | solution.py:261
  61.1 0.5 collective-permute-start.18
  61.6 1.6 %collective-permute-start.15 = (f32[48,1104]{1,0:T(8,128)S(1)}, f32[48,1104]{1,0:T(8,128)S(1)}, u32[]{:S(2)}, u32[]{:S(2)}) collective-permute-start(f32[48,1104]{1,0:T(8,128)S(1)} %get-tuple-element.25), channel_id=1, source_target_pairs={{0,8},{8,16},{16,24},{24,0},{32,56},{40,32},{48,40},{56,48},{64,72... | collective-permute-start | bytes 635912 | tf_op jit(solution)/shard_map/ppermute | solution.py:302
  63.2 2.5 %collective-permute-start.17 = (f32[44,1104]{1,0:T(8,128)S(1)}, f32[44,1104]{1,0:T(8,128)S(1)}, u32[]{:S(2)}, u32[]{:S(2)}) collective-permute-start(f32[44,1104]{1,0:T(8,128)S(1)} %get-tuple-element.26), channel_id=1, source_target_pairs={{0,8},{8,16},{16,24},{24,0},{32,56},{40,32},{48,40},{56,48},{64,72... | collective-permute-start | bytes 582920 | tf_op jit(solution)/shard_map/ppermute | solution.py:302
  65.7 3.8 %collective-permute-done.18 = f32[44,1104]{1,0:T(8,128)S(1)} collective-permute-done((f32[44,1104]{1,0:T(8,128)S(1)}, f32[44,1104]{1,0:T(8,128)S(1)}, u32[]{:S(2)}, u32[]{:S(2)}) %collective-permute-start.18) | collective-permute-done | bytes 194336 | tf_op jit(solution)/shard_map/ppermute | solution.py:302
  69.5 0.5 collective-permute-start.19
  70.0 1.0 %collective-permute-start.14 = (f32[48,1104]{1,0:T(8,128)S(1)}, f32[48,1104]{1,0:T(8,128)S(1)}, u32[]{:S(2)}, u32[]{:S(2)}) collective-permute-start(f32[48,1104]{1,0:T(8,128)S(1)} %get-tuple-element.23), channel_id=1, source_target_pairs={{0,24},{8,0},{16,8},{24,16},{32,40},{40,48},{48,56},{56,32},{64,88... | collective-permute-start | bytes 635912 | tf_op jit(solution)/shard_map/ppermute | solution.py:302
  71.0 0.0 collective-permute-done.15
  71.0 1.3 %collective-permute-start.16 = (f32[48,1104]{1,0:T(8,128)S(1)}, f32[48,1104]{1,0:T(8,128)S(1)}, u32[]{:S(2)}, u32[]{:S(2)}) collective-permute-start(f32[48,1104]{1,0:T(8,128)S(1)} %add.25), channel_id=1, source_target_pairs={{0,8},{8,16},{16,24},{24,0},{32,56},{40,32},{48,40},{56,48},{64,72... | collective-permute-start | bytes 635912 | tf_op jit(solution)/shard_map/ppermute | solution.py:302
  72.3 0.5 collective-permute-done.17
  72.7 3.2 %collective-permute-done.19 = f32[44,1104]{1,0:T(8,128)S(1)} collective-permute-done((f32[44,1104]{1,0:T(8,128)S(1)}, f32[44,1104]{1,0:T(8,128)S(1)}, u32[]{:S(2)}, u32[]{:S(2)}) %collective-permute-start.19) | collective-permute-done | bytes 194336 | tf_op jit(solution)/shard_map/ppermute | solution.py:302
  75.9 0.1 add_convert_fusion
  76.0 2.3 %collective-permute-done.14 = f32[48,1104]{1,0:T(8,128)S(1)} collective-permute-done((f32[48,1104]{1,0:T(8,128)S(1)}, f32[48,1104]{1,0:T(8,128)S(1)}, u32[]{:S(2)}, u32[]{:S(2)}) %collective-permute-start.14) | collective-permute-done | bytes 212000 | tf_op jit(solution)/shard_map/ppermute | solution.py:302
  78.3 0.4 collective-permute-done.16
  78.8 3.2 %collective-permute-start.20 = (bf16[92,1104]{1,0:T(8,128)(2,1)S(1)}, bf16[92,1104]{1,0:T(8,128)(2,1)S(1)}, u32[]{:S(2)}, u32[]{:S(2)}) collective-permute-start(bf16[92,1104]{1,0:T(8,128)(2,1)S(1)} %pad_maximum_fusion), channel_id=1, source_target_pairs={{0,0},{1,9},{2,18},{3,27},{4,31},{5,22},{6,13},{7,4},{8,1},{9,8},{... | collective-permute-start | bytes 609416 | tf_op jit(solution)/shard_map/ppermute | solution.py:291
  81.9 7.9 %collective-permute-done.20 = bf16[92,1104]{1,0:T(8,128)(2,1)S(1)} collective-permute-done((bf16[92,1104]{1,0:T(8,128)(2,1)S(1)}, bf16[92,1104]{1,0:T(8,128)(2,1)S(1)}, u32[]{:S(2)}, u32[]{:S(2)}) %collective-permute-start.20) | collective-permute-done | bytes 203168 | tf_op jit(solution)/shard_map/ppermute | solution.py:291
  89.9 0.7 copy.8
  (9 shorter events, 0.1 us)
Async XLA Ops:
  0.0 0.9 %copy-start = (bf16[48,1,4,529]{3,2,1,0:T(4,128)(2,1)S(1)}, bf16[48,1,4,529]{3,2,1,0:T(4,128)(2,1)}, u32[]{:S(2)}) copy-start(bf16[48,1,4,529]{3,2,1,0:T(4,128)(2,1)} %param.4) | copy-start | bytes 609412
  1.5 23.1 %collective-permute-start = (bf16[48,24,128]{2,1,0:T(8,128)(2,1)S(1)}, bf16[48,24,128]{2,1,0:T(8,128)(2,1)S(1)}, u32[]{:S(2)}, u32[]{:S(2)}) collective-permute-start(bf16[48,24,128]{2,1,0:T(8,128)(2,1)S(1)} %shard_map.46.refs_0_), channel_id=1, source_target_pairs={{0,1},{1,2},{2,3},{3,4},{4,5},{5,6},{6,7},{7,0},{32,39},{33,32},{3... | collective-permute-start | bytes 884744 | tf_op jit(solution)/shard_map/ppermute | solution.py:302
  3.4 21.2 %collective-permute-start.1 = (bf16[48,24,128]{2,1,0:T(8,128)(2,1)S(1)}, bf16[48,24,128]{2,1,0:T(8,128)(2,1)S(1)}, u32[]{:S(2)}, u32[]{:S(2)}) collective-permute-start(bf16[48,24,128]{2,1,0:T(8,128)(2,1)S(1)} %shard_map.46.refs_0_), channel_id=1, source_target_pairs={{0,7},{1,0},{2,1},{3,2},{4,3},{5,4},{6,5},{7,6},{32,33},{33,34},{3... | collective-permute-start | bytes 884744 | tf_op jit(solution)/shard_map/ppermute | solution.py:302
  24.6 9.3 %collective-permute-start.9 = (bf16[48,24,128]{2,1,0:T(8,128)(2,1)S(1)}, bf16[48,24,128]{2,1,0:T(8,128)(2,1)S(1)}, u32[]{:S(2)}, u32[]{:S(2)}) collective-permute-start(bf16[48,24,128]{2,1,0:T(8,128)(2,1)S(1)} %collective-permute-done.refs_1_), channel_id=1, source_target_pairs={{0,1},{1,2},{2,3},{3,4},{4,5},{5,6},{6,7},{7,0},{32,39},{33,32},{3... | collective-permute-start | bytes 884744 | tf_op jit(solution)/shard_map/ppermute | solution.py:302
  25.4 10.9 %collective-permute-start.2 = (bf16[8,3,24,128]{3,2,1,0:T(8,128)(2,1)S(1)}, bf16[8,3,24,128]{3,2,1,0:T(8,128)(2,1)S(1)}, u32[]{:S(2)}, u32[]{:S(2)}) collective-permute-start(bf16[8,3,24,128]{3,2,1,0:T(8,128)(2,1)S(1)} %all_to_all.5.refs_0_), channel_id=1, source_target_pairs={{0,64},{32,224},{64,128},{96,32},{128,192},{160,96},{192,0},{224,1... | collective-permute-start | bytes 442376 | tf_op jit(solution)/shard_map/ppermute | solution.py:302
  26.9 15.6 %collective-permute-start.10 = (bf16[48,24,128]{2,1,0:T(8,128)(2,1)S(1)}, bf16[48,24,128]{2,1,0:T(8,128)(2,1)S(1)}, u32[]{:S(2)}, u32[]{:S(2)}) collective-permute-start(bf16[48,24,128]{2,1,0:T(8,128)(2,1)S(1)} %collective-permute-done.1.refs_2_), channel_id=1, source_target_pairs={{0,7},{1,0},{2,1},{3,2},{4,3},{5,4},{6,5},{7,6},{32,33},{33,34},{3... | collective-permute-start | bytes 884744 | tf_op jit(solution)/shard_map/ppermute | solution.py:302
  33.9 11.8 %collective-permute-start.11 = (bf16[48,24,128]{2,1,0:T(8,128)(2,1)S(1)}, bf16[48,24,128]{2,1,0:T(8,128)(2,1)S(1)}, u32[]{:S(2)}, u32[]{:S(2)}) collective-permute-start(bf16[48,24,128]{2,1,0:T(8,128)(2,1)S(1)} %collective-permute-done.9.refs_3_), channel_id=1, source_target_pairs={{0,1},{1,2},{2,3},{3,4},{4,5},{5,6},{6,7},{7,0},{32,39},{33,32},{3... | collective-permute-start | bytes 884744 | tf_op jit(solution)/shard_map/ppermute | solution.py:302
  34.4 5.1 %collective-permute-start.3 = (bf16[8,3,24,128]{3,2,1,0:T(8,128)(2,1)S(1)}, bf16[8,3,24,128]{3,2,1,0:T(8,128)(2,1)S(1)}, u32[]{:S(2)}, u32[]{:S(2)}) collective-permute-start(bf16[8,3,24,128]{3,2,1,0:T(8,128)(2,1)S(1)} %all_to_all.5.refs_0_), channel_id=1, source_target_pairs={{0,192},{32,96},{64,0},{96,160},{128,64},{160,224},{192,128},{224,... | collective-permute-start | bytes 442376 | tf_op jit(solution)/shard_map/ppermute | solution.py:302
  35.3 6.6 %collective-permute-start.4 = (bf16[8,3,24,128]{3,2,1,0:T(8,128)(2,1)S(1)}, bf16[8,3,24,128]{3,2,1,0:T(8,128)(2,1)S(1)}, u32[]{:S(2)}, u32[]{:S(2)}) collective-permute-start(bf16[8,3,24,128]{3,2,1,0:T(8,128)(2,1)S(1)} %all_to_all.5.refs_0_), channel_id=1, source_target_pairs={{0,128},{32,160},{64,192},{96,224},{128,0},{160,32},{192,64},{224,... | collective-permute-start | bytes 442376 | tf_op jit(solution)/shard_map/ppermute | solution.py:302
  36.3 5.7 %collective-permute-start.5 = (bf16[8,3,24,128]{3,2,1,0:T(8,128)(2,1)S(1)}, bf16[8,3,24,128]{3,2,1,0:T(8,128)(2,1)S(1)}, u32[]{:S(2)}, u32[]{:S(2)}) collective-permute-start(bf16[8,3,24,128]{3,2,1,0:T(8,128)(2,1)S(1)} %all_to_all.5.refs_0_), channel_id=1, source_target_pairs={{0,32},{32,0},{64,96},{96,64},{128,160},{160,128},{192,224},{224,1... | collective-permute-start | bytes 442376 | tf_op jit(solution)/shard_map/ppermute | solution.py:317
  39.5 9.3 %collective-permute-start.6 = (bf16[8,3,24,128]{3,2,1,0:T(8,128)(2,1)S(1)}, bf16[8,3,24,128]{3,2,1,0:T(8,128)(2,1)S(1)}, u32[]{:S(2)}, u32[]{:S(2)}) collective-permute-start(bf16[8,3,24,128]{3,2,1,0:T(8,128)(2,1)S(1)} %collective-permute-done.2.refs_1_), channel_id=1, source_target_pairs={{0,32},{32,0},{64,96},{96,64},{128,160},{160,128},{192,224},{224,1... | collective-permute-start | bytes 442376 | tf_op jit(solution)/shard_map/ppermute | solution.py:317
  42.0 6.9 %collective-permute-start.7 = (bf16[8,3,24,128]{3,2,1,0:T(8,128)(2,1)S(1)}, bf16[8,3,24,128]{3,2,1,0:T(8,128)(2,1)S(1)}, u32[]{:S(2)}, u32[]{:S(2)}) collective-permute-start(bf16[8,3,24,128]{3,2,1,0:T(8,128)(2,1)S(1)} %collective-permute-done.3.refs_2_), channel_id=1, source_target_pairs={{0,32},{32,0},{64,96},{96,64},{128,160},{160,128},{192,224},{224,1... | collective-permute-start | bytes 442376 | tf_op jit(solution)/shard_map/ppermute | solution.py:317
  42.0 6.9 %collective-permute-start.8 = (bf16[8,3,24,128]{3,2,1,0:T(8,128)(2,1)S(1)}, bf16[8,3,24,128]{3,2,1,0:T(8,128)(2,1)S(1)}, u32[]{:S(2)}, u32[]{:S(2)}) collective-permute-start(bf16[8,3,24,128]{3,2,1,0:T(8,128)(2,1)S(1)} %collective-permute-done.4.refs_3_), channel_id=1, source_target_pairs={{0,32},{32,0},{64,96},{96,64},{128,160},{160,128},{192,224},{224,1... | collective-permute-start | bytes 442376 | tf_op jit(solution)/shard_map/ppermute | solution.py:318
  42.5 10.0 %collective-permute-start.12 = (bf16[48,24,128]{2,1,0:T(8,128)(2,1)S(1)}, bf16[48,24,128]{2,1,0:T(8,128)(2,1)S(1)}, u32[]{:S(2)}, u32[]{:S(2)}) collective-permute-start(bf16[48,24,128]{2,1,0:T(8,128)(2,1)S(1)} %collective-permute-done.10.refs_4_), channel_id=1, source_target_pairs={{0,7},{1,0},{2,1},{3,2},{4,3},{5,4},{6,5},{7,6},{32,33},{33,34},{3... | collective-permute-start | bytes 884744 | tf_op jit(solution)/shard_map/ppermute | solution.py:302
  45.7 7.9 %collective-permute-start.13 = (bf16[48,24,128]{2,1,0:T(8,128)(2,1)S(1)}, bf16[48,24,128]{2,1,0:T(8,128)(2,1)S(1)}, u32[]{:S(2)}, u32[]{:S(2)}) collective-permute-start(bf16[48,24,128]{2,1,0:T(8,128)(2,1)S(1)} %collective-permute-done.11.refs_5_), channel_id=1, source_target_pairs={{0,1},{1,2},{2,3},{3,4},{4,5},{5,6},{6,7},{7,0},{32,39},{33,32},{3... | collective-permute-start | bytes 884744 | tf_op jit(solution)/shard_map/ppermute | solution.py:302
  61.1 8.4 %collective-permute-start.18 = (f32[44,1104]{1,0:T(8,128)S(1)}, f32[44,1104]{1,0:T(8,128)S(1)}, u32[]{:S(2)}, u32[]{:S(2)}) collective-permute-start(f32[44,1104]{1,0:T(8,128)S(1)} %get-tuple-element.28), channel_id=1, source_target_pairs={{0,24},{8,0},{16,8},{24,16},{32,40},{40,48},{48,56},{56,32},{64,88... | collective-permute-start | bytes 582920 | tf_op jit(solution)/shard_map/ppermute | solution.py:302
  61.6 9.4 %collective-permute-start.15 = (f32[48,1104]{1,0:T(8,128)S(1)}, f32[48,1104]{1,0:T(8,128)S(1)}, u32[]{:S(2)}, u32[]{:S(2)}) collective-permute-start(f32[48,1104]{1,0:T(8,128)S(1)} %get-tuple-element.25), channel_id=1, source_target_pairs={{0,8},{8,16},{16,24},{24,0},{32,56},{40,32},{48,40},{56,48},{64,72... | collective-permute-start | bytes 635912 | tf_op jit(solution)/shard_map/ppermute | solution.py:302
  63.2 9.6 %collective-permute-start.17 = (f32[44,1104]{1,0:T(8,128)S(1)}, f32[44,1104]{1,0:T(8,128)S(1)}, u32[]{:S(2)}, u32[]{:S(2)}) collective-permute-start(f32[44,1104]{1,0:T(8,128)S(1)} %get-tuple-element.26), channel_id=1, source_target_pairs={{0,8},{8,16},{16,24},{24,0},{32,56},{40,32},{48,40},{56,48},{64,72... | collective-permute-start | bytes 582920 | tf_op jit(solution)/shard_map/ppermute | solution.py:302
  69.5 6.5 %collective-permute-start.19 = (f32[44,1104]{1,0:T(8,128)S(1)}, f32[44,1104]{1,0:T(8,128)S(1)}, u32[]{:S(2)}, u32[]{:S(2)}) collective-permute-start(f32[44,1104]{1,0:T(8,128)S(1)} %add.28), channel_id=1, source_target_pairs={{0,24},{8,0},{16,8},{24,16},{32,40},{40,48},{48,56},{56,32},{64,88... | collective-permute-start | bytes 582920 | tf_op jit(solution)/shard_map/ppermute | solution.py:302
  70.0 8.3 %collective-permute-start.14 = (f32[48,1104]{1,0:T(8,128)S(1)}, f32[48,1104]{1,0:T(8,128)S(1)}, u32[]{:S(2)}, u32[]{:S(2)}) collective-permute-start(f32[48,1104]{1,0:T(8,128)S(1)} %get-tuple-element.23), channel_id=1, source_target_pairs={{0,24},{8,0},{16,8},{24,16},{32,40},{40,48},{48,56},{56,32},{64,88... | collective-permute-start | bytes 635912 | tf_op jit(solution)/shard_map/ppermute | solution.py:302
  71.0 7.7 %collective-permute-start.16 = (f32[48,1104]{1,0:T(8,128)S(1)}, f32[48,1104]{1,0:T(8,128)S(1)}, u32[]{:S(2)}, u32[]{:S(2)}) collective-permute-start(f32[48,1104]{1,0:T(8,128)S(1)} %add.25), channel_id=1, source_target_pairs={{0,8},{8,16},{16,24},{24,0},{32,56},{40,32},{48,40},{56,48},{64,72... | collective-permute-start | bytes 635912 | tf_op jit(solution)/shard_map/ppermute | solution.py:302
  78.8 11.1 %collective-permute-start.20 = (bf16[92,1104]{1,0:T(8,128)(2,1)S(1)}, bf16[92,1104]{1,0:T(8,128)(2,1)S(1)}, u32[]{:S(2)}, u32[]{:S(2)}) collective-permute-start(bf16[92,1104]{1,0:T(8,128)(2,1)S(1)} %pad_maximum_fusion), channel_id=1, source_target_pairs={{0,0},{1,9},{2,18},{3,27},{4,31},{5,22},{6,13},{7,4},{8,1},{9,8},{... | collective-permute-start | bytes 609416 | tf_op jit(solution)/shard_map/ppermute | solution.py:291
